TPU v7x, 8 devices: a whole 2x2x1 slice. The times are simulated.
8 devices in a mesh: dp: 1 (over z), tp: 2 (over y), sp: 4 (over x, core).
Axes of the slice: x: 2, y: 2, z: 1, core: 2. Of those that a mesh axis runs over, the one named last changes fastest.
Arguments:
- tokens: bfloat16 [64, 2560], P('dp')
- positions: int32 [64], P('dp')
- cache_k: bfloat16 [64, 1024, 4, 256], P('dp', 'sp', 'tp')
- cache_v: bfloat16 [64, 1024, 4, 256], P('dp', 'sp', 'tp')
- attn_gain: bfloat16 [2560], replicated
- w_q: bfloat16 [2560, 2048], P(None, 'tp')
- w_k: bfloat16 [2560, 1024], P(None, 'tp')
- w_v: bfloat16 [2560, 1024], P(None, 'tp')
- w_o: bfloat16 [2048, 2560], P('tp')
- mlp_gain: bfloat16 [2560], replicated
- w_gate: bfloat16 [2560, 10240], P(None, 'tp')
- w_up: bfloat16 [2560, 10240], P(None, 'tp')
- w_down: bfloat16 [10240, 2560], P('tp')
Outputs:
- output 1: bfloat16 [64, 2560], P('dp')
- output 2: bfloat16 [64, 1024, 4, 256], P('dp', 'sp', 'tp')
- output 3: bfloat16 [64, 1024, 4, 256], P('dp', 'sp', 'tp')
All inputs are finite; a program needn't handle non-finite values.
Results may differ from a plain program's by a relative error of at most 0.00835539.
Values sent between devices are 32-bit elements.
A program may use at most 1 GiB of HBM per device.

v0:
```python
import math
import jax
import jax.numpy as jnp
from jax import lax
from jax.sharding import PartitionSpec as P

NORM_EPS = 1e-5
ROPE_THETA = 10000.0


def rms_norm(values, gain):
    wide = values.astype(jnp.float32)
    inv_rms = lax.rsqrt(jnp.mean(wide * wide, axis=-1, keepdims=True) + NORM_EPS)
    return (wide * inv_rms * gain.astype(jnp.float32)).astype(jnp.bfloat16)


def rope_tables(positions, head_dim):
    frequencies = ROPE_THETA ** (-2.0 * jnp.arange(head_dim // 2, dtype=jnp.float32) / head_dim)
    angles = positions.astype(jnp.float32)[:, None] * frequencies[None, :]
    return jnp.cos(angles)[:, None, :], jnp.sin(angles)[:, None, :]


def apply_rope(vectors, cos_table, sin_table):
    half = vectors.shape[-1] // 2
    first = vectors[..., :half]
    second = vectors[..., half:]
    return jnp.concatenate([first * cos_table - second * sin_table, second * cos_table + first * sin_table], axis=-1)


def solution(mesh):
    sp_size = mesh.shape["sp"]
    cache_spec = P("dp", "sp", "tp", None)
    row_spec = P("dp", None)
    col_spec = P(None, "tp")
    in_specs = (row_spec, P("dp"), cache_spec, cache_spec, P(None), col_spec, col_spec, col_spec, P("tp", None), P(None), col_spec, col_spec, P("tp", None))
    out_specs = (row_spec, cache_spec, cache_spec)

    def local_step(tokens, positions, cache_k, cache_v, attn_gain, w_q, w_k, w_v, w_o, mlp_gain, w_gate, w_up, w_down):
        rows = tokens.shape[0]
        local_slots = cache_k.shape[1]
        kv_local = cache_k.shape[2]
        head_dim = cache_k.shape[3]
        heads_local = w_q.shape[1] // head_dim
        group = heads_local // kv_local
        slots = local_slots * sp_size
        slot_ids = lax.axis_index("sp") * local_slots + jnp.arange(local_slots)

        normed = rms_norm(tokens, attn_gain)
        cos_table, sin_table = rope_tables(positions, head_dim)
        q_lin = jnp.dot(normed, w_q, preferred_element_type=jnp.float32).reshape(rows, heads_local, head_dim)
        k_lin = jnp.dot(normed, w_k, preferred_element_type=jnp.float32).reshape(rows, kv_local, head_dim)
        v_new = jnp.dot(normed, w_v, preferred_element_type=jnp.float32).astype(jnp.bfloat16).reshape(rows, kv_local, head_dim)
        q_rot = apply_rope(q_lin, cos_table, sin_table).astype(jnp.bfloat16).reshape(rows, kv_local, group, head_dim)
        k_rot = apply_rope(k_lin, cos_table, sin_table).astype(jnp.bfloat16)

        hit_mask = (slot_ids[None, :] == (positions % slots)[:, None])[:, :, None, None]
        new_k = jnp.where(hit_mask, k_rot[:, None], cache_k)
        new_v = jnp.where(hit_mask, v_new[:, None], cache_v)

        scores = jnp.einsum("bkgd,bskd->bkgs", q_rot, new_k, preferred_element_type=jnp.float32) * (1.0 / math.sqrt(head_dim))
        valid = ((positions[:, None] >= slots - 1) | (slot_ids[None, :] <= positions[:, None]))[:, None, None, :]
        local_max = jnp.max(jnp.where(valid, scores, -jnp.inf), axis=-1)
        exp_scores = jnp.exp(jnp.where(valid, scores - local_max[..., None], -jnp.inf))
        local_sum = jnp.sum(exp_scores, axis=-1)
        local_out = jnp.einsum("bkgs,bskd->bkgd", exp_scores.astype(jnp.bfloat16), new_v, preferred_element_type=jnp.float32)

        global_max = lax.pmax(local_max, "sp")
        factor = jnp.exp(local_max - global_max)
        packed = jnp.concatenate([local_out * factor[..., None], (local_sum * factor)[..., None]], axis=-1)
        total = lax.psum(packed, "sp")
        attended = (total[..., :head_dim] / total[..., head_dim:]).astype(jnp.bfloat16).reshape(rows, heads_local * head_dim)

        attn_proj = lax.psum(jnp.dot(attended, w_o, preferred_element_type=jnp.float32), "tp")
        hidden = (tokens.astype(jnp.float32) + attn_proj).astype(jnp.bfloat16)
        normed_mlp = rms_norm(hidden, mlp_gain)
        gate_proj = jnp.dot(normed_mlp, w_gate, preferred_element_type=jnp.float32)
        up_proj = jnp.dot(normed_mlp, w_up, preferred_element_type=jnp.float32)
        activated = (jax.nn.silu(gate_proj) * up_proj).astype(jnp.bfloat16)
        mlp_down = lax.psum(jnp.dot(activated, w_down, preferred_element_type=jnp.float32), "tp")
        layer_out = (hidden.astype(jnp.float32) + mlp_down).astype(jnp.bfloat16)
        return layer_out, new_k, new_v

    return jax.shard_map(local_step, mesh=mesh, in_specs=in_specs, out_specs=out_specs, check_vma=False)
```

profile of v0, /device:TPU:0, one launch (start us, length us, event | category | flops | bytes accessed | tf_op | source)
XLA Modules:
  0.0 226.4 jit_solution(18245021516356783843)
XLA Ops:
  7.2 0.0 copy-start
  7.2 0.0 all-reduce.4.cloned.1.call-start
  7.2 0.8 broadcast_compare_fusion.1
  8.1 0.7 fusion.46
  8.8 1.1 fusion.17
  10.0 0.7 convert_element_type.49
  10.7 0.0 copy-done
  10.7 1.6 convolution_convert_fusion
  12.3 2.5 %fusion.41 = f32[64,512]{1,0:T(8,128)S(1)} fusion(bf16[2560,512]{1,0:T(8,128)(2,1)} %param.19, bf16[64,2560]{1,0:T(8,128)(2,1)} %param.13, f32[2560]{0:T(1024)S(1)} %convert_element_type.49, f32[64]{0:T(128)S(1)} %add_rsqrt_fusion.1), kind=kOutput, calls=%fused_computation.66 | convolution fusion | flops 168427520 | bytes 3090688 | tf_op jit(solution)/shard_map/dot_general | solution.py:51
  14.8 0.1 reshape.175
  14.9 3.7 %fusion.43 = f32[64,1024]{1,0:T(8,128)S(1)} fusion(bf16[2560,1024]{1,0:T(8,128)(2,1)} %param.18, bf16[64,2560]{1,0:T(8,128)(2,1)} %param.13, f32[2560]{0:T(1024)S(1)} %convert_element_type.49, f32[64]{0:T(128)S(1)} %add_rsqrt_fusion.1), kind=kOutput, calls=%fused_computation.67 | convolution fusion | flops 336199680 | bytes 5843200 | tf_op jit(solution)/shard_map/dot_general | solution.py:50
  18.5 0.1 reshape.174
  18.7 0.2 multiply_cosine_fusion
  18.9 0.1 subtract_convert_fusion.1
  18.9 0.1 subtract_convert_fusion
  19.0 0.1 pad_maximum_fusion.1
  19.1 0.8 compare_or_fusion
  19.9 41.4 %broadcast_select_fusion = (bf16[64,256,2,256]{3,2,1,0:T(2,128)(2,1)}, bf16[64,256,2,256]{3,2,1,0:T(2,128)(2,1)}) fusion(bf16[64,256,2,256]{3,2,1,0:T(2,128)(2,1)} %param.16, pred[64,256]{1,0:T(8,128)(4,1)S(1)} %get-tuple-element.14, bf16[64,2,256]{2,1,0:T(2,128)(2,1)S(1)} %broadcast_in_dim.67, bf16[64,256,2,256]{3,2,1,0:T(2,128)(2,1)} %param.15, ...), kind=kLoop, calls=%fused_computation | loop fusion | flops 16777216 | bytes 67256320 | tf_op jit(solution)/shard_map/jit(_where)/select_n | solution.py:58
  61.3 10.3 %select_reduce_fusion = (f32[64,2,2]{2,1,0:T(2,128)S(1)}, f32[64,2,2,256]{3,2,1,0:T(2,128)S(1)}) fusion(pred[64,256]{1,0:T(8,128)(4,1)S(1)} %get-tuple-element.13, bf16[64,256,2,256]{3,2,1,0:T(2,128)(2,1)} %get-tuple-element.12, bf16[64,2,2,128]{3,2,1,0:T(2,128)(2,1)S(1)} %bitcast.16, bf16[64,2,2,128]{3,2,1,0:T(2,128)(2,1)S(1)} %bitcast.15), kind=kOutput, calls=%fused_computation.35 | convolution fusion | flops 34012928 | bytes 17187840 | tf_op jit(solution)/shard_map/bkgd,bskd->bkgs/dot_general | solution.py:60
  71.6 0.0 copy-start.3
  71.6 0.0 copy-start.2
  71.6 13.9 %pmax.7 = f32[64,2,2]{2,1,0:T(2,128)S(1)} all-reduce(f32[64,2,2]{2,1,0:T(2,128)S(1)} %get-tuple-element.19), channel_id=1, replica_groups=mesh['dp'=1,'tp'=2,'sp'=4] {'sp'}, use_global_device_ids=true, to_apply=%region_2.3 | all-reduce | flops 256 | bytes 2048 | tf_op jit(solution)/shard_map/pmax | solution.py:67
  85.6 0.5 fusion.35
  86.1 0.1 multiply_bitcast_fusion
  86.2 0.9 copy.28
  87.1 8.1 %fusion.14 = f32[64,2,2,256]{3,2,1,0:T(2,128)S(1)} fusion(bf16[64,256,2,256]{3,2,1,0:T(2,128)(2,1)} %get-tuple-element.11, f32[64,2,2]{2,1,0:T(2,128)S(1)} %get-tuple-element.6, f32[64,2,2,256]{3,2,1,0:T(2,128)S(1)} %get-tuple-element.20, pred[64,256]{1,0:T(8,128)(4,1)S(1)} %get-tuple-element.13, f32[64,2,2]{2,1,0:T(2,128)S(1)} %get-tuple-element.19), kind=kOutput, calls=%fused_computation.15 | convolution fusion | flops 33816576 | bytes 17319936 | tf_op jit(solution)/shard_map/bkgs,bskd->bkgd/dot_general | solution.py:65
  95.2 1.0 pad_maximum_fusion
  96.2 0.0 all-reduce.4.cloned.1.call-update
  96.2 0.0 all-reduce.6.cloned.1.call-start
  96.2 27.2 %all-reduce.4.cloned.1.call-done = f32[64,2,2,257]{3,2,1,0:T(2,128)} async-done(((f32[64,2,2,257]{3,2,1,0:T(2,128)}), f32[64,2,2,257]{3,2,1,0:T(2,128)}) %all-reduce.4.cloned.1.call-update) | async-done | bytes 263184 | tf_op jit(solution)/shard_map/psum | solution.py:70
  123.4 0.9 slice.29
  124.4 0.9 copy.33
  125.2 1.2 fusion.26
  126.4 0.1 reshape.176
  126.5 4.4 %fusion.47 = f32[64,2560]{1,0:T(8,128)} fusion(bf16[64,1024]{1,0:T(8,128)(2,1)S(1)} %reshape.176, bf16[1024,2560]{1,0:T(8,128)(2,1)} %param.21), kind=kOutput, calls=%fused_computation.69 | convolution fusion | flops 335544320 | bytes 6029312 | tf_op jit(solution)/shard_map/dot_general | solution.py:73
  130.9 0.0 all-reduce.6.cloned.1.call-update
  130.9 0.2 all-reduce.8.cloned.1.call-start
  131.1 0.0 copy-done.3
  131.1 25.6 %all-reduce.6.cloned.1.call-done = f32[64,2560]{1,0:T(8,128)} async-done(((f32[64,2560]{1,0:T(8,128)}), f32[64,2560]{1,0:T(8,128)}) %all-reduce.6.cloned.1.call-update) | async-done | bytes 655376 | tf_op jit(solution)/shard_map/psum | solution.py:73
  156.7 0.0 copy-done.2
  156.7 1.3 fusion.21
  158.0 12.0 %fusion.33 = f32[64,5120]{1,0:T(8,128)} fusion(bf16[2560,5120]{1,0:T(8,128)(2,1)} %param.23, bf16[64,2560]{1,0:T(8,128)(2,1)S(1)} %get-tuple-element.4, f32[2560]{0:T(1024)S(1)} %convert_element_type.57, f32[64]{0:T(128)S(1)} %add_rsqrt_fusion), kind=kOutput, calls=%fused_computation.43 | convolution fusion | flops 1678376960 | bytes 27863296 | tf_op jit(solution)/shard_map/dot_general | solution.py:76
  170.0 0.0 copy-start.1
  170.0 22.1 %fusion.5 = f32[64,2560]{1,0:T(8,128)} fusion(bf16[5120,2560]{1,0:T(8,128)(2,1)} %param.25, bf16[2560,5120]{1,0:T(8,128)(2,1)} %param.24, f32[64,5120]{1,0:T(8,128)} %fusion.33, bf16[64,2560]{1,0:T(8,128)(2,1)S(1)} %get-tuple-element.4, f32[2560]{0:T(1024)S(1)} %convert_element_type.57, f32[64]{0:T(128)S(1)} %add_rsqrt_fusion), kind=kOutput, calls=%fused_computation.8 | convolution fusion | flops 3358064640 | bytes 54733056 | tf_op jit(solution)/shard_map/dot_general | solution.py:79
  192.1 0.0 all-reduce.8.cloned.1.call-update
  192.1 25.8 %all-reduce.8.cloned.1.call-done = f32[64,2560]{1,0:T(8,128)} async-done(((f32[64,2560]{1,0:T(8,128)}), f32[64,2560]{1,0:T(8,128)}) %all-reduce.8.cloned.1.call-update) | async-done | bytes 655376 | tf_op jit(solution)/shard_map/psum | solution.py:79
  218.0 1.9 fusion.24
  219.9 0.0 copy-done.1
  (6 shorter events, 0.1 us)
Async XLA Ops:
  7.2 3.5 %copy-start = (bf16[2560,512]{1,0:T(8,128)(2,1)S(1)}, bf16[2560,512]{1,0:T(8,128)(2,1)}, u32[]{:S(2)}) copy-start(bf16[2560,512]{1,0:T(8,128)(2,1)} %param.20) | copy-start | bytes 7864324
  7.2 116.3 %all-reduce.4.cloned.1.call-start = ((), (), s32[]{:S(2)}) async-start(), calls=%async_computation | async-start | bytes 786432 | tf_op jit(solution)/shard_map/psum | solution.py:70
  71.6 59.5 %copy-start.3 = (bf16[2560]{0:T(1024)(128)(2,1)S(1)}, bf16[2560]{0:T(1024)(128)(2,1)}, u32[]{:S(2)}) copy-start(bf16[2560]{0:T(1024)(128)(2,1)} %param.22) | copy-start | bytes 15364
  71.6 85.1 %copy-start.2 = (bf16[64,2560]{1,0:T(8,128)(2,1)S(1)}, bf16[64,2560]{1,0:T(8,128)(2,1)}, u32[]{:S(2)}) copy-start(bf16[64,2560]{1,0:T(8,128)(2,1)} %param.13) | copy-start | bytes 983044
  96.2 60.5 %all-reduce.6.cloned.1.call-start = ((), (), s32[]{:S(2)}) async-start(), calls=%async_computation.1 | async-start | bytes 1310720 | tf_op jit(solution)/shard_map/psum | solution.py:73
  130.9 87.1 %all-reduce.8.cloned.1.call-start = ((), (), s32[]{:S(2)}) async-start(), calls=%async_computation.2 | async-start | bytes 1310720 | tf_op jit(solution)/shard_map/psum | solution.py:79
  170.0 49.8 %copy-start.1 = (bf16[2560,512]{1,0:T(8,128)(2,1)S(1)}, bf16[2560,512]{1,0:T(8,128)(2,1)}, u32[]{:S(2)}) copy-start(bf16[2560,512]{1,0:T(8,128)(2,1)} %param.20) | copy-start | bytes 7864324
Sparse Core Ops, SparseCore 0:
  96.3 27.0 all-reduce.3
  131.0 25.6 all-reduce.5
  192.3 25.6 all-reduce.7
where the time goes:
time: 227 us; the launch traced here: 226 us
  waiting for transfers between devices  78.7 us (35%)
  matrix products  64.6 us (28%)
  other arithmetic  51.8 us (23%)
  between operations  14 us (6%)
  blocking collectives  13.9 us (6%)
  local copies, waits for them, and re-layouts  3.02 us (1%)
    select_n x1, other arithmetic, local_step(): new_v = jnp.where(hit_mask, v_new[:, None], cache_v)  41.4 us
    psum x1, waiting for transfers between devices, local_step(): total = lax.psum(packed, 'sp')  27.2 us
    psum x1, waiting for transfers between devices, local_step(): lax.psum(jnp.dot(activated, w_down, preferred_element_type=jnp.float32),...  25.8 us
    psum x1, waiting for transfers between devices, local_step(): lax.psum(jnp.dot(attended, w_o, preferred_element_type=jnp.float32), 'tp')  25.6 us
    dot_general x1, matrix products, local_step(): jnp.dot(activated, w_down, preferred_element_type=jnp.float32)  22.1 us
    pmax x1, blocking collectives, local_step(): global_max = lax.pmax(local_max, 'sp')  13.9 us
    dot_general x1, matrix products, local_step(): gate_proj = jnp.dot(normed_mlp, w_gate, preferred_element_type=jnp.float32)  12 us
    dot_general x1, matrix products, local_step(): jnp.einsum('bkgd,bskd->bkgs', q_rot, new_k, preferred_element_type=jnp.fl...  10.3 us
  transfers between devices with their start and end apart: 3, of which 3 were waited for; matrix products, arithmetic and copies ran while one was open for 0% of the time, Pallas kernels for 0%

commit v1 on v0

v1 whole, which is shorter than its diff:
```python
import functools
import math

import jax
import jax.numpy as jnp
from jax import lax
from jax.experimental import pallas as pl
from jax.experimental.pallas import tpu as pltpu
from jax.sharding import PartitionSpec as P

NORM_EPS = 1e-5
ROPE_THETA = 10000.0
LANES = 128
F32 = jnp.float32
BF16 = jnp.bfloat16
FAR = 1 << 28
BLOCK = 4
AHEAD = 5


def rms_norm(values, gain):
    wide = values.astype(F32)
    inv_rms = lax.rsqrt(jnp.mean(wide * wide, axis=-1, keepdims=True) + NORM_EPS)
    return (wide * inv_rms * gain.astype(F32)).astype(BF16)


def attention_kernel(
    pos, x_ref, gain_ref, wq_hbm, wk_hbm, wv_hbm, ck_hbm, cv_hbm,
    part_ref, nk_hbm, nv_hbm,
    wbuf, kbuf, vbuf, q_s, kn_s, vn_s, ang_s, o_s, m_s, l_s,
    w_sem, k_sem, v_sem, out_sem,
):
    rows = x_ref.shape[0]
    head_dim = 2 * LANES
    heads = wq_hbm.shape[1] // head_dim
    kvs = wk_hbm.shape[1] // head_dim
    group = heads // kvs
    per_slot = 2 * kvs
    qrows = 2 * heads
    key_rows = ck_hbm.shape[1]
    local_slots = key_rows // per_slot
    slots = local_slots * lax.axis_size("sp")
    slices = key_rows // LANES
    n_blocks = rows // BLOCK
    base = lax.axis_index("sp") * local_slots

    def w_copy(n):
        src, col = (
            (wk_hbm, n) if n < kvs else (wv_hbm, n - kvs) if n < 2 * kvs else (wq_hbm, n - 2 * kvs)
        )
        return pltpu.make_async_copy(src.at[:, pl.ds(col * head_dim, head_dim)], wbuf.at[n], w_sem.at[n])

    def in_copies(j):
        span = pl.ds(j * BLOCK, BLOCK)
        return (
            pltpu.make_async_copy(ck_hbm.at[span], kbuf.at[span], k_sem.at[j]),
            pltpu.make_async_copy(cv_hbm.at[span], vbuf.at[span], v_sem.at[j]),
        )

    def out_copies(j):
        span = pl.ds(j * BLOCK, BLOCK)
        return (
            pltpu.make_async_copy(kbuf.at[span], nk_hbm.at[span], out_sem.at[0]),
            pltpu.make_async_copy(vbuf.at[span], nv_hbm.at[span], out_sem.at[1]),
        )

    n_w = heads + 2 * kvs
    for n in range(n_w):
        w_copy(n).start()
    for j in range(AHEAD):
        for copy in in_copies(j):
            copy.start()

    lane = lax.broadcasted_iota(jnp.int32, (1, LANES), 1).astype(F32)
    freq = jnp.exp2(lane * (-math.log2(ROPE_THETA) / LANES))

    def angle_row(b, carry):
        ang_s[pl.ds(b, 1), :] = freq * pos[b].astype(F32)
        return carry

    lax.fori_loop(0, rows, angle_row, 0, unroll=8)
    angles = ang_s[...]
    cos_t, sin_t = jnp.cos(angles), jnp.sin(angles)
    normed = rms_norm(x_ref[...], gain_ref[...])

    for n in range(n_w):
        w_copy(n).wait()
        lin = jnp.dot(normed, wbuf[n], preferred_element_type=F32)
        first, second = lin[:, :LANES], lin[:, LANES:]
        if not kvs <= n < 2 * kvs:
            first, second = first * cos_t - second * sin_t, second * cos_t + first * sin_t
        if n >= 2 * kvs:
            h = n - 2 * kvs
            q_s[pl.ds(h, rows, stride=qrows), :] = first
            q_s[pl.ds(heads + h, rows, stride=qrows), :] = second
        else:
            dst, kv = (kn_s, n) if n < kvs else (vn_s, n - kvs)
            for rep in range(16 // per_slot):
                dst[pl.ds(rep * per_slot + kv, rows, stride=16), :] = first
                dst[pl.ds(rep * per_slot + kvs + kv, rows, stride=16), :] = second

    row = lax.broadcasted_iota(jnp.int32, (qrows, LANES), 0)
    col = lax.broadcasted_iota(jnp.int32, (qrows, LANES), 1)
    half_of_col = (col // kvs) % 2
    fits = (half_of_col == row // heads) & (col % kvs == (row % heads) // group)
    slot_of_col = jnp.where(fits, col // per_slot, FAR)
    low_half = half_of_col == 0
    patch_row = lax.broadcasted_iota(jnp.int32, (16, LANES), 0) // per_slot
    scale = 1.0 / math.sqrt(head_dim)

    def block_step(j, carry):
        @pl.when(j + AHEAD < n_blocks)
        def _():
            for copy in in_copies(j + AHEAD):
                copy.start()

        for copy in in_copies(j):
            copy.wait()
        for i in range(BLOCK):
            b = j * BLOCK + i
            local = lax.rem(pos[b], slots) - base
            owned = (local >= 0) & (local < local_slots)
            safe = jnp.where(owned, local, 0)
            hit = jnp.where(owned, lax.rem(safe, 16 // per_slot), -1)
            span = pl.ds(pl.multiple_of((safe // (16 // per_slot)) * 16, 16), 16)
            for buf, new in ((kbuf, kn_s), (vbuf, vn_s)):
                old = buf[b, span, :].astype(F32)
                fresh = new[pl.ds(pl.multiple_of(b * 16, 16), 16), :]
                buf[b, span, :] = jnp.where(patch_row == hit, fresh, old).astype(BF16)
        scores = []
        for i in range(BLOCK):
            b = j * BLOCK + i
            q = q_s[pl.ds(pl.multiple_of(b * qrows, qrows), qrows), :].astype(BF16)
            scores.append(
                lax.dot_general(q, kbuf[b], (((1,), (1,)), ((), ())), preferred_element_type=F32)
            )
        probs = []
        for i in range(BLOCK):
            b = j * BLOCK + i
            limit = jnp.where(pos[b] >= slots - 1, FAR // 2, pos[b]) - base
            parts = []
            for t in range(slices):
                own = scores[i][:, t * LANES : (t + 1) * LANES]
                other = pltpu.roll(own, heads, 0)
                other = jnp.where(
                    low_half, pltpu.roll(other, LANES - kvs, 1), pltpu.roll(other, kvs, 1)
                )
                ok = slot_of_col <= limit - t * (LANES // per_slot)
                parts.append(jnp.where(ok, (own + other) * scale, -jnp.inf))
            top = functools.reduce(jnp.maximum, parts)
            top = jnp.max(top, axis=1, keepdims=True)
            floor = jnp.where(top == -jnp.inf, 0.0, top)
            parts = [jnp.exp(part - floor) for part in parts]
            total = jnp.sum(functools.reduce(jnp.add, parts), axis=1, keepdims=True)
            span = pl.ds(pl.multiple_of(b * qrows, qrows), qrows)
            m_s[span, :] = jnp.broadcast_to(top, (qrows, LANES))
            l_s[span, :] = jnp.broadcast_to(total, (qrows, LANES))
            probs.append(jnp.concatenate([part.astype(BF16) for part in parts], axis=1))
        for i in range(BLOCK):
            b = j * BLOCK + i
            span = pl.ds(pl.multiple_of(b * qrows, qrows), qrows)
            o_s[span, :] = jnp.dot(probs[i], vbuf[b], preferred_element_type=F32)
        for copy in out_copies(j):
            copy.start()
        return carry

    lax.fori_loop(0, n_blocks, block_step, 0)

    left = lax.broadcasted_iota(jnp.int32, (rows, LANES), 1) < LANES // 2
    for h in range(heads):
        part_ref[h, 0] = o_s[pl.ds(h, rows, stride=qrows), :]
        part_ref[h, 1] = o_s[pl.ds(heads + h, rows, stride=qrows), :]
        part_ref[h, 2] = jnp.where(
            left, m_s[pl.ds(h, rows, stride=qrows), :], l_s[pl.ds(h, rows, stride=qrows), :]
        )
    for j in range(n_blocks):
        for copy in out_copies(j):
            copy.wait()


def attention(positions, tokens, gain, w_q, w_k, w_v, rows_k, rows_v):
    rows, width = tokens.shape
    head_dim = 2 * LANES
    heads = w_q.shape[1] // head_dim
    kvs = w_k.shape[1] // head_dim
    qrows = 2 * heads
    vmem = pl.BlockSpec(memory_space=pltpu.VMEM)
    hbm = pl.BlockSpec(memory_space=pl.ANY)
    n_blocks = rows // BLOCK
    return pl.pallas_call(
        attention_kernel,
        out_shape=(
            jax.ShapeDtypeStruct((heads, 3, rows, LANES), F32),
            jax.ShapeDtypeStruct(rows_k.shape, BF16),
            jax.ShapeDtypeStruct(rows_v.shape, BF16),
        ),
        in_specs=[pl.BlockSpec(memory_space=pltpu.SMEM), vmem, vmem] + [hbm] * 5,
        out_specs=(vmem, hbm, hbm),
        scratch_shapes=[
            pltpu.VMEM((heads + 2 * kvs, width, head_dim), BF16),
            pltpu.VMEM(rows_k.shape, BF16),
            pltpu.VMEM(rows_v.shape, BF16),
            pltpu.VMEM((rows * qrows, LANES), F32),
            pltpu.VMEM((rows * 16, LANES), F32),
            pltpu.VMEM((rows * 16, LANES), F32),
            pltpu.VMEM((rows, LANES), F32),
            pltpu.VMEM((rows * qrows, LANES), F32),
            pltpu.VMEM((rows * qrows, LANES), F32),
            pltpu.VMEM((rows * qrows, LANES), F32),
            pltpu.SemaphoreType.DMA((heads + 2 * kvs,)),
            pltpu.SemaphoreType.DMA((n_blocks,)),
            pltpu.SemaphoreType.DMA((n_blocks,)),
            pltpu.SemaphoreType.DMA((2,)),
        ],
        compiler_params=pltpu.CompilerParams(vmem_limit_bytes=60 << 20),
        name="attention_part",
    )(positions, tokens, gain, w_q, w_k, w_v, rows_k, rows_v)


def to_rows(cache):
    b, s, kv, d = cache.shape
    return cache.reshape(b, s, kv, d // LANES, LANES).transpose(0, 1, 3, 2, 4).reshape(b, -1, LANES)


def from_rows(rows, shape):
    b, s, kv, d = shape
    return rows.reshape(b, s, d // LANES, kv, LANES).transpose(0, 1, 3, 2, 4).reshape(shape)


def solution(mesh):
    cache_spec = P("dp", "sp", "tp", None)
    row_spec = P("dp", None)
    col_spec = P(None, "tp")
    in_specs = (row_spec, P("dp"), cache_spec, cache_spec, P(None), col_spec, col_spec, col_spec, P("tp", None), P(None), col_spec, col_spec, P("tp", None))
    out_specs = (row_spec, cache_spec, cache_spec)

    def local_step(tokens, positions, cache_k, cache_v, attn_gain, w_q, w_k, w_v, w_o, mlp_gain, w_gate, w_up, w_down):
        rows = tokens.shape[0]
        part, rows_k, rows_v = attention(
            positions, tokens, attn_gain, w_q, w_k, w_v, to_rows(cache_k), to_rows(cache_v)
        )
        new_k = from_rows(rows_k, cache_k.shape)
        new_v = from_rows(rows_v, cache_v.shape)
        heads = part.shape[0]
        local_max, local_sum = part[:, 2, :, 0], part[:, 2, :, LANES // 2]
        global_max = lax.pmax(local_max, "sp")
        factor = jnp.exp(local_max - global_max)[..., None]
        packed = jnp.concatenate([part[:, 0] * factor, part[:, 1] * factor, local_sum[..., None] * factor], axis=-1)
        total = lax.psum(packed, "sp")
        attended = (total[..., : 2 * LANES] / total[..., 2 * LANES :]).astype(BF16)
        attended = attended.transpose(1, 0, 2).reshape(rows, heads * 2 * LANES)

        attn_proj = lax.psum(jnp.dot(attended, w_o, preferred_element_type=F32), "tp")
        hidden = (tokens.astype(F32) + attn_proj).astype(BF16)
        normed_mlp = rms_norm(hidden, mlp_gain)
        gate_proj = jnp.dot(normed_mlp, w_gate, preferred_element_type=F32)
        up_proj = jnp.dot(normed_mlp, w_up, preferred_element_type=F32)
        activated = (jax.nn.silu(gate_proj) * up_proj).astype(BF16)
        mlp_down = lax.psum(jnp.dot(activated, w_down, preferred_element_type=F32), "tp")
        layer_out = (hidden.astype(F32) + mlp_down).astype(BF16)
        return layer_out, new_k, new_v

    return jax.shard_map(local_step, mesh=mesh, in_specs=in_specs, out_specs=out_specs, check_vma=False)
```

time: 227 us -> 176 us (0.78)
  other arithmetic: 51.8 us -> 6.08 us
  Pallas kernels: 0 us -> 28.8 us
  matrix products: 64.6 us -> 36.9 us
  blocking collectives: 13.9 us -> 8.75 us
    select_n x1 -> x0, other arithmetic: 41.4 us -> none  [local_step(): new_v = jnp.where(hit_mask, v_new[:, None], cache_v)]
    pallas_call x0 -> x1, Pallas kernels: none -> 28.8 us  [attention(): pl.pallas_call(attention_kernel, out_shape=(jax.ShapeDtypeStruct((heads,...]
    dot_general x8 -> x3, matrix products: 64.6 us -> 36.9 us  [the longest x1 21.6 us: local_step(): jnp.dot(activated, w_down, preferred_element_type=F32)]
    pmax x1, blocking collectives: 13.9 us -> 8.75 us  [local_step(): global_max = lax.pmax(local_max, 'sp')]
    convert_element_type x5 -> x2, other arithmetic: 4.46 us -> 1.87 us  [the longest x1 1.87 us: local_step(): layer_out = (hidden.astype(F32) + mlp_down).astype(BF16)]
where the time goes in v1:
time: 176 us
  waiting for transfers between devices  78.9 us (45%)
  matrix products  36.9 us (21%)
  Pallas kernels  28.8 us (16%)
  between operations  13.8 us (8%)
  blocking collectives  8.75 us (5%)
  other arithmetic  6.08 us (3%)
  local copies, waits for them, and re-layouts  2.36 us (1%)
    pallas_call x1, Pallas kernels, attention(): pl.pallas_call(attention_kernel, out_shape=(jax.ShapeDtypeStruct((heads,...  28.8 us
    psum x1, waiting for transfers between devices, local_step(): total = lax.psum(packed, 'sp')  27.2 us
    psum x1, waiting for transfers between devices, local_step(): lax.psum(jnp.dot(activated, w_down, preferred_element_type=F32), 'tp')  25.8 us
    psum x1, waiting for transfers between devices, local_step(): lax.psum(jnp.dot(attended, w_o, preferred_element_type=F32), 'tp')  25.8 us
    dot_general x1, matrix products, local_step(): jnp.dot(activated, w_down, preferred_element_type=F32)  21.6 us
    dot_general x1, matrix products, local_step(): gate_proj = jnp.dot(normed_mlp, w_gate, preferred_element_type=F32)  10.9 us
    pmax x1, blocking collectives, local_step(): global_max = lax.pmax(local_max, 'sp')  8.75 us
    dot_general x1, matrix products, local_step(): jnp.dot(attended, w_o, preferred_element_type=F32)  4.36 us
  transfers between devices with their start and end apart: 3, of which 3 were waited for; matrix products, arithmetic and copies ran while one was open for 0% of the time, Pallas kernels for 0%

profile of v1, /device:TPU:0, one launch (start us, length us, event | category | flops | bytes accessed | tf_op | source)
XLA Modules:
  0.0 175.7 jit_solution(1036832043942007954)
XLA Ops:
  7.2 0.0 all-reduce.4.cloned.1.call-start
  7.2 28.8 %attention_part.1 = (f32[4,3,64,128]{3,2,1,0:T(8,128)}, bf16[64,1024,128]{2,1,0:T(8,128)(2,1)}, bf16[64,1024,128]{2,1,0:T(8,128)(2,1)}) custom-call(s32[64]{0:T(128)} %pos.1, bf16[64,2560]{1,0:T(8,128)(2,1)} %x_ref.1, bf16[2560]{0:T(1024)(128)(2,1)} %gain_ref.1, bf16[2560,1024]{1,0:T(8,128)(2,1)} %wq_hbm.1, bf16[2560,512]{1,0:T(8,128)(2,1)} %wk_hbm.1, ...), custom_call_target="tpu_custom_call" | custom-call | tf_op jit(solution)/shard_map/attention_part/pallas_call | solution.py:190
  36.0 0.0 copy-start.1
  36.0 0.0 copy-start
  36.0 1.2 slice_reduce_fusion.2
  37.2 8.7 %pmax.7 = f32[4,64]{1,0:T(4,128)S(1)} all-reduce(f32[4,64]{1,0:T(4,128)S(1)} %get-tuple-element.9), channel_id=1, replica_groups=mesh['dp'=1,'tp'=2,'sp'=4] {'sp'}, use_global_device_ids=true, to_apply=%region_0.0 | all-reduce | flops 256 | bytes 2048 | tf_op jit(solution)/shard_map/pmax | solution.py:246
  46.0 1.1 fusion.13
  47.1 0.1 copy.40
  47.2 0.8 pad_maximum_fusion
  48.0 0.0 all-reduce.4.cloned.1.call-update
  48.0 0.0 all-reduce.6.cloned.1.call-start
  48.0 27.2 %all-reduce.4.cloned.1.call-done = f32[4,64,257]{2,1,0:T(8,128)} async-done(((f32[4,64,257]{2,1,0:T(8,128)}), f32[4,64,257]{2,1,0:T(8,128)}) %all-reduce.4.cloned.1.call-update) | async-done | bytes 263184 | tf_op jit(solution)/shard_map/psum | solution.py:249
  75.3 1.0 slice_reduce_fusion
  76.3 1.1 fusion.14
  77.4 4.4 %fusion.20 = f32[64,2560]{1,0:T(8,128)} fusion(bf16[64,1024]{1,0:T(8,128)(2,1)S(1)} %bitcast.39, bf16[1024,2560]{1,0:T(8,128)(2,1)} %param.21), kind=kOutput, calls=%fused_computation.32 | convolution fusion | flops 335544320 | bytes 6029312 | tf_op jit(solution)/shard_map/dot_general | solution.py:253
  81.7 0.0 all-reduce.6.cloned.1.call-update
  81.7 0.0 all-reduce.8.cloned.1.call-start
  81.8 0.0 copy-done.1
  81.8 25.8 %all-reduce.6.cloned.1.call-done = f32[64,2560]{1,0:T(8,128)} async-done(((f32[64,2560]{1,0:T(8,128)}), f32[64,2560]{1,0:T(8,128)}) %all-reduce.6.cloned.1.call-update) | async-done | bytes 655376 | tf_op jit(solution)/shard_map/psum | solution.py:253
  107.6 0.0 copy-done
  107.6 1.3 fusion.7
  108.9 10.9 %fusion.17 = f32[64,5120]{1,0:T(8,128)S(1)} fusion(bf16[2560,5120]{1,0:T(8,128)(2,1)} %param.23, bf16[64,2560]{1,0:T(8,128)(2,1)S(1)} %get-tuple-element.12, f32[2560]{0:T(1024)S(1)} %convert_element_type.29, f32[64]{0:T(128)S(1)} %add_rsqrt_fusion), kind=kOutput, calls=%fused_computation.27 | convolution fusion | flops 1678376960 | bytes 27863296 | tf_op jit(solution)/shard_map/dot_general | solution.py:256
  119.8 21.6 %fusion.1 = f32[64,2560]{1,0:T(8,128)} fusion(bf16[5120,2560]{1,0:T(8,128)(2,1)} %param.25, bf16[2560,5120]{1,0:T(8,128)(2,1)} %param.24, f32[64,5120]{1,0:T(8,128)S(1)} %fusion.17, bf16[64,2560]{1,0:T(8,128)(2,1)S(1)} %get-tuple-element.12, f32[2560]{0:T(1024)S(1)} %convert_element_type.29, f32[64]{0:T(128)S(1)} %add_rsqrt_fusion), kind=kOutput, calls=%fused_computation.2 | convolution fusion | flops 3358064640 | bytes 54733056 | tf_op jit(solution)/shard_map/dot_general | solution.py:259
  141.4 0.0 all-reduce.8.cloned.1.call-update
  141.4 25.8 %all-reduce.8.cloned.1.call-done = f32[64,2560]{1,0:T(8,128)} async-done(((f32[64,2560]{1,0:T(8,128)}), f32[64,2560]{1,0:T(8,128)}) %all-reduce.8.cloned.1.call-update) | async-done | bytes 655376 | tf_op jit(solution)/shard_map/psum | solution.py:259
  167.3 1.9 %fusion.10 = bf16[64,2560]{1,0:T(8,128)(2,1)} fusion(f32[64,2560]{1,0:T(8,128)} %all-reduce.8.cloned.1.call-done, bf16[64,2560]{1,0:T(8,128)(2,1)S(1)} %get-tuple-element.12), kind=kLoop, calls=%fused_computation.14 | loop fusion | flops 491520 | bytes 1310720 | tf_op jit(solution)/shard_map/convert_element_type | solution.py:260
  (4 shorter events, 0.0 us)
Async XLA Ops:
  7.2 68.1 %all-reduce.4.cloned.1.call-start = ((), (), s32[]{:S(2)}) async-start(), calls=%async_computation | async-start | bytes 786432 | tf_op jit(solution)/shard_map/psum | solution.py:249
  36.0 45.8 %copy-start.1 = (bf16[2560]{0:T(1024)(128)(2,1)S(1)}, bf16[2560]{0:T(1024)(128)(2,1)}, u32[]{:S(2)}) copy-start(bf16[2560]{0:T(1024)(128)(2,1)} %param.22) | copy-start | bytes 15364
  36.0 71.6 %copy-start = (bf16[64,2560]{1,0:T(8,128)(2,1)S(1)}, bf16[64,2560]{1,0:T(8,128)(2,1)}, u32[]{:S(2)}) copy-start(bf16[64,2560]{1,0:T(8,128)(2,1)} %x_ref.1) | copy-start | bytes 983044
  48.0 59.6 %all-reduce.6.cloned.1.call-start = ((), (), s32[]{:S(2)}) async-start(), calls=%async_computation.1 | async-start | bytes 1310720 | tf_op jit(solution)/shard_map/psum | solution.py:253
  81.7 85.5 %all-reduce.8.cloned.1.call-start = ((), (), s32[]{:S(2)}) async-start(), calls=%async_computation.2 | async-start | bytes 1310720 | tf_op jit(solution)/shard_map/psum | solution.py:259
Sparse Core Ops, SparseCore 0:
  48.1 27.0 all-reduce.3
  81.9 25.6 all-reduce.5
  141.5 25.6 all-reduce.7

commit v2 on v1

--- a/solution.py
+++ b/solution.py
@@ -217,6 +217,224 @@
     )(positions, tokens, gain, w_q, w_k, w_v, rows_k, rows_v)
 
 
+CHUNKS = 2
+MESH = pl.DeviceIdType.MESH
+
+
+def combine(mine, theirs):
+    left = lax.broadcasted_iota(jnp.int32, mine[2].shape, mine[2].ndim - 1) < LANES // 2
+    axis = mine[2].ndim - 1
+
+    def unpack(stats):
+        turned = pltpu.roll(stats, LANES // 2, axis)
+        return jnp.where(left, stats, turned), jnp.where(left, turned, stats)
+
+    (m_a, l_a), (m_b, l_b) = unpack(mine[2]), unpack(theirs[2])
+    top = jnp.maximum(m_a, m_b)
+    f_a = jnp.where(m_a == -jnp.inf, 0.0, jnp.exp(m_a - top))
+    f_b = jnp.where(m_b == -jnp.inf, 0.0, jnp.exp(m_b - top))
+    return mine[0] * f_a + theirs[0] * f_b, mine[1] * f_a + theirs[1] * f_b, top, l_a * f_a + l_b * f_b
+
+
+def tail_kernel(
+    part_ref, x_ref, gain_ref, wo_hbm, wg_hbm, wu_hbm, wd_hbm,
+    out_ref,
+    wo, wg, wu, wd, rd, sx, rx, po, ro, so, yo, hb, act, pm, rm, sm, ym, ob,
+    w_sem, g_sem, u_sem, d_sem, send_sem, recv_sem,
+):
+    heads, _, rows, _ = part_ref.shape
+    width = x_ref.shape[1]
+    mine_h = heads // 2
+    half, quarter = rows // 2, rows // 4
+    sp, tp = lax.axis_index("sp"), lax.axis_index("tp")
+    x, k = sp // 2, lax.rem(sp, 2)
+    d_dev, x_dev, y_dev = {"sp": x * 2 + 1 - k}, {"sp": (1 - x) * 2 + k}, {"tp": 1 - tp}
+    o_rows, n_gate = wo.shape[0], wg.shape[0]
+    g_cols = wg.shape[2]
+    m_cols = n_gate * g_cols
+    n_down = wd.shape[0]
+    d_rows = wd.shape[1]
+    span = width // CHUNKS
+
+    def weight_copies():
+        yield pltpu.make_async_copy(wo_hbm.at[pl.ds(k * o_rows, o_rows)], wo, w_sem)
+        for c in range(n_gate):
+            cols = pl.ds(pl.multiple_of(k * m_cols + c * g_cols, LANES), g_cols)
+            yield pltpu.make_async_copy(wg_hbm.at[:, cols], wg.at[c], g_sem.at[c])
+            yield pltpu.make_async_copy(wu_hbm.at[:, cols], wu.at[c], u_sem.at[c])
+        for c in range(n_down):
+            yield pltpu.make_async_copy(
+                wd_hbm.at[pl.ds(pl.multiple_of(k * m_cols + c * d_rows, 8), d_rows)], wd.at[c], d_sem.at[c]
+            )
+
+    for copy in weight_copies():
+        copy.start()
+
+    barrier = pltpu.get_barrier_semaphore()
+    for dev in (d_dev, x_dev, y_dev):
+        pl.semaphore_signal(barrier, inc=1, device_id=dev, device_id_type=MESH)
+    pl.semaphore_wait(barrier, 3)
+
+    counter = [0]
+
+    def remote(src, dst, dev):
+        n = counter[0]
+        counter[0] += 1
+        return pltpu.make_async_remote_copy(
+            src_ref=src, dst_ref=dst, send_sem=send_sem.at[n], recv_sem=recv_sem.at[n],
+            device_id=dev, device_id_type=MESH,
+        )
+
+    far_rows, near_rows = pl.ds((1 - x) * half, half), pl.ds(x * half, half)
+    swap = remote(part_ref.at[pl.ds((1 - k) * mine_h, mine_h)], rd, d_dev)
+    swap.start()
+    swap.wait_recv()
+    my_heads = pl.ds(k * mine_h, mine_h)
+
+    def chip_part(at):
+        return combine(
+            [part_ref[my_heads, i, at] for i in range(3)], [rd[:, i, at] for i in range(3)]
+        )
+
+    left = lax.broadcasted_iota(jnp.int32, (mine_h, half, LANES), 2) < LANES // 2
+    o_a, o_b, m, l = chip_part(far_rows)
+    sx[:, 0], sx[:, 1], sx[:, 2] = o_a, o_b, jnp.where(left, m, l)
+    cross = remote(sx, rx, x_dev)
+    cross.start()
+    o_a, o_b, m, l = chip_part(near_rows)
+    cross.wait_recv()
+    o_a, o_b, _, l = combine([o_a, o_b, jnp.where(left, m, l)], [rx[:, i] for i in range(3)])
+    o_a, o_b = (o_a / l).astype(BF16), (o_b / l).astype(BF16)
+    attended = jnp.concatenate([v[h] for h in range(mine_h) for v in (o_a, o_b)], axis=-1)
+
+    own, other = pl.ds(k * quarter, quarter), pl.ds((1 - k) * quarter, quarter)
+    my_rows = pl.ds(pl.multiple_of(x * half + k * quarter, quarter), quarter)
+    x_peer_rows = pl.ds(pl.multiple_of((1 - x) * half + k * quarter, quarter), quarter)
+    cols = [pl.ds(c * span, span) for c in range(CHUNKS)]
+
+    def staged(stages):
+        for t in range(CHUNKS + len(stages) - 1):
+            for s in reversed(range(len(stages))):
+                if 0 <= t - s < CHUNKS:
+                    stages[s](t - s)
+
+    swaps = [remote(po.at[other, c], ro.at[:, c], d_dev) for c in cols]
+    crosses = [remote(so.at[:, c], yo.at[:, c], y_dev) for c in cols]
+    gathers = [remote(hb.at[own, c], hb.at[own, c], d_dev) for c in cols]
+    weights = weight_copies()
+    next(weights).wait()
+
+    def o_dot(c):
+        po[:, cols[c]] = jnp.dot(attended, wo[:, cols[c]], preferred_element_type=F32)
+        swaps[c].start()
+
+    def o_swap(c):
+        swaps[c].wait_recv()
+        so[:, cols[c]] = po[own, cols[c]] + ro[:, cols[c]]
+        crosses[c].start()
+
+    def o_cross(c):
+        crosses[c].wait_recv()
+        total = so[:, cols[c]] + yo[:, cols[c]]
+        hb[own, cols[c]] = (x_ref[my_rows, cols[c]].astype(F32) + total).astype(BF16).astype(F32)
+        gathers[c].start()
+
+    def o_gather(c):
+        gathers[c].wait_recv()
+
+    staged([o_dot, o_swap, o_cross, o_gather])
+
+    normed = rms_norm(hb[...], gain_ref[...])
+    for c in range(n_gate):
+        next(weights).wait()
+        next(weights).wait()
+        gate = jnp.dot(normed, wg[c], preferred_element_type=F32)
+        up = jnp.dot(normed, wu[c], preferred_element_type=F32)
+        act[:, c * g_cols : (c + 1) * g_cols] = (jax.nn.silu(gate) * up).astype(BF16)
+    for copy in weights:
+        copy.wait()
+
+    swaps_m = [remote(pm.at[other, c], rm.at[:, c], d_dev) for c in cols]
+    crosses_m = [remote(sm.at[:, c], ym.at[:, c], y_dev) for c in cols]
+    to_core = [remote(ob.at[my_rows, c], ob.at[my_rows, c], d_dev) for c in cols]
+    to_x = [remote(ob.at[my_rows, c], ob.at[my_rows, c], x_dev) for c in cols]
+    onward = [remote(ob.at[x_peer_rows, c], ob.at[x_peer_rows, c], d_dev) for c in cols]
+
+    def m_dot(c):
+        total = None
+        for r in range(n_down):
+            piece = jnp.dot(
+                act[:, r * d_rows : (r + 1) * d_rows], wd[r, :, cols[c]], preferred_element_type=F32
+            )
+            total = piece if total is None else total + piece
+        pm[:, cols[c]] = total
+        swaps_m[c].start()
+
+    def m_swap(c):
+        swaps_m[c].wait_recv()
+        sm[:, cols[c]] = pm[own, cols[c]] + rm[:, cols[c]]
+        crosses_m[c].start()
+
+    def m_cross(c):
+        crosses_m[c].wait_recv()
+        total = sm[:, cols[c]] + ym[:, cols[c]]
+        ob[my_rows, cols[c]] = (hb[own, cols[c]] + total).astype(BF16).astype(F32)
+        to_x[c].start()
+        to_core[c].start()
+
+    def m_gather(c):
+        to_x[c].wait_recv()
+        onward[c].start()
+
+    def m_last(c):
+        to_core[c].wait_recv()
+        onward[c].wait_recv()
+        out_ref[:, cols[c]] = ob[:, cols[c]].astype(BF16)
+
+    staged([m_dot, m_swap, m_cross, m_gather, m_last])
+    for copy in [swap, cross, *swaps, *crosses, *gathers, *swaps_m, *crosses_m, *to_core, *to_x, *onward]:
+        copy.wait_send()
+
+
+def tail(part, tokens, gain, w_o, w_gate, w_up, w_down):
+    heads, _, rows, _ = part.shape
+    width = tokens.shape[1]
+    half, quarter = rows // 2, rows // 4
+    cut = w_gate.shape[1] // 2
+    n_gate, n_down = cut // 256, 4
+    vmem = pl.BlockSpec(memory_space=pltpu.VMEM)
+    hbm = pl.BlockSpec(memory_space=pl.ANY)
+    flat = lambda n: pltpu.VMEM((n, width), F32)
+    stats = lambda n: pltpu.VMEM((heads // 2, 3, n, LANES), F32)
+    n_remote = 2 + 8 * CHUNKS
+    return pl.pallas_call(
+        tail_kernel,
+        out_shape=jax.ShapeDtypeStruct(tokens.shape, BF16),
+        in_specs=[vmem, vmem, vmem] + [hbm] * 4,
+        out_specs=vmem,
+        scratch_shapes=[
+            pltpu.VMEM((w_o.shape[0] // 2, width), BF16),
+            pltpu.VMEM((n_gate, width, 256), BF16),
+            pltpu.VMEM((n_gate, width, 256), BF16),
+            pltpu.VMEM((n_down, cut // n_down, width), BF16),
+            stats(rows), stats(half), stats(half),
+            flat(half), flat(quarter), flat(quarter), flat(quarter), flat(half),
+            pltpu.VMEM((half, cut), BF16),
+            flat(half), flat(quarter), flat(quarter), flat(quarter), flat(rows),
+            pltpu.SemaphoreType.DMA,
+            pltpu.SemaphoreType.DMA((n_gate,)),
+            pltpu.SemaphoreType.DMA((n_gate,)),
+            pltpu.SemaphoreType.DMA((n_down,)),
+            pltpu.SemaphoreType.DMA((n_remote,)),
+            pltpu.SemaphoreType.DMA((n_remote,)),
+        ],
+        compiler_params=pltpu.CompilerParams(
+            vmem_limit_bytes=60 << 20, collective_id=0, has_side_effects=True
+        ),
+        name="tail",
+    )(part, tokens, gain, w_o, w_gate, w_up, w_down)
+
+
 def to_rows(cache):
     b, s, kv, d = cache.shape
     return cache.reshape(b, s, kv, d // LANES, LANES).transpose(0, 1, 3, 2, 4).reshape(b, -1, LANES)
@@ -235,29 +453,12 @@
     out_specs = (row_spec, cache_spec, cache_spec)
 
     def local_step(tokens, positions, cache_k, cache_v, attn_gain, w_q, w_k, w_v, w_o, mlp_gain, w_gate, w_up, w_down):
-        rows = tokens.shape[0]
         part, rows_k, rows_v = attention(
             positions, tokens, attn_gain, w_q, w_k, w_v, to_rows(cache_k), to_rows(cache_v)
         )
         new_k = from_rows(rows_k, cache_k.shape)
         new_v = from_rows(rows_v, cache_v.shape)
-        heads = part.shape[0]
-        local_max, local_sum = part[:, 2, :, 0], part[:, 2, :, LANES // 2]
-        global_max = lax.pmax(local_max, "sp")
-        factor = jnp.exp(local_max - global_max)[..., None]
-        packed = jnp.concatenate([part[:, 0] * factor, part[:, 1] * factor, local_sum[..., None] * factor], axis=-1)
-        total = lax.psum(packed, "sp")
-        attended = (total[..., : 2 * LANES] / total[..., 2 * LANES :]).astype(BF16)
-        attended = attended.transpose(1, 0, 2).reshape(rows, heads * 2 * LANES)
-
-        attn_proj = lax.psum(jnp.dot(attended, w_o, preferred_element_type=F32), "tp")
-        hidden = (tokens.astype(F32) + attn_proj).astype(BF16)
-        normed_mlp = rms_norm(hidden, mlp_gain)
-        gate_proj = jnp.dot(normed_mlp, w_gate, preferred_element_type=F32)
-        up_proj = jnp.dot(normed_mlp, w_up, preferred_element_type=F32)
-        activated = (jax.nn.silu(gate_proj) * up_proj).astype(BF16)
-        mlp_down = lax.psum(jnp.dot(activated, w_down, preferred_element_type=F32), "tp")
-        layer_out = (hidden.astype(F32) + mlp_down).astype(BF16)
+        layer_out = tail(part, tokens, mlp_gain, w_o, w_gate, w_up, w_down)
         return layer_out, new_k, new_v
 
     return jax.shard_map(local_step, mesh=mesh, in_specs=in_specs, out_specs=out_specs, check_vma=False)

time: 176 us -> 77.2 us (0.44)
  waiting for transfers between devices: 78.9 us -> 0 us
  Pallas kernels: 28.8 us -> 74.7 us
  matrix products: 36.9 us -> 0 us
  between operations: 13.8 us -> 0.65 us
  blocking collectives: 8.75 us -> 0 us
  other arithmetic: 6.08 us -> 0 us
    psum x3 -> x0, waiting for transfers between devices: 78.8 us -> none  [the longest x1 27.2 us: local_step(): total = lax.psum(packed, 'sp')]
    pallas_call x0 -> x1, Pallas kernels: none -> 46 us  [tail(): pl.pallas_call(tail_kernel, out_shape=jax.ShapeDtypeStruct(tokens.shape,...]
    dot_general x3 -> x0, matrix products: 36.9 us -> none  [the longest x1 21.6 us: local_step(): jnp.dot(activated, w_down, preferred_element_type=F32)]
    pmax x1 -> x0, blocking collectives: 8.75 us -> none  [local_step(): global_max = lax.pmax(local_max, 'sp')]
    slice x2 -> x0, local copies, waits for them, and re-layouts: 2.22 us -> none  [the longest x1 1.21 us: local_step(): local_max, local_sum = (part[:, 2, :, 0], part[:, 2, :, LANES // 2])]
    convert_element_type x2 -> x0, other arithmetic: 1.87 us -> none  [the longest x1 1.87 us: local_step(): layer_out = (hidden.astype(F32) + mlp_down).astype(BF16)]
  transfers between devices with their start and end apart: 3 -> 0, of which waited for: 3 -> 0; matrix products, arithmetic and copies ran while one was open for 0% -> 0% of each run, Pallas kernels for 0% -> 0%
where the time goes in v2:
time: 77.2 us; the launch traced here: 77.1 us
  Pallas kernels  74.7 us (97%)
  local copies, waits for them, and re-layouts  1.72 us (2%)
    pallas_call x1, Pallas kernels, tail(): pl.pallas_call(tail_kernel, out_shape=jax.ShapeDtypeStruct(tokens.shape,...  46 us
    pallas_call x1, Pallas kernels, attention(): pl.pallas_call(attention_kernel, out_shape=(jax.ShapeDtypeStruct((heads,...  28.8 us
    unnamed x1, local copies, waits for them, and re-layouts  1.72 us

profile of v2, /device:TPU:0, one launch (start us, length us, event | category | flops | bytes accessed | tf_op | source)
XLA Modules:
  0.0 77.1 jit_solution(5238206506908201332)
XLA Ops:
  0.6 28.8 %attention_part.1 = (f32[4,3,64,128]{3,2,1,0:T(8,128)}, bf16[64,1024,128]{2,1,0:T(8,128)(2,1)}, bf16[64,1024,128]{2,1,0:T(8,128)(2,1)}) custom-call(s32[64]{0:T(128)} %pos.1, bf16[64,2560]{1,0:T(8,128)(2,1)} %x_ref.3, bf16[2560]{0:T(1024)(128)(2,1)} %gain_ref.2, bf16[2560,1024]{1,0:T(8,128)(2,1)} %wq_hbm.1, bf16[2560,512]{1,0:T(8,128)(2,1)} %wk_hbm.1, ...), custom_call_target="tpu_custom_call" | custom-call | tf_op jit(solution)/shard_map/attention_part/pallas_call | solution.py:190
  29.4 46.0 %tail.1 = bf16[64,2560]{1,0:T(8,128)(2,1)} custom-call(f32[4,3,64,128]{3,2,1,0:T(8,128)} %get-tuple-element.6.part_ref, bf16[64,2560]{1,0:T(8,128)(2,1)} %x_ref.3, bf16[2560]{0:T(1024)(128)(2,1)} %gain_ref.3, bf16[1024,2560]{1,0:T(8,128)(2,1)} %wo_hbm.1, bf16[2560,5120]{1,0:T(8,128)(2,1)} %wg_hbm.1, bf16[2560,5120]{1,0:T(8,128)(2,1)} %wu_hbm.1, ...), custom_call_target="tpu_custom_call" | custom-call | tf_op jit(solution)/shard_map/tail/pallas_call | solution.py:410
  75.4 1.7 %copy.21 = bf16[64,2560]{1,0:T(8,128)(2,1)} copy(bf16[64,2560]{1,0:T(8,128)(2,1)} %tail.1) | data formatting | bytes 655360

commit v3 on v2

--- a/solution.py
+++ b/solution.py
@@ -1,4 +1,5 @@
 import functools
+import itertools
 import math
 
 import jax
@@ -25,10 +26,10 @@
 
 
 def attention_kernel(
-    pos, x_ref, gain_ref, wq_hbm, wk_hbm, wv_hbm, ck_hbm, cv_hbm,
+    pos_hbm, x_hbm, gain_hbm, wq_hbm, wk_hbm, wv_hbm, ck_hbm, cv_hbm,
     part_ref, nk_hbm, nv_hbm,
     wbuf, kbuf, vbuf, q_s, kn_s, vn_s, ang_s, o_s, m_s, l_s,
-    w_sem, k_sem, v_sem, out_sem,
+    pos, x_ref, gain_ref, w_sem, k_sem, v_sem, out_sem, x_sem,
 ):
     rows = x_ref.shape[0]
     head_dim = 2 * LANES
@@ -64,6 +65,12 @@
             pltpu.make_async_copy(vbuf.at[span], nv_hbm.at[span], out_sem.at[1]),
         )
 
+    small = [
+        pltpu.make_async_copy(src, dst, x_sem.at[i])
+        for i, (src, dst) in enumerate(((pos_hbm, pos), (x_hbm, x_ref), (gain_hbm, gain_ref)))
+    ]
+    for copy in small:
+        copy.start()
     n_w = heads + 2 * kvs
     for n in range(n_w):
         w_copy(n).start()
@@ -73,6 +80,9 @@
 
     lane = lax.broadcasted_iota(jnp.int32, (1, LANES), 1).astype(F32)
     freq = jnp.exp2(lane * (-math.log2(ROPE_THETA) / LANES))
+
+    for copy in small:
+        copy.wait()
 
     def angle_row(b, carry):
         ang_s[pl.ds(b, 1), :] = freq * pos[b].astype(F32)
@@ -185,16 +195,16 @@
     kvs = w_k.shape[1] // head_dim
     qrows = 2 * heads
     vmem = pl.BlockSpec(memory_space=pltpu.VMEM)
-    hbm = pl.BlockSpec(memory_space=pl.ANY)
+    hbm = pl.BlockSpec(memory_space=pltpu.HBM)
     n_blocks = rows // BLOCK
     return pl.pallas_call(
         attention_kernel,
         out_shape=(
-            jax.ShapeDtypeStruct((heads, 3, rows, LANES), F32),
+            pltpu.VMEM((heads, 3, rows, LANES), F32),
             jax.ShapeDtypeStruct(rows_k.shape, BF16),
             jax.ShapeDtypeStruct(rows_v.shape, BF16),
         ),
-        in_specs=[pl.BlockSpec(memory_space=pltpu.SMEM), vmem, vmem] + [hbm] * 5,
+        in_specs=[hbm] * 8,
         out_specs=(vmem, hbm, hbm),
         scratch_shapes=[
             pltpu.VMEM((heads + 2 * kvs, width, head_dim), BF16),
@@ -207,17 +217,21 @@
             pltpu.VMEM((rows * qrows, LANES), F32),
             pltpu.VMEM((rows * qrows, LANES), F32),
             pltpu.VMEM((rows * qrows, LANES), F32),
+            pltpu.SMEM((rows,), jnp.int32),
+            pltpu.VMEM(tokens.shape, BF16),
+            pltpu.VMEM(gain.shape, BF16),
             pltpu.SemaphoreType.DMA((heads + 2 * kvs,)),
             pltpu.SemaphoreType.DMA((n_blocks,)),
             pltpu.SemaphoreType.DMA((n_blocks,)),
             pltpu.SemaphoreType.DMA((2,)),
+            pltpu.SemaphoreType.DMA((3,)),
         ],
-        compiler_params=pltpu.CompilerParams(vmem_limit_bytes=60 << 20),
+        compiler_params=pltpu.CompilerParams(vmem_limit_bytes=52 << 20),
         name="attention_part",
-    )(positions, tokens, gain, w_q, w_k, w_v, rows_k, rows_v)
-
-
-CHUNKS = 2
+    )(*(pltpu.with_memory_space_constraint(v, pltpu.HBM) for v in (positions, tokens, gain)), w_q, w_k, w_v, rows_k, rows_v)
+
+
+CHUNKS = 5
 MESH = pl.DeviceIdType.MESH
 
 
@@ -252,27 +266,30 @@
     o_rows, n_gate = wo.shape[0], wg.shape[0]
     g_cols = wg.shape[2]
     m_cols = n_gate * g_cols
-    n_down = wd.shape[0]
-    d_rows = wd.shape[1]
+    d_rows = g_cols
+    n_down = wd.shape[0] // d_rows
     span = width // CHUNKS
-
-    def weight_copies():
-        yield pltpu.make_async_copy(wo_hbm.at[pl.ds(k * o_rows, o_rows)], wo, w_sem)
-        for c in range(n_gate):
-            cols = pl.ds(pl.multiple_of(k * m_cols + c * g_cols, LANES), g_cols)
-            yield pltpu.make_async_copy(wg_hbm.at[:, cols], wg.at[c], g_sem.at[c])
-            yield pltpu.make_async_copy(wu_hbm.at[:, cols], wu.at[c], u_sem.at[c])
-        for c in range(n_down):
-            yield pltpu.make_async_copy(
-                wd_hbm.at[pl.ds(pl.multiple_of(k * m_cols + c * d_rows, 8), d_rows)], wd.at[c], d_sem.at[c]
-            )
-
-    for copy in weight_copies():
-        copy.start()
 
     barrier = pltpu.get_barrier_semaphore()
     for dev in (d_dev, x_dev, y_dev):
         pl.semaphore_signal(barrier, inc=1, device_id=dev, device_id_type=MESH)
+
+    o_copy = pltpu.make_async_copy(wo_hbm.at[pl.ds(k * o_rows, o_rows)], wo, w_sem)
+    g_copies, d_copies = [], []
+    for c in range(n_gate):
+        at = pl.ds(pl.multiple_of(k * m_cols + c * g_cols, LANES), g_cols)
+        g_copies.append(pltpu.make_async_copy(wg_hbm.at[:, at], wg.at[c], g_sem.at[c]))
+        g_copies.append(pltpu.make_async_copy(wu_hbm.at[:, at], wu.at[c], u_sem.at[c]))
+    for c in range(n_down):
+        at = pl.ds(pl.multiple_of(k * m_cols + c * d_rows, LANES), d_rows)
+        d_copies.append(pltpu.make_async_copy(wd_hbm.at[at], wd.at[pl.ds(c * d_rows, d_rows)], d_sem.at[c]))
+    queue = iter(g_copies + d_copies)
+
+    def fetch(n):
+        for copy in itertools.islice(queue, n):
+            copy.start()
+
+    o_copy.start()
     pl.semaphore_wait(barrier, 3)
 
     counter = [0]
@@ -288,6 +305,7 @@
     far_rows, near_rows = pl.ds((1 - x) * half, half), pl.ds(x * half, half)
     swap = remote(part_ref.at[pl.ds((1 - k) * mine_h, mine_h)], rd, d_dev)
     swap.start()
+    fetch(2)
     swap.wait_recv()
     my_heads = pl.ds(k * mine_h, mine_h)
 
@@ -301,6 +319,7 @@
     sx[:, 0], sx[:, 1], sx[:, 2] = o_a, o_b, jnp.where(left, m, l)
     cross = remote(sx, rx, x_dev)
     cross.start()
+    fetch(8)
     o_a, o_b, m, l = chip_part(near_rows)
     cross.wait_recv()
     o_a, o_b, _, l = combine([o_a, o_b, jnp.where(left, m, l)], [rx[:, i] for i in range(3)])
@@ -312,17 +331,23 @@
     x_peer_rows = pl.ds(pl.multiple_of((1 - x) * half + k * quarter, quarter), quarter)
     cols = [pl.ds(c * span, span) for c in range(CHUNKS)]
 
-    def staged(stages):
-        for t in range(CHUNKS + len(stages) - 1):
-            for s in reversed(range(len(stages))):
-                if 0 <= t - s < CHUNKS:
-                    stages[s](t - s)
+    def staged(dot, swap, cross, *rest):
+        for c in range(CHUNKS + 2):
+            if c < CHUNKS:
+                dot(c)
+            if c >= 2:
+                swap(c - 2)
+        for c in range(CHUNKS):
+            cross(c)
+        for c in range(CHUNKS + len(rest) - 1):
+            for s, stage in enumerate(rest):
+                if 0 <= c - s < CHUNKS:
+                    stage(c - s)
 
     swaps = [remote(po.at[other, c], ro.at[:, c], d_dev) for c in cols]
     crosses = [remote(so.at[:, c], yo.at[:, c], y_dev) for c in cols]
     gathers = [remote(hb.at[own, c], hb.at[own, c], d_dev) for c in cols]
-    weights = weight_copies()
-    next(weights).wait()
+    o_copy.wait()
 
     def o_dot(c):
         po[:, cols[c]] = jnp.dot(attended, wo[:, cols[c]], preferred_element_type=F32)
@@ -332,6 +357,7 @@
         swaps[c].wait_recv()
         so[:, cols[c]] = po[own, cols[c]] + ro[:, cols[c]]
         crosses[c].start()
+        fetch(3)
 
     def o_cross(c):
         crosses[c].wait_recv()
@@ -342,16 +368,17 @@
     def o_gather(c):
         gathers[c].wait_recv()
 
-    staged([o_dot, o_swap, o_cross, o_gather])
+    staged(o_dot, o_swap, o_cross, o_gather)
+    fetch(len(g_copies) + len(d_copies))
 
     normed = rms_norm(hb[...], gain_ref[...])
     for c in range(n_gate):
-        next(weights).wait()
-        next(weights).wait()
+        g_copies[2 * c].wait()
+        g_copies[2 * c + 1].wait()
         gate = jnp.dot(normed, wg[c], preferred_element_type=F32)
         up = jnp.dot(normed, wu[c], preferred_element_type=F32)
         act[:, c * g_cols : (c + 1) * g_cols] = (jax.nn.silu(gate) * up).astype(BF16)
-    for copy in weights:
+    for copy in d_copies:
         copy.wait()
 
     swaps_m = [remote(pm.at[other, c], rm.at[:, c], d_dev) for c in cols]
@@ -361,13 +388,7 @@
     onward = [remote(ob.at[x_peer_rows, c], ob.at[x_peer_rows, c], d_dev) for c in cols]
 
     def m_dot(c):
-        total = None
-        for r in range(n_down):
-            piece = jnp.dot(
-                act[:, r * d_rows : (r + 1) * d_rows], wd[r, :, cols[c]], preferred_element_type=F32
-            )
-            total = piece if total is None else total + piece
-        pm[:, cols[c]] = total
+        pm[:, cols[c]] = jnp.dot(act[...], wd[:, cols[c]], preferred_element_type=F32)
         swaps_m[c].start()
 
     def m_swap(c):
@@ -391,7 +412,7 @@
         onward[c].wait_recv()
         out_ref[:, cols[c]] = ob[:, cols[c]].astype(BF16)
 
-    staged([m_dot, m_swap, m_cross, m_gather, m_last])
+    staged(m_dot, m_swap, m_cross, m_gather, m_last)
     for copy in [swap, cross, *swaps, *crosses, *gathers, *swaps_m, *crosses_m, *to_core, *to_x, *onward]:
         copy.wait_send()
 
@@ -401,22 +422,22 @@
     width = tokens.shape[1]
     half, quarter = rows // 2, rows // 4
     cut = w_gate.shape[1] // 2
-    n_gate, n_down = cut // 256, 4
+    n_gate = cut // 256
     vmem = pl.BlockSpec(memory_space=pltpu.VMEM)
-    hbm = pl.BlockSpec(memory_space=pl.ANY)
+    hbm = pl.BlockSpec(memory_space=pltpu.HBM)
     flat = lambda n: pltpu.VMEM((n, width), F32)
     stats = lambda n: pltpu.VMEM((heads // 2, 3, n, LANES), F32)
     n_remote = 2 + 8 * CHUNKS
     return pl.pallas_call(
         tail_kernel,
-        out_shape=jax.ShapeDtypeStruct(tokens.shape, BF16),
+        out_shape=pltpu.VMEM(tokens.shape, BF16),
         in_specs=[vmem, vmem, vmem] + [hbm] * 4,
         out_specs=vmem,
         scratch_shapes=[
             pltpu.VMEM((w_o.shape[0] // 2, width), BF16),
             pltpu.VMEM((n_gate, width, 256), BF16),
             pltpu.VMEM((n_gate, width, 256), BF16),
-            pltpu.VMEM((n_down, cut // n_down, width), BF16),
+            pltpu.VMEM((cut, width), BF16),
             stats(rows), stats(half), stats(half),
             flat(half), flat(quarter), flat(quarter), flat(quarter), flat(half),
             pltpu.VMEM((half, cut), BF16),
@@ -424,12 +445,12 @@
             pltpu.SemaphoreType.DMA,
             pltpu.SemaphoreType.DMA((n_gate,)),
             pltpu.SemaphoreType.DMA((n_gate,)),
-            pltpu.SemaphoreType.DMA((n_down,)),
+            pltpu.SemaphoreType.DMA((n_gate,)),
             pltpu.SemaphoreType.DMA((n_remote,)),
             pltpu.SemaphoreType.DMA((n_remote,)),
         ],
         compiler_params=pltpu.CompilerParams(
-            vmem_limit_bytes=60 << 20, collective_id=0, has_side_effects=True
+            vmem_limit_bytes=50 << 20, collective_id=0, has_side_effects=True
         ),
         name="tail",
     )(part, tokens, gain, w_o, w_gate, w_up, w_down)

time: 77.2 us -> 66.4 us (0.86)
  Pallas kernels: 74.7 us -> 64.9 us
  local copies, waits for them, and re-layouts: 1.72 us -> 0.74 us
    pallas_call x2, Pallas kernels: 74.7 us -> 64.9 us  [the longest x1 34.2 us: tail(): pl.pallas_call(tail_kernel, out_shape=pltpu.VMEM(tokens.shape, BF16), in_...]
    unnamed x1 -> x5, local copies, waits for them, and re-layouts: 1.72 us -> 0.74 us
where the time goes in v3:
time: 66.4 us; the launch traced here: 66.3 us
  Pallas kernels  64.9 us (98%)
  local copies, waits for them, and re-layouts  0.74 us (1%)
  between operations  0.68 us (1%)
    pallas_call x1, Pallas kernels, tail(): pl.pallas_call(tail_kernel, out_shape=pltpu.VMEM(tokens.shape, BF16), in_...  34.2 us
    pallas_call x1, Pallas kernels, attention(): pl.pallas_call(attention_kernel, out_shape=(pltpu.VMEM((heads, 3, rows, L...  30.7 us

profile of v3, /device:TPU:0, one launch (start us, length us, event | category | flops | bytes accessed | tf_op | source)
XLA Modules:
  0.0 66.3 jit_solution(10672861046021419740)
XLA Ops:
  0.6 0.0 copy-start
  0.6 0.0 copy-start.1
  0.7 30.7 %attention_part.1 = (f32[4,3,64,128]{3,2,1,0:T(8,128)S(1)}, bf16[64,1024,128]{2,1,0:T(8,128)(2,1)}, bf16[64,1024,128]{2,1,0:T(8,128)(2,1)}) custom-call(s32[64]{0:T(128)} %pos_hbm.1, bf16[64,2560]{1,0:T(8,128)(2,1)} %x_ref.1, bf16[2560]{0:T(1024)(128)(2,1)} %gain_hbm.1, bf16[2560,1024]{1,0:T(8,128)(2,1)} %wq_hbm.1, bf16[2560,512]{1,0:T(8,128)(2,1)} %wk_hbm.1, ...), custom_call_target="tpu_custom_call" | custom-call | tf_op jit(solution)/shard_map/attention_part/pallas_call | solution.py:200
  31.4 0.0 copy-done
  31.4 0.0 copy-done.1
  31.4 34.2 %tail.1 = bf16[64,2560]{1,0:T(8,128)(2,1)S(1)} custom-call(f32[4,3,64,128]{3,2,1,0:T(8,128)S(1)} %get-tuple-element.6.part_ref, bf16[64,2560]{1,0:T(8,128)(2,1)S(1)} %copy-done, bf16[2560]{0:T(1024)(128)(2,1)S(1)} %copy-done.1, bf16[1024,2560]{1,0:T(8,128)(2,1)} %wo_hbm.1, bf16[2560,5120]{1,0:T(8,128)(2,1)} %wg_hbm.1, bf16[2560,5120]{1,0:T(8,128)(2,1)} %wu_hbm.1, ...), custom_call_target="tpu_custom_call" | custom-call | tf_op jit(solution)/shard_map/tail/pallas_call | solution.py:431
  65.6 0.7 %copy.21 = bf16[64,2560]{1,0:T(8,128)(2,1)} copy(bf16[64,2560]{1,0:T(8,128)(2,1)S(1)} %tail.1) | data formatting | bytes 655360
Async XLA Ops:
  0.6 30.7 %copy-start = (bf16[64,2560]{1,0:T(8,128)(2,1)S(1)}, bf16[64,2560]{1,0:T(8,128)(2,1)}, u32[]{:S(2)}) copy-start(bf16[64,2560]{1,0:T(8,128)(2,1)} %x_ref.1) | copy-start | bytes 983044
  0.6 30.7 %copy-start.1 = (bf16[2560]{0:T(1024)(128)(2,1)S(1)}, bf16[2560]{0:T(1024)(128)(2,1)}, u32[]{:S(2)}) copy-start(bf16[2560]{0:T(1024)(128)(2,1)} %gain_ref.1) | copy-start | bytes 15364

commit v4 on v3

--- a/solution.py
+++ b/solution.py
@@ -16,7 +16,7 @@
 BF16 = jnp.bfloat16
 FAR = 1 << 28
 BLOCK = 4
-AHEAD = 5
+FIRST = 4
 
 
 def rms_norm(values, gain):
@@ -72,17 +72,20 @@
     for copy in small:
         copy.start()
     n_w = heads + 2 * kvs
-    for n in range(n_w):
+    ahead = FIRST + n_w
+    for n in range(n_w // 2):
         w_copy(n).start()
-    for j in range(AHEAD):
+
+    lane = lax.broadcasted_iota(jnp.int32, (1, LANES), 1).astype(F32)
+    freq = jnp.exp2(lane * (-math.log2(ROPE_THETA) / LANES))
+
+    for copy in small:
+        copy.wait()
+    for n in range(n_w // 2, n_w):
+        w_copy(n).start()
+    for j in range(FIRST):
         for copy in in_copies(j):
             copy.start()
-
-    lane = lax.broadcasted_iota(jnp.int32, (1, LANES), 1).astype(F32)
-    freq = jnp.exp2(lane * (-math.log2(ROPE_THETA) / LANES))
-
-    for copy in small:
-        copy.wait()
 
     def angle_row(b, carry):
         ang_s[pl.ds(b, 1), :] = freq * pos[b].astype(F32)
@@ -95,6 +98,8 @@
 
     for n in range(n_w):
         w_copy(n).wait()
+        for copy in in_copies(FIRST + n):
+            copy.start()
         lin = jnp.dot(normed, wbuf[n], preferred_element_type=F32)
         first, second = lin[:, :LANES], lin[:, LANES:]
         if not kvs <= n < 2 * kvs:
@@ -119,9 +124,9 @@
     scale = 1.0 / math.sqrt(head_dim)
 
     def block_step(j, carry):
-        @pl.when(j + AHEAD < n_blocks)
+        @pl.when(j + ahead < n_blocks)
         def _():
-            for copy in in_copies(j + AHEAD):
+            for copy in in_copies(j + ahead):
                 copy.start()
 
         for copy in in_copies(j):

time: 66.4 us -> 62.4 us (0.940)
  Pallas kernels: 64.9 us -> 60.8 us
    pallas_call x1, Pallas kernels: 30.7 us -> 26.6 us  [attention(): pl.pallas_call(attention_kernel, out_shape=(pltpu.VMEM((heads, 3, rows, L...]
where the time goes in v4:
time: 62.4 us; the launch traced here: 62.3 us
  Pallas kernels  60.8 us (97%)
  local copies, waits for them, and re-layouts  0.74 us (1%)
  between operations  0.68 us (1%)
    pallas_call x1, Pallas kernels, tail(): pl.pallas_call(tail_kernel, out_shape=pltpu.VMEM(tokens.shape, BF16), in_...  34.2 us
    pallas_call x1, Pallas kernels, attention(): pl.pallas_call(attention_kernel, out_shape=(pltpu.VMEM((heads, 3, rows, L...  26.6 us

profile of v4, /device:TPU:0, one launch (start us, length us, event | category | flops | bytes accessed | tf_op | source)
XLA Modules:
  0.0 62.3 jit_solution(10043745636629412004)
XLA Ops:
  0.6 0.0 copy-start
  0.6 0.0 copy-start.1
  0.7 26.6 %attention_part.1 = (f32[4,3,64,128]{3,2,1,0:T(8,128)S(1)}, bf16[64,1024,128]{2,1,0:T(8,128)(2,1)}, bf16[64,1024,128]{2,1,0:T(8,128)(2,1)}) custom-call(s32[64]{0:T(128)} %pos_hbm.1, bf16[64,2560]{1,0:T(8,128)(2,1)} %x_ref.1, bf16[2560]{0:T(1024)(128)(2,1)} %gain_hbm.1, bf16[2560,1024]{1,0:T(8,128)(2,1)} %wq_hbm.1, bf16[2560,512]{1,0:T(8,128)(2,1)} %wk_hbm.1, ...), custom_call_target="tpu_custom_call" | custom-call | tf_op jit(solution)/shard_map/attention_part/pallas_call | solution.py:205
  27.3 0.0 copy-done
  27.3 0.0 copy-done.1
  27.3 34.2 %tail.1 = bf16[64,2560]{1,0:T(8,128)(2,1)S(1)} custom-call(f32[4,3,64,128]{3,2,1,0:T(8,128)S(1)} %get-tuple-element.6.part_ref, bf16[64,2560]{1,0:T(8,128)(2,1)S(1)} %copy-done, bf16[2560]{0:T(1024)(128)(2,1)S(1)} %copy-done.1, bf16[1024,2560]{1,0:T(8,128)(2,1)} %wo_hbm.1, bf16[2560,5120]{1,0:T(8,128)(2,1)} %wg_hbm.1, bf16[2560,5120]{1,0:T(8,128)(2,1)} %wu_hbm.1, ...), custom_call_target="tpu_custom_call" | custom-call | tf_op jit(solution)/shard_map/tail/pallas_call | solution.py:436
  61.5 0.7 %copy.21 = bf16[64,2560]{1,0:T(8,128)(2,1)} copy(bf16[64,2560]{1,0:T(8,128)(2,1)S(1)} %tail.1) | data formatting | bytes 655360
Async XLA Ops:
  0.6 26.7 %copy-start = (bf16[64,2560]{1,0:T(8,128)(2,1)S(1)}, bf16[64,2560]{1,0:T(8,128)(2,1)}, u32[]{:S(2)}) copy-start(bf16[64,2560]{1,0:T(8,128)(2,1)} %x_ref.1) | copy-start | bytes 983044
  0.6 26.7 %copy-start.1 = (bf16[2560]{0:T(1024)(128)(2,1)S(1)}, bf16[2560]{0:T(1024)(128)(2,1)}, u32[]{:S(2)}) copy-start(bf16[2560]{0:T(1024)(128)(2,1)} %gain_ref.1) | copy-start | bytes 15364

commit v5 on v4

v5 whole, which is shorter than its diff:
```python
import functools
import itertools
import math

import jax
import jax.numpy as jnp
from jax import lax
from jax.experimental import pallas as pl
from jax.experimental.pallas import tpu as pltpu
from jax.sharding import PartitionSpec as P

NORM_EPS = 1e-5
ROPE_THETA = 10000.0
LANES = 128
F32 = jnp.float32
BF16 = jnp.bfloat16
FAR = 1 << 28
BLOCK = 4
AHEAD = 3
FIRST = 4
SLOTS = 22
LAYER_VMEM = 35
CHUNKS = 5
GROUPS = 4
MESH = pl.DeviceIdType.MESH


def rms_norm(values, gain):
    wide = values.astype(F32)
    inv_rms = lax.rsqrt(jnp.mean(wide * wide, axis=-1, keepdims=True) + NORM_EPS)
    return (wide * inv_rms * gain.astype(F32)).astype(BF16)


def first_kernel(
    pos_hbm, x_hbm, gain_hbm, wq_hbm, wk_hbm, wv_hbm, ck_hbm, cv_hbm,
    part_ref, nk_hbm, nv_hbm, q_s, kx_s, vx_s, tiles,
    wbuf, kn_s, vn_s, kbuf, vbuf, ang_s, o_s, m_s, l_s,
    pos, x_ref, gain_ref, w_sem, k_sem, v_sem, out_sem, x_sem, old, t_sem,
):
    rows = x_ref.shape[0]
    head_dim = 2 * LANES
    heads = wq_hbm.shape[1] // head_dim
    kvs = wk_hbm.shape[1] // head_dim
    group = heads // kvs
    per_slot = 2 * kvs
    qrows = 2 * heads
    key_rows = ck_hbm.shape[1]
    local_slots = key_rows // per_slot
    slots = local_slots * lax.axis_size("sp")
    slices = key_rows // LANES
    half = rows // 2
    n_blocks = half // BLOCK
    start = (1 - lax.axis_index("sp") // 2) * half
    base = lax.axis_index("sp") * local_slots

    def w_copy(n):
        src, col = (
            (wk_hbm, n) if n < kvs else (wv_hbm, n - kvs) if n < 2 * kvs else (wq_hbm, n - 2 * kvs)
        )
        return pltpu.make_async_copy(src.at[:, pl.ds(col * head_dim, head_dim)], wbuf.at[n], w_sem.at[n])

    def in_copies(j):
        far, here = pl.ds(start + j * BLOCK, BLOCK), pl.ds(j * BLOCK, BLOCK)
        return (
            pltpu.make_async_copy(ck_hbm.at[far], kbuf.at[here], k_sem.at[j]),
            pltpu.make_async_copy(cv_hbm.at[far], vbuf.at[here], v_sem.at[j]),
        )

    def out_copies(j):
        far, here = pl.ds(start + j * BLOCK, BLOCK), pl.ds(j * BLOCK, BLOCK)
        return (
            pltpu.make_async_copy(kbuf.at[here], nk_hbm.at[far], out_sem.at[0]),
            pltpu.make_async_copy(vbuf.at[here], nv_hbm.at[far], out_sem.at[1]),
        )

    small = [
        pltpu.make_async_copy(src, dst, x_sem.at[i])
        for i, (src, dst) in enumerate(((pos_hbm, pos), (x_hbm, x_ref), (gain_hbm, gain_ref)))
    ]
    for copy in small:
        copy.start()
    n_w = heads + 2 * kvs
    for n in range(n_w // 2):
        w_copy(n).start()

    lane = lax.broadcasted_iota(jnp.int32, (1, LANES), 1).astype(F32)
    freq = jnp.exp2(lane * (-math.log2(ROPE_THETA) / LANES))

    for copy in small:
        copy.wait()
    for n in range(n_w // 2, n_w):
        w_copy(n).start()
    for j in range(FIRST):
        for copy in in_copies(j):
            copy.start()

    per_tile = 16 // per_slot
    near = lax.axis_index("sp") // 2 * half
    tile_row = lax.broadcasted_iota(jnp.int32, (16, LANES), 0) // per_slot

    def target(b):
        local = lax.rem(pos[b], slots) - base
        owned = (local >= 0) & (local < local_slots)
        safe = jnp.where(owned, local, 0)
        hit = jnp.where(owned, lax.rem(safe, per_tile), -1)
        return hit, pl.ds(pl.multiple_of((safe // per_tile) * 16, 16), 16)

    def tile_copies(n):
        at = target(near + n)[1]
        return (
            pltpu.make_async_copy(ck_hbm.at[near + n, at], old.at[0, n], t_sem.at[0]),
            pltpu.make_async_copy(cv_hbm.at[near + n, at], old.at[1, n], t_sem.at[1]),
        )

    def start_tile(n, carry):
        for copy in tile_copies(n):
            copy.start()
        return carry

    def wait_tile(n, carry):
        for copy in tile_copies(n):
            copy.wait()
        return carry

    def make_tile(n, carry):
        hit = target(near + n)[0]
        for i, new in enumerate((kn_s, vn_s)):
            fresh = new[pl.ds(pl.multiple_of((near + n) * 16, 16), 16), :]
            tiles[i, n] = jnp.where(tile_row == hit, fresh, old[i, n].astype(F32)).astype(BF16)
        return carry

    lax.fori_loop(0, half, start_tile, 0, unroll=4)

    def angle_row(b, carry):
        ang_s[pl.ds(b, 1), :] = freq * pos[b].astype(F32)
        return carry

    lax.fori_loop(0, rows, angle_row, 0, unroll=8)
    angles = ang_s[...]
    cos_t, sin_t = jnp.cos(angles), jnp.sin(angles)
    normed = rms_norm(x_ref[...], gain_ref[...])

    for n in range(n_w):
        w_copy(n).wait()
        if FIRST + n < n_blocks:
            for copy in in_copies(FIRST + n):
                copy.start()
        lin = jnp.dot(normed, wbuf[n], preferred_element_type=F32)
        first, second = lin[:, :LANES], lin[:, LANES:]
        if not kvs <= n < 2 * kvs:
            first, second = first * cos_t - second * sin_t, second * cos_t + first * sin_t
        first, second = first.astype(BF16).astype(F32), second.astype(BF16).astype(F32)
        if n >= 2 * kvs:
            h = n - 2 * kvs
            q_s[pl.ds(h, rows, stride=qrows), :] = first
            q_s[pl.ds(heads + h, rows, stride=qrows), :] = second
        else:
            dst, tile, kv = (kn_s, kx_s, n) if n < kvs else (vn_s, vx_s, n - kvs)
            for rep in range(16 // per_slot):
                dst[pl.ds(rep * per_slot + kv, rows, stride=16), :] = first
                dst[pl.ds(rep * per_slot + kvs + kv, rows, stride=16), :] = second
            for g in range(group):
                tile[pl.ds(kv * group + g, rows, stride=qrows), :] = first
                tile[pl.ds(heads + kv * group + g, rows, stride=qrows), :] = second

    row = lax.broadcasted_iota(jnp.int32, (qrows, LANES), 0)
    col = lax.broadcasted_iota(jnp.int32, (qrows, LANES), 1)
    half_of_col = (col // kvs) % 2
    fits = (half_of_col == row // heads) & (col % kvs == (row % heads) // group)
    slot_of_col = jnp.where(fits, col // per_slot, FAR)
    low_half = half_of_col == 0
    patch_row = lax.broadcasted_iota(jnp.int32, (16, LANES), 0) // per_slot
    scale = 1.0 / math.sqrt(head_dim)

    def block_step(j, carry):
        for copy in in_copies(j):
            copy.wait()
        for i in range(BLOCK):
            n = j * BLOCK + i
            b = start + n
            local = lax.rem(pos[b], slots) - base
            owned = (local >= 0) & (local < local_slots)
            safe = jnp.where(owned, local, 0)
            hit = jnp.where(owned, lax.rem(safe, 16 // per_slot), -1)
            span = pl.ds(pl.multiple_of((safe // (16 // per_slot)) * 16, 16), 16)
            for buf, new in ((kbuf, kn_s), (vbuf, vn_s)):
                old = buf[n, span, :].astype(F32)
                fresh = new[pl.ds(pl.multiple_of(b * 16, 16), 16), :]
                buf[n, span, :] = jnp.where(patch_row == hit, fresh, old).astype(BF16)
        scores = []
        for i in range(BLOCK):
            b = start + j * BLOCK + i
            q = q_s[pl.ds(pl.multiple_of(b * qrows, qrows), qrows), :].astype(BF16)
            scores.append(
                lax.dot_general(q, kbuf[j * BLOCK + i], (((1,), (1,)), ((), ())), preferred_element_type=F32)
            )
        probs = []
        for i in range(BLOCK):
            n = j * BLOCK + i
            p = pos[start + n]
            limit = jnp.where(p >= slots - 1, FAR // 2, p) - base
            parts = []
            for t in range(slices):
                own = scores[i][:, t * LANES : (t + 1) * LANES]
                other = pltpu.roll(own, heads, 0)
                other = jnp.where(
                    low_half, pltpu.roll(other, LANES - kvs, 1), pltpu.roll(other, kvs, 1)
                )
                ok = slot_of_col <= limit - t * (LANES // per_slot)
                parts.append(jnp.where(ok, (own + other) * scale, -jnp.inf))
            top = functools.reduce(jnp.maximum, parts)
            top = jnp.max(top, axis=1, keepdims=True)
            floor = jnp.where(top == -jnp.inf, 0.0, top)
            parts = [jnp.exp(part - floor) for part in parts]
            total = jnp.sum(functools.reduce(jnp.add, parts), axis=1, keepdims=True)
            span = pl.ds(pl.multiple_of(n * qrows, qrows), qrows)
            m_s[span, :] = jnp.broadcast_to(top, (qrows, LANES))
            l_s[span, :] = jnp.broadcast_to(total, (qrows, LANES))
            probs.append(jnp.concatenate([part.astype(BF16) for part in parts], axis=1))
        for i in range(BLOCK):
            n = j * BLOCK + i
            span = pl.ds(pl.multiple_of(n * qrows, qrows), qrows)
            o_s[span, :] = jnp.dot(probs[i], vbuf[n], preferred_element_type=F32)
        for copy in out_copies(j):
            copy.start()
        return carry

    lax.fori_loop(0, n_blocks, block_step, 0)

    lax.fori_loop(0, half, wait_tile, 0, unroll=8)
    lax.fori_loop(0, half, make_tile, 0, unroll=4)
    left = lax.broadcasted_iota(jnp.int32, (half, LANES), 1) < LANES // 2
    for h in range(heads):
        lo, hi = pl.ds(h, half, stride=qrows), pl.ds(heads + h, half, stride=qrows)
        part_ref[h, 0], part_ref[h, 1] = o_s[lo, :], o_s[hi, :]
        part_ref[h, 2] = jnp.where(left, m_s[lo, :], l_s[lo, :])
    for j in range(n_blocks):
        for copy in out_copies(j):
            copy.wait()


def first_half(positions, tokens, gain, w_q, w_k, w_v, rows_k, rows_v):
    rows, width = tokens.shape
    head_dim = 2 * LANES
    heads = w_q.shape[1] // head_dim
    kvs = w_k.shape[1] // head_dim
    qrows = 2 * heads
    vmem = pl.BlockSpec(memory_space=pltpu.VMEM)
    hbm = pl.BlockSpec(memory_space=pltpu.HBM)
    n_blocks = rows // 2 // BLOCK
    tile = lambda n: pltpu.VMEM((rows * n, LANES), F32)
    return pl.pallas_call(
        first_kernel,
        out_shape=(
            pltpu.VMEM((heads, 3, rows // 2, LANES), F32),
            jax.ShapeDtypeStruct(rows_k.shape, BF16),
            jax.ShapeDtypeStruct(rows_v.shape, BF16),
            tile(qrows), tile(qrows), tile(qrows),
            pltpu.VMEM((2, rows // 2, 16, LANES), BF16),
        ),
        in_specs=[hbm] * 8,
        out_specs=(vmem, hbm, hbm) + (vmem,) * 4,
        scratch_shapes=[
            pltpu.VMEM((heads + 2 * kvs, width, head_dim), BF16),
            tile(16), tile(16),
            pltpu.VMEM((rows // 2, *rows_k.shape[1:]), BF16),
            pltpu.VMEM((rows // 2, *rows_v.shape[1:]), BF16),
            tile(1),
            pltpu.VMEM((rows // 2 * qrows, LANES), F32),
            pltpu.VMEM((rows // 2 * qrows, LANES), F32),
            pltpu.VMEM((rows // 2 * qrows, LANES), F32),
            pltpu.SMEM((rows,), jnp.int32),
            pltpu.VMEM(tokens.shape, BF16),
            pltpu.VMEM(gain.shape, BF16),
            pltpu.SemaphoreType.DMA((heads + 2 * kvs,)),
            pltpu.SemaphoreType.DMA((n_blocks,)),
            pltpu.SemaphoreType.DMA((n_blocks,)),
            pltpu.SemaphoreType.DMA((2,)),
            pltpu.SemaphoreType.DMA((3,)),
            pltpu.VMEM((2, rows // 2, 16, LANES), BF16),
            pltpu.SemaphoreType.DMA((2,)),
        ],
        compiler_params=pltpu.CompilerParams(vmem_limit_bytes=36 << 20),
        name="first",
    )(*(pltpu.with_memory_space_constraint(v, pltpu.HBM) for v in (positions, tokens, gain, w_q, w_k, w_v, rows_k, rows_v)))


def combine(mine, theirs):
    left = lax.broadcasted_iota(jnp.int32, mine[2].shape, mine[2].ndim - 1) < LANES // 2
    axis = mine[2].ndim - 1

    def unpack(stats):
        turned = pltpu.roll(stats, LANES // 2, axis)
        return jnp.where(left, stats, turned), jnp.where(left, turned, stats)

    (m_a, l_a), (m_b, l_b) = unpack(mine[2]), unpack(theirs[2])
    top = jnp.maximum(m_a, m_b)
    f_a = jnp.where(m_a == -jnp.inf, 0.0, jnp.exp(m_a - top))
    f_b = jnp.where(m_b == -jnp.inf, 0.0, jnp.exp(m_b - top))
    return mine[0] * f_a + theirs[0] * f_b, mine[1] * f_a + theirs[1] * f_b, top, l_a * f_a + l_b * f_b


def layer_kernel(
    kv_heads, pos_hbm, x_hbm, gm_hbm, wo_hbm, wg_hbm, wu_hbm, wd_hbm, ck_hbm, cv_hbm,
    far_ref, q_s, kx_s, vx_s,
    out_ref, kbuf, vbuf,
    ring, o_s, m_s, l_s, part, rd, sx, rx,
    po, ro, so, yo, hb, act, pm, rm, sm, ym, ob,
    pos, x_ref, gm_ref,
    small_sem, k_sem, v_sem, o_sem, c_sem, send_sem, recv_sem,
):
    rows, width = x_ref.shape
    head_dim = ring.shape[2]
    heads = far_ref.shape[0]
    kvs = kv_heads
    group = heads // kvs
    per_slot, qrows = 2 * kvs, 2 * heads
    key_rows = ck_hbm.shape[1]
    local_slots = key_rows // per_slot
    slots = local_slots * lax.axis_size("sp")
    slices = key_rows // LANES
    n_blocks = rows // 2 // BLOCK
    mine_h = heads // 2
    half, quarter = rows // 2, rows // 4
    sp, tp = lax.axis_index("sp"), lax.axis_index("tp")
    x, k = sp // 2, lax.rem(sp, 2)
    d_dev, x_dev, y_dev = {"sp": x * 2 + 1 - k}, {"sp": (1 - x) * 2 + k}, {"tp": 1 - tp}
    base = sp * local_slots
    m_cols = act.shape[1]
    span = width // CHUNKS

    barrier = pltpu.get_barrier_semaphore()
    for dev in (d_dev, x_dev, y_dev):
        pl.semaphore_signal(barrier, inc=1, device_id=dev, device_id_type=MESH)

    counter = [0]

    def remote(src, dst, dev):
        n = counter[0]
        counter[0] += 1
        return pltpu.make_async_remote_copy(
            src_ref=src, dst_ref=dst, send_sem=send_sem.at[n], recv_sem=recv_sem.at[n],
            device_id=dev, device_id_type=MESH,
        )

    def in_copies(j):
        near, here = pl.ds(x * half + j * BLOCK, BLOCK), pl.ds(j * BLOCK, BLOCK)
        return (
            pltpu.make_async_copy(ck_hbm.at[near], kbuf.at[here], k_sem.at[j]),
            pltpu.make_async_copy(cv_hbm.at[near], vbuf.at[here], v_sem.at[j]),
        )

    small = [
        pltpu.make_async_copy(src, dst, small_sem.at[i])
        for i, (src, dst) in enumerate(
            ((pos_hbm, pos), (x_hbm, x_ref), (gm_hbm, gm_ref))
        )
    ]
    for copy in small:
        copy.start()
    for j in range(AHEAD):
        for copy in in_copies(j):
            copy.start()

    n_w = 0
    o_rows = mine_h * head_dim
    per_o = width // o_rows
    o_copies = [
        pltpu.make_async_copy(
            wo_hbm.at[pl.ds(k * o_rows, o_rows), pl.ds(c * head_dim, head_dim)],
            ring.at[n_w + c // per_o, pl.ds((c % per_o) * o_rows, o_rows)],
            o_sem.at[c],
        )
        for c in range(width // head_dim)
    ]
    n_gate = m_cols // head_dim
    ring_at = lambda i: (n_w + 2 + i) % SLOTS
    chunks = []
    for c in range(n_gate):
        at = pl.ds(pl.multiple_of(k * m_cols + c * head_dim, LANES), head_dim)
        chunks += [wg_hbm.at[:, at], wu_hbm.at[:, at]]
    for c in range(width // head_dim):
        chunks.append(wd_hbm.at[pl.ds(pl.multiple_of(k * m_cols, LANES), m_cols), pl.ds(c * head_dim, head_dim)])
    chunks = [
        pltpu.make_async_copy(src, ring.at[ring_at(i)], c_sem.at[i]) for i, src in enumerate(chunks)
    ]
    queue = iter(chunks)

    def fetch(n):
        for copy in itertools.islice(queue, n):
            copy.start()

    for copy in small:
        copy.wait()
    pl.semaphore_wait(barrier, 3)

    row = lax.broadcasted_iota(jnp.int32, (qrows, LANES), 0)
    col = lax.broadcasted_iota(jnp.int32, (qrows, LANES), 1)
    half_of_col = (col // kvs) % 2
    fits = (half_of_col == row // heads) & (col % kvs == (row % heads) // group)
    slot_of_col = jnp.where(fits, col // per_slot, FAR)
    low_half = half_of_col == 0
    scale = 1.0 / math.sqrt(head_dim)

    def block_step(j, carry):
        @pl.when(j + AHEAD < n_blocks)
        def _():
            for copy in in_copies(j + AHEAD):
                copy.start()

        for copy in in_copies(j):
            copy.wait()
        first = x * half + j * BLOCK
        at_rows = [pl.ds(pl.multiple_of((first + i) * qrows, qrows), qrows) for i in range(BLOCK)]
        scores = []
        for i in range(BLOCK):
            scores.append(
                lax.dot_general(
                    q_s[at_rows[i], :].astype(BF16), kbuf[j * BLOCK + i], (((1,), (1,)), ((), ())),
                    preferred_element_type=F32,
                )
            )
        probs, news = [], []
        for i in range(BLOCK):
            p = pos[first + i]
            local = lax.rem(p, slots) - base
            owned = (local >= 0) & (local < local_slots)
            hidden = jnp.where(owned, local, -FAR)
            limit = jnp.where(p >= slots - 1, FAR // 2, p) - base
            fresh = q_s[at_rows[i], :] * kx_s[at_rows[i], :]
            fresh = jnp.sum(fresh + pltpu.roll(fresh, heads, 0), axis=1, keepdims=True) * scale
            fresh = jnp.where(jnp.broadcast_to(owned, fresh.shape), fresh, -jnp.inf)
            parts = []
            for t in range(slices):
                own = scores[i][:, t * LANES : (t + 1) * LANES]
                other = pltpu.roll(own, heads, 0)
                other = jnp.where(
                    low_half, pltpu.roll(other, LANES - kvs, 1), pltpu.roll(other, kvs, 1)
                )
                shift = t * (LANES // per_slot)
                ok = (slot_of_col <= limit - shift) & (slot_of_col != hidden - shift)
                parts.append(jnp.where(ok, (own + other) * scale, -jnp.inf))
            top = functools.reduce(jnp.maximum, parts)
            top = jnp.maximum(jnp.max(top, axis=1, keepdims=True), fresh)
            floor = jnp.where(top == -jnp.inf, 0.0, top)
            parts = [jnp.exp(part_t - floor) for part_t in parts]
            new = jnp.exp(fresh - floor)
            total = jnp.sum(functools.reduce(jnp.add, parts), axis=1, keepdims=True) + new
            at = pl.ds(pl.multiple_of((j * BLOCK + i) * qrows, qrows), qrows)
            m_s[at, :] = jnp.broadcast_to(top, (qrows, LANES))
            l_s[at, :] = jnp.broadcast_to(total, (qrows, LANES))
            news.append(new)
            probs.append(jnp.concatenate([part_t.astype(BF16) for part_t in parts], axis=1))
        for i in range(BLOCK):
            at = pl.ds(pl.multiple_of((j * BLOCK + i) * qrows, qrows), qrows)
            o_s[at, :] = (
                jnp.dot(probs[i], vbuf[j * BLOCK + i], preferred_element_type=F32) + news[i] * vx_s[at_rows[i], :]
            )
        return carry

    size = rows // GROUPS
    my_heads, their_heads = pl.ds(k * mine_h, mine_h), pl.ds((1 - k) * mine_h, mine_h)
    spans = [pl.ds(g * size, size) for g in range(GROUPS)]
    near = GROUPS // 2
    sources = [far_ref.at[their_heads, :, spans[g]] for g in range(near)]
    sources += [part.at[their_heads, :, spans[g]] for g in range(near)]
    swaps_a = [remote(src, rd.at[:, :, at], d_dev) for src, at in zip(sources, spans)]
    cross_a = [remote(sx.at[:, :, at], rx.at[:, :, at], x_dev) for at in spans[: GROUPS // 2]]
    left = lax.broadcasted_iota(jnp.int32, (mine_h, size, LANES), 2) < LANES // 2
    joined = [None] * GROUPS

    def publish(g):
        at = spans[g - near]
        for h in range(heads):
            lo = pl.ds((g - near) * size * qrows + h, size, stride=qrows)
            hi = pl.ds((g - near) * size * qrows + heads + h, size, stride=qrows)
            part[h, 0, at], part[h, 1, at] = o_s[lo, :], o_s[hi, :]
            part[h, 2, at] = jnp.where(left[0], m_s[lo, :], l_s[lo, :])
        swaps_a[g].start()

    def chip(g):
        swaps_a[g].wait_recv()
        at = spans[g]
        here, local = (far_ref, at) if g < near else (part, spans[g - near])
        o_a, o_b, m, l = combine(
            [here[my_heads, i, local] for i in range(3)], [rd[:, i, at] for i in range(3)]
        )
        value = [o_a, o_b, jnp.where(left, m, l)]
        if g < GROUPS // 2:
            for i in range(3):
                sx[:, i, at] = value[i]
            cross_a[g].start()
        joined[g] = value

    for g in range(near):
        swaps_a[g].start()
    step = n_blocks // GROUPS
    for g in range(GROUPS):
        lax.fori_loop(g * step, (g + 1) * step, block_step, 0)
        if g == 0:
            for n in range(near):
                chip(n)
        elif g == 1:
            publish(near)
        elif g == 2:
            chip(near)
            for copy in o_copies:
                copy.start()
    publish(GROUPS - 1)
    fetch(3)
    chip(GROUPS - 1)
    pieces = []
    for g in range(GROUPS // 2):
        cross_a[g].wait_recv()
        o_a, o_b, _, l = combine(joined[GROUPS // 2 + g], [rx[:, i, spans[g]] for i in range(3)])
        o_a, o_b = (o_a / l).astype(BF16), (o_b / l).astype(BF16)
        pieces.append(jnp.concatenate([v[h] for h in range(mine_h) for v in (o_a, o_b)], axis=-1))
    attended = jnp.concatenate(pieces, axis=0)

    own, other = pl.ds(k * quarter, quarter), pl.ds((1 - k) * quarter, quarter)
    my_rows = pl.ds(pl.multiple_of(x * half + k * quarter, quarter), quarter)
    x_peer_rows = pl.ds(pl.multiple_of((1 - x) * half + k * quarter, quarter), quarter)
    cols = [pl.ds(c * span, span) for c in range(CHUNKS)]
    per_span = span // head_dim

    def staged(dot, swap, cross, *rest):
        for c in range(CHUNKS + 2):
            if c < CHUNKS:
                dot(c)
            if c >= 2:
                swap(c - 2)
        for c in range(CHUNKS):
            cross(c)
        for c in range(CHUNKS + len(rest) - 1):
            for s, stage in enumerate(rest):
                if 0 <= c - s < CHUNKS:
                    stage(c - s)

    swaps = [remote(po.at[other, c], ro.at[:, c], d_dev) for c in cols]
    crosses = [remote(so.at[:, c], yo.at[:, c], y_dev) for c in cols]
    gathers = [remote(hb.at[own, c], hb.at[own, c], d_dev) for c in cols]

    def o_dot(c):
        for i in range(c * per_span, (c + 1) * per_span):
            o_copies[i].wait()
            w = ring[n_w + i // per_o, (i % per_o) * o_rows : (i % per_o + 1) * o_rows, :]
            po[:, i * head_dim : (i + 1) * head_dim] = jnp.dot(attended, w, preferred_element_type=F32)
        swaps[c].start()

    def o_swap(c):
        swaps[c].wait_recv()
        so[:, cols[c]] = po[own, cols[c]] + ro[:, cols[c]]
        crosses[c].start()
        fetch(3)

    def o_cross(c):
        crosses[c].wait_recv()
        total = so[:, cols[c]] + yo[:, cols[c]]
        hb[own, cols[c]] = (x_ref[my_rows, cols[c]].astype(F32) + total).astype(BF16).astype(F32)
        gathers[c].start()

    def o_gather(c):
        gathers[c].wait_recv()

    staged(o_dot, o_swap, o_cross, o_gather)

    normed_m = rms_norm(hb[...], gm_ref[...])
    for c in range(n_gate):
        chunks[2 * c].wait()
        chunks[2 * c + 1].wait()
        gate = jnp.dot(normed_m, ring[ring_at(2 * c)], preferred_element_type=F32)
        up = jnp.dot(normed_m, ring[ring_at(2 * c + 1)], preferred_element_type=F32)
        act[:, c * head_dim : (c + 1) * head_dim] = (jax.nn.silu(gate) * up).astype(BF16)
        fetch(2)

    swaps_m = [remote(pm.at[other, c], rm.at[:, c], d_dev) for c in cols]
    crosses_m = [remote(sm.at[:, c], ym.at[:, c], y_dev) for c in cols]
    to_core = [remote(ob.at[my_rows, c], ob.at[my_rows, c], d_dev) for c in cols]
    to_x = [remote(ob.at[my_rows, c], ob.at[my_rows, c], x_dev) for c in cols]
    onward = [remote(ob.at[x_peer_rows, c], ob.at[x_peer_rows, c], d_dev) for c in cols]

    def m_dot(c):
        for i in range(c * per_span, (c + 1) * per_span):
            chunks[2 * n_gate + i].wait()
            pm[:, i * head_dim : (i + 1) * head_dim] = jnp.dot(
                act[...], ring[ring_at(2 * n_gate + i)], preferred_element_type=F32
            )
        swaps_m[c].start()

    def m_swap(c):
        swaps_m[c].wait_recv()
        sm[:, cols[c]] = pm[own, cols[c]] + rm[:, cols[c]]
        crosses_m[c].start()

    def m_cross(c):
        crosses_m[c].wait_recv()
        total = sm[:, cols[c]] + ym[:, cols[c]]
        ob[my_rows, cols[c]] = (hb[own, cols[c]] + total).astype(BF16).astype(F32)
        to_x[c].start()
        to_core[c].start()

    def m_gather(c):
        to_x[c].wait_recv()
        onward[c].start()

    def m_last(c):
        to_core[c].wait_recv()
        onward[c].wait_recv()
        out_ref[:, cols[c]] = ob[:, cols[c]].astype(BF16)

    staged(m_dot, m_swap, m_cross, m_gather, m_last)
    for copy in [*swaps_a, *cross_a, *swaps, *crosses, *gathers, *swaps_m, *crosses_m, *to_core, *to_x, *onward]:
        copy.wait_send()


def layer(positions, tokens, gain, w_o, w_gate, w_up, w_down, rows_k, rows_v, kvs, carried):
    rows, width = tokens.shape
    head_dim = 2 * LANES
    heads = carried[0].shape[0]
    qrows = 2 * heads
    half, quarter = rows // 2, rows // 4
    cut = w_gate.shape[1] // 2
    n_blocks = half // BLOCK
    vmem = pl.BlockSpec(memory_space=pltpu.VMEM)
    hbm = pl.BlockSpec(memory_space=pltpu.HBM)
    flat = lambda n: pltpu.VMEM((n, width), F32)
    stats = lambda h, n: pltpu.VMEM((h, 3, n, LANES), F32)
    dma = lambda n: pltpu.SemaphoreType.DMA((n,))
    n_remote = GROUPS + GROUPS // 2 + 8 * CHUNKS
    args = (positions, tokens, gain, w_o, w_gate, w_up, w_down, rows_k, rows_v)
    shape = (half, *rows_k.shape[1:])
    return pl.pallas_call(
        functools.partial(layer_kernel, kvs),
        out_shape=(
            pltpu.VMEM(tokens.shape, BF16),
            pltpu.VMEM(shape, BF16),
            pltpu.VMEM(shape, BF16),
        ),
        in_specs=[hbm] * len(args) + [vmem] * len(carried),
        out_specs=(vmem,) * 3,
        scratch_shapes=[
            pltpu.VMEM((SLOTS, width, head_dim), BF16),
            *(pltpu.VMEM((half * qrows, LANES), F32) for _ in range(3)),
            stats(heads, half), stats(heads // 2, rows), stats(heads // 2, half), stats(heads // 2, half),
            flat(half), flat(quarter), flat(quarter), flat(quarter), flat(half),
            pltpu.VMEM((half, cut), BF16),
            flat(half), flat(quarter), flat(quarter), flat(quarter), flat(rows),
            pltpu.SMEM((rows,), jnp.int32),
            pltpu.VMEM(tokens.shape, BF16),
            pltpu.VMEM(gain.shape, BF16),
            dma(3), dma(n_blocks), dma(n_blocks), dma(width // head_dim),
            dma(2 * (cut // head_dim) + width // head_dim), dma(n_remote), dma(n_remote),
        ],
        compiler_params=pltpu.CompilerParams(
            vmem_limit_bytes=LAYER_VMEM << 20, collective_id=0, has_side_effects=True
        ),
        name="layer",
    )(*(pltpu.with_memory_space_constraint(v, pltpu.HBM) for v in args), *carried)


def write_kernel(pos_hbm, t_ref, tiles, kbuf, vbuf, _k, _v, out_ref, nk_hbm, nv_hbm, pos, sem, tile_sem, pos_sem):
    rows, key_rows, _ = kbuf.shape
    per_slot = 4
    local_slots = key_rows // per_slot
    slots = local_slots * lax.axis_size("sp")
    base = lax.axis_index("sp") * local_slots
    start = lax.axis_index("sp") // 2 * rows
    per_tile = 16 // per_slot
    n_blocks = rows // BLOCK

    def copies(j):
        here, near = pl.ds(j * BLOCK, BLOCK), pl.ds(start + j * BLOCK, BLOCK)
        return (
            pltpu.make_async_copy(kbuf.at[here], nk_hbm.at[near], sem.at[0, j]),
            pltpu.make_async_copy(vbuf.at[here], nv_hbm.at[near], sem.at[1, j]),
        )

    def where(b):
        local = lax.rem(pos[b], slots) - base
        owned = (local >= 0) & (local < local_slots)
        safe = jnp.where(owned, local, 0)
        return pl.ds(pl.multiple_of((safe // per_tile) * 16, 16), 16)

    def tile_copies(b):
        at = where(start + b)
        return (
            pltpu.make_async_copy(tiles.at[0, b], nk_hbm.at[start + b, at], tile_sem.at[0]),
            pltpu.make_async_copy(tiles.at[1, b], nv_hbm.at[start + b, at], tile_sem.at[1]),
        )

    pos_copy = pltpu.make_async_copy(pos_hbm, pos, pos_sem)
    pos_copy.start()
    for j in range(n_blocks):
        for copy in copies(j):
            copy.start()
    pos_copy.wait()

    out_ref[...] = t_ref[...]

    def place_tiles(j, carry):
        for copy in copies(j):
            copy.wait()
        for i in range(BLOCK):
            for copy in tile_copies(j * BLOCK + i):
                copy.start()
        return carry

    lax.fori_loop(0, n_blocks, place_tiles, 0)

    def finish(b, carry):
        for copy in tile_copies(b):
            copy.wait()
        return carry

    lax.fori_loop(0, rows, finish, 0, unroll=8)


def write(positions, layer_out, tiles, buf_k, buf_v, new_k, new_v):
    vmem = pl.BlockSpec(memory_space=pltpu.VMEM)
    hbm = pl.BlockSpec(memory_space=pltpu.HBM)
    rows = buf_k.shape[0]
    any_space = pl.BlockSpec(memory_space=pl.ANY)
    return pl.pallas_call(
        write_kernel,
        out_shape=tuple(jax.ShapeDtypeStruct(v.shape, BF16) for v in (layer_out, new_k, new_v)),
        in_specs=[hbm, vmem, vmem] + [any_space] * 2 + [hbm] * 2,
        out_specs=(vmem, hbm, hbm),
        input_output_aliases={5: 1, 6: 2},
        scratch_shapes=[
            pltpu.SMEM(positions.shape, jnp.int32),
            pltpu.SemaphoreType.DMA((2, rows // BLOCK)),
            pltpu.SemaphoreType.DMA((2,)),
            pltpu.SemaphoreType.DMA,
        ],
        compiler_params=pltpu.CompilerParams(vmem_limit_bytes=LAYER_VMEM << 20),
        name="write",
    )(pltpu.with_memory_space_constraint(positions, pltpu.HBM), layer_out, tiles, buf_k, buf_v, new_k, new_v)


def to_rows(cache):
    b, s, kv, d = cache.shape
    return cache.reshape(b, s, kv, d // LANES, LANES).transpose(0, 1, 3, 2, 4).reshape(b, -1, LANES)


def from_rows(rows, shape):
    b, s, kv, d = shape
    return rows.reshape(b, s, d // LANES, kv, LANES).transpose(0, 1, 3, 2, 4).reshape(shape)


def solution(mesh):
    cache_spec = P("dp", "sp", "tp", None)
    row_spec = P("dp", None)
    col_spec = P(None, "tp")
    in_specs = (row_spec, P("dp"), cache_spec, cache_spec, P(None), col_spec, col_spec, col_spec, P("tp", None), P(None), col_spec, col_spec, P("tp", None))
    out_specs = (row_spec, cache_spec, cache_spec)

    def local_step(tokens, positions, cache_k, cache_v, attn_gain, w_q, w_k, w_v, w_o, mlp_gain, w_gate, w_up, w_down):
        old_k, old_v = to_rows(cache_k), to_rows(cache_v)
        far, rows_k, rows_v, *carried, tiles = first_half(
            positions, tokens, attn_gain, w_q, w_k, w_v, old_k, old_v
        )
        out, buf_k, buf_v = layer(
            positions, tokens, mlp_gain, w_o, w_gate, w_up, w_down, old_k, old_v, cache_k.shape[2], (far, *carried)
        )
        layer_out, rows_k, rows_v = write(positions, out, tiles, buf_k, buf_v, rows_k, rows_v)
        new_k = from_rows(rows_k, cache_k.shape)
        new_v = from_rows(rows_v, cache_v.shape)
        return layer_out, new_k, new_v

    return jax.shard_map(local_step, mesh=mesh, in_specs=in_specs, out_specs=out_specs, check_vma=False)
```

time: 62.4 us -> 61.3 us (0.982)
  local copies, waits for them, and re-layouts: 0.74 us -> 0 us
    unnamed x5 -> x0, local copies, waits for them, and re-layouts: 0.74 us -> none
    pallas_call x2 -> x3, Pallas kernels: 60.8 us -> 60.6 us  [the longest x1 38.7 us: layer(): pl.pallas_call(functools.partial(layer_kernel, kvs), out_shape=(pltpu.VME...]
where the time goes in v5:
time: 61.3 us; the launch traced here: 61.2 us
  Pallas kernels  60.6 us (99%)
  between operations  0.65 us (1%)
    pallas_call x1, Pallas kernels, layer(): pl.pallas_call(functools.partial(layer_kernel, kvs), out_shape=(pltpu.VME...  38.7 us
    pallas_call x1, Pallas kernels, first_half(): pl.pallas_call(first_kernel, out_shape=(pltpu.VMEM((heads, 3, rows // 2,...  14.5 us
    pallas_call x1, Pallas kernels, write(): pl.pallas_call(write_kernel, out_shape=tuple((jax.ShapeDtypeStruct(v.shap...  7.34 us

profile of v5, /device:TPU:0, one launch (start us, length us, event | category | flops | bytes accessed | tf_op | source)
XLA Modules:
  0.0 61.2 jit_solution(1839183579347201710)
XLA Ops:
  0.6 14.5 %first.1 = (f32[4,3,32,128]{3,2,1,0:T(8,128)S(1)}, bf16[64,1024,128]{2,1,0:T(8,128)(2,1)}, bf16[64,1024,128]{2,1,0:T(8,128)(2,1)}, f32[512,128]{1,0:T(8,128)S(1)...) custom-call(s32[64]{0:T(128)} %pos_hbm.5, bf16[64,2560]{1,0:T(8,128)(2,1)} %x_hbm.3, ...), custom_call_target="tpu_custom_call" | custom-call | tf_op jit(solution)/shard_map/first/pallas_call | solution.py:252
  15.1 38.7 %layer.1 = (bf16[64,2560]{1,0:T(8,128)(2,1)S(1)}, bf16[32,1024,128]{2,1,0:T(8,128)(2,1)S(1)}, bf16[32,1024,128]{2,1,0:T(8,128)(2,1)S(1)}) custom-call(s32[64]{0:T(128)} %pos_hbm.5, bf16[64,2560]{1,0:T(8,128)(2,1)} %x_hbm.3, bf16[2560]{0:T(1024)(128)(2,1)} %gm_hbm.1, bf16[1024,2560]{1,0:T(8,128)(2,1)} %wo_hbm.1, bf16[2560,5120]{1,0:T(8,128)(2,1)} %wg_hbm.1, ...), custom_call_target="tpu_custom_call" | custom-call | tf_op jit(solution)/shard_map/layer/pallas_call | solution.py:632
  53.9 7.3 %write.1 = (bf16[64,2560]{1,0:T(8,128)(2,1)}, bf16[64,1024,128]{2,1,0:T(8,128)(2,1)}, bf16[64,1024,128]{2,1,0:T(8,128)(2,1)}) custom-call(s32[64]{0:T(128)} %pos_hbm.5, bf16[64,2560]{1,0:T(8,128)(2,1)S(1)} %get-tuple-element.20.t_ref, bf16[2,32,16,128]{3,2,1,0:T(8,128)(2,1)S(1)} %get-tuple-element.21.tiles, ...), custom_call_target="tpu_custom_call", output_to_operand_aliasing={{1}: (5, {}), {2}: (6, {})} | custom-call | tf_op jit(solution)/shard_map/write/pallas_call | solution.py:723

commit v6 on v5

--- a/solution.py
+++ b/solution.py
@@ -16,7 +16,7 @@
 BF16 = jnp.bfloat16
 FAR = 1 << 28
 BLOCK = 4
-AHEAD = 3
+AHEAD = 2
 FIRST = 4
 SLOTS = 22
 LAYER_VMEM = 35
@@ -33,9 +33,9 @@
 
 def first_kernel(
     pos_hbm, x_hbm, gain_hbm, wq_hbm, wk_hbm, wv_hbm, ck_hbm, cv_hbm,
-    part_ref, nk_hbm, nv_hbm, q_s, kx_s, vx_s, tiles,
-    wbuf, kn_s, vn_s, kbuf, vbuf, ang_s, o_s, m_s, l_s,
-    pos, x_ref, gain_ref, w_sem, k_sem, v_sem, out_sem, x_sem, old, t_sem,
+    part_ref, nk_hbm, nv_hbm, q_s, kx_s, vx_s, kn_s, vn_s,
+    wbuf, kbuf, vbuf, ang_s, o_s, m_s, l_s,
+    pos, x_ref, gain_ref, w_sem, k_sem, v_sem, out_sem, x_sem,
 ):
     rows = x_ref.shape[0]
     head_dim = 2 * LANES
@@ -93,43 +93,6 @@
     for j in range(FIRST):
         for copy in in_copies(j):
             copy.start()
-
-    per_tile = 16 // per_slot
-    near = lax.axis_index("sp") // 2 * half
-    tile_row = lax.broadcasted_iota(jnp.int32, (16, LANES), 0) // per_slot
-
-    def target(b):
-        local = lax.rem(pos[b], slots) - base
-        owned = (local >= 0) & (local < local_slots)
-        safe = jnp.where(owned, local, 0)
-        hit = jnp.where(owned, lax.rem(safe, per_tile), -1)
-        return hit, pl.ds(pl.multiple_of((safe // per_tile) * 16, 16), 16)
-
-    def tile_copies(n):
-        at = target(near + n)[1]
-        return (
-            pltpu.make_async_copy(ck_hbm.at[near + n, at], old.at[0, n], t_sem.at[0]),
-            pltpu.make_async_copy(cv_hbm.at[near + n, at], old.at[1, n], t_sem.at[1]),
-        )
-
-    def start_tile(n, carry):
-        for copy in tile_copies(n):
-            copy.start()
-        return carry
-
-    def wait_tile(n, carry):
-        for copy in tile_copies(n):
-            copy.wait()
-        return carry
-
-    def make_tile(n, carry):
-        hit = target(near + n)[0]
-        for i, new in enumerate((kn_s, vn_s)):
-            fresh = new[pl.ds(pl.multiple_of((near + n) * 16, 16), 16), :]
-            tiles[i, n] = jnp.where(tile_row == hit, fresh, old[i, n].astype(F32)).astype(BF16)
-        return carry
-
-    lax.fori_loop(0, half, start_tile, 0, unroll=4)
 
     def angle_row(b, carry):
         ang_s[pl.ds(b, 1), :] = freq * pos[b].astype(F32)
@@ -227,8 +190,6 @@
 
     lax.fori_loop(0, n_blocks, block_step, 0)
 
-    lax.fori_loop(0, half, wait_tile, 0, unroll=8)
-    lax.fori_loop(0, half, make_tile, 0, unroll=4)
     left = lax.broadcasted_iota(jnp.int32, (half, LANES), 1) < LANES // 2
     for h in range(heads):
         lo, hi = pl.ds(h, half, stride=qrows), pl.ds(heads + h, half, stride=qrows)
@@ -255,14 +216,12 @@
             pltpu.VMEM((heads, 3, rows // 2, LANES), F32),
             jax.ShapeDtypeStruct(rows_k.shape, BF16),
             jax.ShapeDtypeStruct(rows_v.shape, BF16),
-            tile(qrows), tile(qrows), tile(qrows),
-            pltpu.VMEM((2, rows // 2, 16, LANES), BF16),
+            tile(qrows), tile(qrows), tile(qrows), tile(16), tile(16),
         ),
         in_specs=[hbm] * 8,
-        out_specs=(vmem, hbm, hbm) + (vmem,) * 4,
+        out_specs=(vmem, hbm, hbm) + (vmem,) * 5,
         scratch_shapes=[
             pltpu.VMEM((heads + 2 * kvs, width, head_dim), BF16),
-            tile(16), tile(16),
             pltpu.VMEM((rows // 2, *rows_k.shape[1:]), BF16),
             pltpu.VMEM((rows // 2, *rows_v.shape[1:]), BF16),
             tile(1),
@@ -277,8 +236,6 @@
             pltpu.SemaphoreType.DMA((n_blocks,)),
             pltpu.SemaphoreType.DMA((2,)),
             pltpu.SemaphoreType.DMA((3,)),
-            pltpu.VMEM((2, rows // 2, 16, LANES), BF16),
-            pltpu.SemaphoreType.DMA((2,)),
         ],
         compiler_params=pltpu.CompilerParams(vmem_limit_bytes=36 << 20),
         name="first",
@@ -658,7 +615,7 @@
     )(*(pltpu.with_memory_space_constraint(v, pltpu.HBM) for v in args), *carried)
 
 
-def write_kernel(pos_hbm, t_ref, tiles, kbuf, vbuf, _k, _v, out_ref, nk_hbm, nv_hbm, pos, sem, tile_sem, pos_sem):
+def write_kernel(pos_hbm, t_ref, kn_s, vn_s, _bk, _bv, _k, _v, out_ref, nk_hbm, nv_hbm, kbuf, vbuf, pos, sem, pos_sem):
     rows, key_rows, _ = kbuf.shape
     per_slot = 4
     local_slots = key_rows // per_slot
@@ -667,74 +624,63 @@
     start = lax.axis_index("sp") // 2 * rows
     per_tile = 16 // per_slot
     n_blocks = rows // BLOCK
+    tile_row = lax.broadcasted_iota(jnp.int32, (16, LANES), 0) // per_slot
 
     def copies(j):
         here, near = pl.ds(j * BLOCK, BLOCK), pl.ds(start + j * BLOCK, BLOCK)
         return (
-            pltpu.make_async_copy(kbuf.at[here], nk_hbm.at[near], sem.at[0, j]),
-            pltpu.make_async_copy(vbuf.at[here], nv_hbm.at[near], sem.at[1, j]),
-        )
-
-    def where(b):
+            pltpu.make_async_copy(kbuf.at[here], nk_hbm.at[near], sem.at[0]),
+            pltpu.make_async_copy(vbuf.at[here], nv_hbm.at[near], sem.at[1]),
+        )
+
+    def patch(n):
+        b = start + n
         local = lax.rem(pos[b], slots) - base
         owned = (local >= 0) & (local < local_slots)
         safe = jnp.where(owned, local, 0)
-        return pl.ds(pl.multiple_of((safe // per_tile) * 16, 16), 16)
-
-    def tile_copies(b):
-        at = where(start + b)
-        return (
-            pltpu.make_async_copy(tiles.at[0, b], nk_hbm.at[start + b, at], tile_sem.at[0]),
-            pltpu.make_async_copy(tiles.at[1, b], nv_hbm.at[start + b, at], tile_sem.at[1]),
-        )
+        hit = jnp.where(owned, lax.rem(safe, per_tile), -1)
+        at = pl.ds(pl.multiple_of((safe // per_tile) * 16, 16), 16)
+        for buf, new in ((kbuf, kn_s), (vbuf, vn_s)):
+            fresh = new[pl.ds(pl.multiple_of(b * 16, 16), 16), :]
+            buf[n, at, :] = jnp.where(tile_row == hit, fresh, buf[n, at, :].astype(F32)).astype(BF16)
 
     pos_copy = pltpu.make_async_copy(pos_hbm, pos, pos_sem)
     pos_copy.start()
+    out_ref[...] = t_ref[...]
+    pos_copy.wait()
+    for j in range(n_blocks + 1):
+        if j < n_blocks:
+            for i in range(BLOCK):
+                patch(j * BLOCK + i)
+        if j:
+            for copy in copies(j - 1):
+                copy.start()
     for j in range(n_blocks):
         for copy in copies(j):
-            copy.start()
-    pos_copy.wait()
-
-    out_ref[...] = t_ref[...]
-
-    def place_tiles(j, carry):
-        for copy in copies(j):
             copy.wait()
-        for i in range(BLOCK):
-            for copy in tile_copies(j * BLOCK + i):
-                copy.start()
-        return carry
-
-    lax.fori_loop(0, n_blocks, place_tiles, 0)
-
-    def finish(b, carry):
-        for copy in tile_copies(b):
-            copy.wait()
-        return carry
-
-    lax.fori_loop(0, rows, finish, 0, unroll=8)
-
-
-def write(positions, layer_out, tiles, buf_k, buf_v, new_k, new_v):
+
+
+def write(positions, layer_out, fresh_k, fresh_v, buf_k, buf_v, new_k, new_v):
     vmem = pl.BlockSpec(memory_space=pltpu.VMEM)
     hbm = pl.BlockSpec(memory_space=pltpu.HBM)
-    rows = buf_k.shape[0]
-    any_space = pl.BlockSpec(memory_space=pl.ANY)
     return pl.pallas_call(
         write_kernel,
-        out_shape=tuple(jax.ShapeDtypeStruct(v.shape, BF16) for v in (layer_out, new_k, new_v)),
-        in_specs=[hbm, vmem, vmem] + [any_space] * 2 + [hbm] * 2,
-        out_specs=(vmem, hbm, hbm),
-        input_output_aliases={5: 1, 6: 2},
+        out_shape=(
+            *(jax.ShapeDtypeStruct(v.shape, BF16) for v in (layer_out, new_k, new_v)),
+            pltpu.VMEM(buf_k.shape, BF16),
+            pltpu.VMEM(buf_v.shape, BF16),
+        ),
+        in_specs=[hbm] + [vmem] * 5 + [hbm] * 2,
+        out_specs=(vmem, hbm, hbm, vmem, vmem),
+        input_output_aliases={4: 3, 5: 4, 6: 1, 7: 2},
         scratch_shapes=[
             pltpu.SMEM(positions.shape, jnp.int32),
-            pltpu.SemaphoreType.DMA((2, rows // BLOCK)),
             pltpu.SemaphoreType.DMA((2,)),
             pltpu.SemaphoreType.DMA,
         ],
         compiler_params=pltpu.CompilerParams(vmem_limit_bytes=LAYER_VMEM << 20),
         name="write",
-    )(pltpu.with_memory_space_constraint(positions, pltpu.HBM), layer_out, tiles, buf_k, buf_v, new_k, new_v)
+    )(pltpu.with_memory_space_constraint(positions, pltpu.HBM), layer_out, fresh_k, fresh_v, buf_k, buf_v, new_k, new_v)[:3]
 
 
 def to_rows(cache):
@@ -756,13 +702,13 @@
 
     def local_step(tokens, positions, cache_k, cache_v, attn_gain, w_q, w_k, w_v, w_o, mlp_gain, w_gate, w_up, w_down):
         old_k, old_v = to_rows(cache_k), to_rows(cache_v)
-        far, rows_k, rows_v, *carried, tiles = first_half(
+        far, rows_k, rows_v, *carried, fresh_k, fresh_v = first_half(
             positions, tokens, attn_gain, w_q, w_k, w_v, old_k, old_v
         )
         out, buf_k, buf_v = layer(
             positions, tokens, mlp_gain, w_o, w_gate, w_up, w_down, old_k, old_v, cache_k.shape[2], (far, *carried)
         )
-        layer_out, rows_k, rows_v = write(positions, out, tiles, buf_k, buf_v, rows_k, rows_v)
+        layer_out, rows_k, rows_v = write(positions, out, fresh_k, fresh_v, buf_k, buf_v, rows_k, rows_v)
         new_k = from_rows(rows_k, cache_k.shape)
         new_v = from_rows(rows_v, cache_v.shape)
         return layer_out, new_k, new_v

time: 61.3 us -> 61.1 us (level)
  no operation moved by 1% of the time
where the time goes in v6:
time: 61.1 us; the launch traced here: 61 us
  Pallas kernels  60.3 us (99%)
  between operations  0.65 us (1%)
    pallas_call x1, Pallas kernels, layer(): pl.pallas_call(functools.partial(layer_kernel, kvs), out_shape=(pltpu.VME...  38.8 us
    pallas_call x1, Pallas kernels, first_half(): pl.pallas_call(first_kernel, out_shape=(pltpu.VMEM((heads, 3, rows // 2,...  14.2 us
    pallas_call x1, Pallas kernels, write(): pl.pallas_call(write_kernel, out_shape=(*(jax.ShapeDtypeStruct(v.shape, B...  7.32 us

profile of v6, /device:TPU:0, one launch (start us, length us, event | category | flops | bytes accessed | tf_op | source)
XLA Modules:
  0.0 61.0 jit_solution(10719516675365329956)
XLA Ops:
  0.6 14.2 %first.1 = (f32[4,3,32,128]{3,2,1,0:T(8,128)S(1)}, bf16[64,1024,128]{2,1,0:T(8,128)(2,1)}, bf16[64,1024,128]{2,1,0:T(8,128)(2,1)}, f32[512,128]{1,0:T(8,128)S(1)...) custom-call(s32[64]{0:T(128)} %pos_hbm.5, ...), custom_call_target="tpu_custom_call" | custom-call | tf_op jit(solution)/shard_map/first/pallas_call | solution.py:213
  14.8 38.8 %layer.1 = (bf16[64,2560]{1,0:T(8,128)(2,1)S(1)}, bf16[32,1024,128]{2,1,0:T(8,128)(2,1)S(1)}, bf16[32,1024,128]{2,1,0:T(8,128)(2,1)S(1)}) custom-call(s32[64]{0:T(128)} %pos_hbm.5, bf16[64,2560]{1,0:T(8,128)(2,1)} %x_hbm.3, bf16[2560]{0:T(1024)(128)(2,1)} %gm_hbm.1, bf16[1024,2560]{1,0:T(8,128)(2,1)} %wo_hbm.1, bf16[2560,5120]{1,0:T(8,128)(2,1)} %wg_hbm.1, ...), custom_call_target="tpu_custom_call" | custom-call | tf_op jit(solution)/shard_map/layer/pallas_call | solution.py:589
  53.7 7.3 %write.1 = (bf16[64,2560]{1,0:T(8,128)(2,1)}, bf16[64,1024,128]{2,1,0:T(8,128)(2,1)}, bf16[64,1024,128]{2,1,0:T(8,128)(2,1)}, bf16[32,1024,128]{2,1,0:T(8,128)(2,1)S(1)}, bf16[32,1024,128]{2,1,0:T(8,128)(2,1)S(1)}) custom-call(s32[64]{0:T(128)} %pos_hbm.5, ...), custom_call_target="tpu_custom_call", output_to_operand_aliasing={{3}: (4, {}), {4}: (5, {}), {1}: (6, {}), {2}: (7, {})} | custom-call | tf_op jit(solution)/shard_map/write/pallas_call | solution.py:666

commit v7 on v6

--- a/solution.py
+++ b/solution.py
@@ -16,7 +16,8 @@
 BF16 = jnp.bfloat16
 FAR = 1 << 28
 BLOCK = 4
-AHEAD = 2
+EARLY = 3
+AHEAD = 3
 FIRST = 4
 SLOTS = 22
 LAYER_VMEM = 35
@@ -33,7 +34,7 @@
 
 def first_kernel(
     pos_hbm, x_hbm, gain_hbm, wq_hbm, wk_hbm, wv_hbm, ck_hbm, cv_hbm,
-    part_ref, nk_hbm, nv_hbm, q_s, kx_s, vx_s, kn_s, vn_s,
+    part_ref, nk_hbm, nv_hbm, q_s, kx_s, vx_s, lim_s, hid_s, kn_s, vn_s,
     wbuf, kbuf, vbuf, ang_s, o_s, m_s, l_s,
     pos, x_ref, gain_ref, w_sem, k_sem, v_sem, out_sem, x_sem,
 ):
@@ -95,7 +96,13 @@
             copy.start()
 
     def angle_row(b, carry):
-        ang_s[pl.ds(b, 1), :] = freq * pos[b].astype(F32)
+        p = pos[b]
+        ang_s[pl.ds(b, 1), :] = freq * p.astype(F32)
+        local = lax.rem(p, slots) - base
+        owned = (local >= 0) & (local < local_slots)
+        span = pl.ds(pl.multiple_of(b * qrows, qrows), qrows)
+        lim_s[span, :] = jnp.full((qrows, LANES), jnp.where(p >= slots - 1, FAR // 2, p) - base, jnp.int32)
+        hid_s[span, :] = jnp.full((qrows, LANES), jnp.where(owned, local, -FAR), jnp.int32)
         return carry
 
     lax.fori_loop(0, rows, angle_row, 0, unroll=8)
@@ -216,10 +223,12 @@
             pltpu.VMEM((heads, 3, rows // 2, LANES), F32),
             jax.ShapeDtypeStruct(rows_k.shape, BF16),
             jax.ShapeDtypeStruct(rows_v.shape, BF16),
-            tile(qrows), tile(qrows), tile(qrows), tile(16), tile(16),
+            tile(qrows), tile(qrows), tile(qrows),
+            *(pltpu.VMEM((rows * qrows, LANES), jnp.int32) for _ in range(2)),
+            tile(16), tile(16),
         ),
         in_specs=[hbm] * 8,
-        out_specs=(vmem, hbm, hbm) + (vmem,) * 5,
+        out_specs=(vmem, hbm, hbm) + (vmem,) * 7,
         scratch_shapes=[
             pltpu.VMEM((heads + 2 * kvs, width, head_dim), BF16),
             pltpu.VMEM((rows // 2, *rows_k.shape[1:]), BF16),
@@ -258,12 +267,12 @@
 
 
 def layer_kernel(
-    kv_heads, pos_hbm, x_hbm, gm_hbm, wo_hbm, wg_hbm, wu_hbm, wd_hbm, ck_hbm, cv_hbm,
-    far_ref, q_s, kx_s, vx_s,
+    kv_heads, x_hbm, gm_hbm, wo_hbm, wg_hbm, wu_hbm, wd_hbm, ck_hbm, cv_hbm,
+    far_ref, q_s, kx_s, vx_s, lim_s, hid_s,
     out_ref, kbuf, vbuf,
     ring, o_s, m_s, l_s, part, rd, sx, rx,
     po, ro, so, yo, hb, act, pm, rm, sm, ym, ob,
-    pos, x_ref, gm_ref,
+    x_ref, gm_ref,
     small_sem, k_sem, v_sem, o_sem, c_sem, send_sem, recv_sem,
 ):
     rows, width = x_ref.shape
@@ -274,7 +283,6 @@
     per_slot, qrows = 2 * kvs, 2 * heads
     key_rows = ck_hbm.shape[1]
     local_slots = key_rows // per_slot
-    slots = local_slots * lax.axis_size("sp")
     slices = key_rows // LANES
     n_blocks = rows // 2 // BLOCK
     mine_h = heads // 2
@@ -282,7 +290,6 @@
     sp, tp = lax.axis_index("sp"), lax.axis_index("tp")
     x, k = sp // 2, lax.rem(sp, 2)
     d_dev, x_dev, y_dev = {"sp": x * 2 + 1 - k}, {"sp": (1 - x) * 2 + k}, {"tp": 1 - tp}
-    base = sp * local_slots
     m_cols = act.shape[1]
     span = width // CHUNKS
 
@@ -310,14 +317,11 @@
     small = [
         pltpu.make_async_copy(src, dst, small_sem.at[i])
         for i, (src, dst) in enumerate(
-            ((pos_hbm, pos), (x_hbm, x_ref), (gm_hbm, gm_ref))
+            ((x_hbm, x_ref), (gm_hbm, gm_ref))
         )
     ]
-    for copy in small:
+    for copy in in_copies(0):
         copy.start()
-    for j in range(AHEAD):
-        for copy in in_copies(j):
-            copy.start()
 
     n_w = 0
     o_rows = mine_h * head_dim
@@ -347,10 +351,6 @@
         for copy in itertools.islice(queue, n):
             copy.start()
 
-    for copy in small:
-        copy.wait()
-    pl.semaphore_wait(barrier, 3)
-
     row = lax.broadcasted_iota(jnp.int32, (qrows, LANES), 0)
     col = lax.broadcasted_iota(jnp.int32, (qrows, LANES), 1)
     half_of_col = (col // kvs) % 2
@@ -379,14 +379,10 @@
             )
         probs, news = [], []
         for i in range(BLOCK):
-            p = pos[first + i]
-            local = lax.rem(p, slots) - base
-            owned = (local >= 0) & (local < local_slots)
-            hidden = jnp.where(owned, local, -FAR)
-            limit = jnp.where(p >= slots - 1, FAR // 2, p) - base
+            limit, hidden = lim_s[at_rows[i], :], hid_s[at_rows[i], :]
             fresh = q_s[at_rows[i], :] * kx_s[at_rows[i], :]
             fresh = jnp.sum(fresh + pltpu.roll(fresh, heads, 0), axis=1, keepdims=True) * scale
-            fresh = jnp.where(jnp.broadcast_to(owned, fresh.shape), fresh, -jnp.inf)
+            fresh = jnp.where(hidden[:, :1] >= 0, fresh, -jnp.inf)
             parts = []
             for t in range(slices):
                 own = scores[i][:, t * LANES : (t + 1) * LANES]
@@ -449,8 +445,14 @@
             cross_a[g].start()
         joined[g] = value
 
+    pl.semaphore_wait(barrier, 3)
     for g in range(near):
         swaps_a[g].start()
+    for j in range(1, AHEAD):
+        for copy in in_copies(j):
+            copy.start()
+    for copy in small:
+        copy.start()
     step = n_blocks // GROUPS
     for g in range(GROUPS):
         lax.fori_loop(g * step, (g + 1) * step, block_step, 0)
@@ -473,6 +475,8 @@
         o_a, o_b = (o_a / l).astype(BF16), (o_b / l).astype(BF16)
         pieces.append(jnp.concatenate([v[h] for h in range(mine_h) for v in (o_a, o_b)], axis=-1))
     attended = jnp.concatenate(pieces, axis=0)
+    for copy in small:
+        copy.wait()
 
     own, other = pl.ds(k * quarter, quarter), pl.ds((1 - k) * quarter, quarter)
     my_rows = pl.ds(pl.multiple_of(x * half + k * quarter, quarter), quarter)
@@ -570,7 +574,7 @@
         copy.wait_send()
 
 
-def layer(positions, tokens, gain, w_o, w_gate, w_up, w_down, rows_k, rows_v, kvs, carried):
+def layer(tokens, gain, w_o, w_gate, w_up, w_down, rows_k, rows_v, kvs, carried):
     rows, width = tokens.shape
     head_dim = 2 * LANES
     heads = carried[0].shape[0]
@@ -584,7 +588,7 @@
     stats = lambda h, n: pltpu.VMEM((h, 3, n, LANES), F32)
     dma = lambda n: pltpu.SemaphoreType.DMA((n,))
     n_remote = GROUPS + GROUPS // 2 + 8 * CHUNKS
-    args = (positions, tokens, gain, w_o, w_gate, w_up, w_down, rows_k, rows_v)
+    args = (tokens, gain, w_o, w_gate, w_up, w_down, rows_k, rows_v)
     shape = (half, *rows_k.shape[1:])
     return pl.pallas_call(
         functools.partial(layer_kernel, kvs),
@@ -602,10 +606,9 @@
             flat(half), flat(quarter), flat(quarter), flat(quarter), flat(half),
             pltpu.VMEM((half, cut), BF16),
             flat(half), flat(quarter), flat(quarter), flat(quarter), flat(rows),
-            pltpu.SMEM((rows,), jnp.int32),
             pltpu.VMEM(tokens.shape, BF16),
             pltpu.VMEM(gain.shape, BF16),
-            dma(3), dma(n_blocks), dma(n_blocks), dma(width // head_dim),
+            dma(2), dma(n_blocks), dma(n_blocks), dma(width // head_dim),
             dma(2 * (cut // head_dim) + width // head_dim), dma(n_remote), dma(n_remote),
         ],
         compiler_params=pltpu.CompilerParams(
@@ -615,7 +618,7 @@
     )(*(pltpu.with_memory_space_constraint(v, pltpu.HBM) for v in args), *carried)
 
 
-def write_kernel(pos_hbm, t_ref, kn_s, vn_s, _bk, _bv, _k, _v, out_ref, nk_hbm, nv_hbm, kbuf, vbuf, pos, sem, pos_sem):
+def write_kernel(pos_hbm, t_ref, kn_s, vn_s, _bk, _bv, _k, _v, out_ref, nk_hbm, nv_hbm, kbuf, vbuf, pos, sem, tile_sem, pos_sem):
     rows, key_rows, _ = kbuf.shape
     per_slot = 4
     local_slots = key_rows // per_slot
@@ -629,34 +632,62 @@
     def copies(j):
         here, near = pl.ds(j * BLOCK, BLOCK), pl.ds(start + j * BLOCK, BLOCK)
         return (
-            pltpu.make_async_copy(kbuf.at[here], nk_hbm.at[near], sem.at[0]),
-            pltpu.make_async_copy(vbuf.at[here], nv_hbm.at[near], sem.at[1]),
-        )
-
-    def patch(n):
-        b = start + n
+            pltpu.make_async_copy(kbuf.at[here], nk_hbm.at[near], sem.at[0, j]),
+            pltpu.make_async_copy(vbuf.at[here], nv_hbm.at[near], sem.at[1, j]),
+        )
+
+    def target(b):
         local = lax.rem(pos[b], slots) - base
         owned = (local >= 0) & (local < local_slots)
         safe = jnp.where(owned, local, 0)
         hit = jnp.where(owned, lax.rem(safe, per_tile), -1)
-        at = pl.ds(pl.multiple_of((safe // per_tile) * 16, 16), 16)
+        return hit, pl.ds(pl.multiple_of((safe // per_tile) * 16, 16), 16)
+
+    def tile_copies(n):
+        at = target(start + n)[1]
+        return (
+            pltpu.make_async_copy(kbuf.at[n, at], nk_hbm.at[start + n, at], tile_sem.at[0]),
+            pltpu.make_async_copy(vbuf.at[n, at], nv_hbm.at[start + n, at], tile_sem.at[1]),
+        )
+
+    def patch(n):
+        b = start + n
+        hit, at = target(b)
         for buf, new in ((kbuf, kn_s), (vbuf, vn_s)):
             fresh = new[pl.ds(pl.multiple_of(b * 16, 16), 16), :]
             buf[n, at, :] = jnp.where(tile_row == hit, fresh, buf[n, at, :].astype(F32)).astype(BF16)
 
     pos_copy = pltpu.make_async_copy(pos_hbm, pos, pos_sem)
     pos_copy.start()
+    for j in range(EARLY):
+        for copy in copies(j):
+            copy.start()
     out_ref[...] = t_ref[...]
     pos_copy.wait()
-    for j in range(n_blocks + 1):
+    for j in range(EARLY, n_blocks + 1):
         if j < n_blocks:
             for i in range(BLOCK):
                 patch(j * BLOCK + i)
-        if j:
+        if j > EARLY:
             for copy in copies(j - 1):
                 copy.start()
-    for j in range(n_blocks):
+    for j in range(EARLY):
         for copy in copies(j):
+            copy.wait()
+        for i in range(BLOCK):
+            patch(j * BLOCK + i)
+        if j:
+            for i in range(BLOCK):
+                for copy in tile_copies((j - 1) * BLOCK + i):
+                    copy.start()
+    for i in range(BLOCK):
+        for copy in tile_copies((EARLY - 1) * BLOCK + i):
+            copy.start()
+    for j in range(EARLY, n_blocks):
+        for copy in copies(j):
+            copy.wait()
+    for n in range(EARLY * BLOCK):
+        for copy in tile_copies(n):
             copy.wait()
 
 
@@ -675,6 +706,7 @@
         input_output_aliases={4: 3, 5: 4, 6: 1, 7: 2},
         scratch_shapes=[
             pltpu.SMEM(positions.shape, jnp.int32),
+            pltpu.SemaphoreType.DMA((2, buf_k.shape[0] // BLOCK)),
             pltpu.SemaphoreType.DMA((2,)),
             pltpu.SemaphoreType.DMA,
         ],
@@ -706,7 +738,7 @@
             positions, tokens, attn_gain, w_q, w_k, w_v, old_k, old_v
         )
         out, buf_k, buf_v = layer(
-            positions, tokens, mlp_gain, w_o, w_gate, w_up, w_down, old_k, old_v, cache_k.shape[2], (far, *carried)
+            tokens, mlp_gain, w_o, w_gate, w_up, w_down, old_k, old_v, cache_k.shape[2], (far, *carried)
         )
         layer_out, rows_k, rows_v = write(positions, out, fresh_k, fresh_v, buf_k, buf_v, rows_k, rows_v)
         new_k = from_rows(rows_k, cache_k.shape)

time: 61.1 us -> 61.7 us (level)
    pallas_call x1, Pallas kernels: 38.8 us -> 39.9 us  [layer(): pl.pallas_call(functools.partial(layer_kernel, kvs), out_shape=(pltpu.VME...]
where the time goes in v7:
time: 61.7 us; the launch traced here: 61.5 us
  Pallas kernels  60.7 us (98%)
  between operations  0.81 us (1%)
    pallas_call x1, Pallas kernels, layer(): pl.pallas_call(functools.partial(layer_kernel, kvs), out_shape=(pltpu.VME...  39.9 us
    pallas_call x1, Pallas kernels, first_half(): pl.pallas_call(first_kernel, out_shape=(pltpu.VMEM((heads, 3, rows // 2,...  14.1 us
    pallas_call x1, Pallas kernels, write(): pl.pallas_call(write_kernel, out_shape=(*(jax.ShapeDtypeStruct(v.shape, B...  6.77 us

profile of v7, /device:TPU:0, one launch (start us, length us, event | category | flops | bytes accessed | tf_op | source)
XLA Modules:
  0.0 61.5 jit_solution(1324617878554698371)
XLA Ops:
  0.6 14.1 %first.1 = (f32[4,3,32,128]{3,2,1,0:T(8,128)S(1)}, bf16[64,1024,128]{2,1,0:T(8,128)(2,1)}, bf16[64,1024,128]{2,1,0:T(8,128)(2,1)}, f32[512,128]{1,0:T(8,128)S(1)...) custom-call(s32[64]{0:T(128)} %pos_hbm.3, ...), custom_call_target="tpu_custom_call" | custom-call | tf_op jit(solution)/shard_map/first/pallas_call | solution.py:220
  14.7 39.9 %layer.1 = (bf16[64,2560]{1,0:T(8,128)(2,1)S(1)}, bf16[32,1024,128]{2,1,0:T(8,128)(2,1)S(1)}, bf16[32,1024,128]{2,1,0:T(8,128)(2,1)S(1)}) custom-call(bf16[64,2560]{1,0:T(8,128)(2,1)} %x_hbm.3, bf16[2560]{0:T(1024)(128)(2,1)} %gm_hbm.1, bf16[1024,2560]{1,0:T(8,128)(2,1)} %wo_hbm.1, bf16[2560,5120]{1,0:T(8,128)(2,1)} %wg_hbm.1, bf16[2560,5120]{1,0:T(8,128)(2,1)} %wu_hbm.1, ...), custom_call_target="tpu_custom_call" | custom-call | tf_op jit(solution)/shard_map/layer/pallas_call | solution.py:593
  54.6 6.8 %write.1 = (bf16[64,2560]{1,0:T(8,128)(2,1)}, bf16[64,1024,128]{2,1,0:T(8,128)(2,1)}, bf16[64,1024,128]{2,1,0:T(8,128)(2,1)}, bf16[32,1024,128]{2,1,0:T(8,128)(2,1)S(1)}, bf16[32,1024,128]{2,1,0:T(8,128)(2,1)S(1)}) custom-call(s32[64]{0:T(128)} %pos_hbm.3, ...), custom_call_target="tpu_custom_call", output_to_operand_aliasing={{3}: (4, {}), {4}: (5, {}), {1}: (6, {}), {2}: (7, {})} | custom-call | tf_op jit(solution)/shard_map/write/pallas_call | solution.py:697

commit v8 on v7

--- a/solution.py
+++ b/solution.py
@@ -17,7 +17,7 @@
 FAR = 1 << 28
 BLOCK = 4
 EARLY = 3
-AHEAD = 3
+EAGER = (2, 6)
 FIRST = 4
 SLOTS = 22
 LAYER_VMEM = 35
@@ -320,8 +320,12 @@
             ((x_hbm, x_ref), (gm_hbm, gm_ref))
         )
     ]
-    for copy in in_copies(0):
-        copy.start()
+    def read(blocks):
+        for j in blocks:
+            for copy in in_copies(j):
+                copy.start()
+
+    read(range(EAGER[0]))
 
     n_w = 0
     o_rows = mine_h * head_dim
@@ -360,11 +364,6 @@
     scale = 1.0 / math.sqrt(head_dim)
 
     def block_step(j, carry):
-        @pl.when(j + AHEAD < n_blocks)
-        def _():
-            for copy in in_copies(j + AHEAD):
-                copy.start()
-
         for copy in in_copies(j):
             copy.wait()
         first = x * half + j * BLOCK
@@ -448,26 +447,22 @@
     pl.semaphore_wait(barrier, 3)
     for g in range(near):
         swaps_a[g].start()
-    for j in range(1, AHEAD):
-        for copy in in_copies(j):
-            copy.start()
+    read(range(*EAGER))
     for copy in small:
         copy.start()
-    step = n_blocks // GROUPS
-    for g in range(GROUPS):
-        lax.fori_loop(g * step, (g + 1) * step, block_step, 0)
-        if g == 0:
-            for n in range(near):
-                chip(n)
-        elif g == 1:
-            publish(near)
-        elif g == 2:
-            chip(near)
-            for copy in o_copies:
-                copy.start()
+    step = n_blocks // near
+    lax.fori_loop(0, step, block_step, 0)
+    for g in range(near):
+        chip(g)
+    read(range(EAGER[1], n_blocks))
+    publish(near)
+    for copy in o_copies:
+        copy.start()
+    lax.fori_loop(step, n_blocks, block_step, 0)
     publish(GROUPS - 1)
     fetch(3)
-    chip(GROUPS - 1)
+    for g in range(near, GROUPS):
+        chip(g)
     pieces = []
     for g in range(GROUPS // 2):
         cross_a[g].wait_recv()

time: 61.7 us -> 60.6 us (0.982)
  Pallas kernels: 60.7 us -> 59.9 us
    pallas_call x1, Pallas kernels: 39.9 us -> 39 us  [layer(): pl.pallas_call(functools.partial(layer_kernel, kvs), out_shape=(pltpu.VME...]
where the time goes in v8:
time: 60.6 us; the launch traced here: 60.5 us
  Pallas kernels  59.9 us (99%)
  between operations  0.65 us (1%)
    pallas_call x1, Pallas kernels, layer(): pl.pallas_call(functools.partial(layer_kernel, kvs), out_shape=(pltpu.VME...  39 us
    pallas_call x1, Pallas kernels, first_half(): pl.pallas_call(first_kernel, out_shape=(pltpu.VMEM((heads, 3, rows // 2,...  14.1 us
    pallas_call x1, Pallas kernels, write(): pl.pallas_call(write_kernel, out_shape=(*(jax.ShapeDtypeStruct(v.shape, B...  6.77 us

profile of v8, /device:TPU:0, one launch (start us, length us, event | category | flops | bytes accessed | tf_op | source)
XLA Modules:
  0.0 60.5 jit_solution(14116917919249515588)
XLA Ops:
  0.6 14.1 %first.1 = (f32[4,3,32,128]{3,2,1,0:T(8,128)S(1)}, bf16[64,1024,128]{2,1,0:T(8,128)(2,1)}, bf16[64,1024,128]{2,1,0:T(8,128)(2,1)}, f32[512,128]{1,0:T(8,128)S(1)...) custom-call(s32[64]{0:T(128)} %pos_hbm.3, ...), custom_call_target="tpu_custom_call" | custom-call | tf_op jit(solution)/shard_map/first/pallas_call | solution.py:220
  14.7 39.0 %layer.1 = (bf16[64,2560]{1,0:T(8,128)(2,1)S(1)}, bf16[32,1024,128]{2,1,0:T(8,128)(2,1)S(1)}, bf16[32,1024,128]{2,1,0:T(8,128)(2,1)S(1)}) custom-call(bf16[64,2560]{1,0:T(8,128)(2,1)} %x_hbm.3, bf16[2560]{0:T(1024)(128)(2,1)} %gm_hbm.1, bf16[1024,2560]{1,0:T(8,128)(2,1)} %wo_hbm.1, bf16[2560,5120]{1,0:T(8,128)(2,1)} %wg_hbm.1, bf16[2560,5120]{1,0:T(8,128)(2,1)} %wu_hbm.1, ...), custom_call_target="tpu_custom_call" | custom-call | tf_op jit(solution)/shard_map/layer/pallas_call | solution.py:588
  53.7 6.8 %write.1 = (bf16[64,2560]{1,0:T(8,128)(2,1)}, bf16[64,1024,128]{2,1,0:T(8,128)(2,1)}, bf16[64,1024,128]{2,1,0:T(8,128)(2,1)}, bf16[32,1024,128]{2,1,0:T(8,128)(2,1)S(1)}, bf16[32,1024,128]{2,1,0:T(8,128)(2,1)S(1)}) custom-call(s32[64]{0:T(128)} %pos_hbm.3, ...), custom_call_target="tpu_custom_call", output_to_operand_aliasing={{3}: (4, {}), {4}: (5, {}), {1}: (6, {}), {2}: (7, {})} | custom-call | tf_op jit(solution)/shard_map/write/pallas_call | solution.py:692

commit v9 on v8

--- a/solution.py
+++ b/solution.py
@@ -17,11 +17,11 @@
 FAR = 1 << 28
 BLOCK = 4
 EARLY = 3
-EAGER = (2, 6)
+EAGER = (2, 5)
 FIRST = 4
 SLOTS = 22
 LAYER_VMEM = 35
-CHUNKS = 5
+CHUNKS = 10
 GROUPS = 4
 MESH = pl.DeviceIdType.MESH
 
@@ -351,7 +351,11 @@
     ]
     queue = iter(chunks)
 
-    def fetch(n):
+    started = [0]
+
+    def fetch(n, limit=len(chunks)):
+        n = min(n, limit - started[0])
+        started[0] += n
         for copy in itertools.islice(queue, n):
             copy.start()
 
@@ -507,7 +511,7 @@
         swaps[c].wait_recv()
         so[:, cols[c]] = po[own, cols[c]] + ro[:, cols[c]]
         crosses[c].start()
-        fetch(3)
+        fetch(2, SLOTS)
 
     def o_cross(c):
         crosses[c].wait_recv()

time: 60.6 us -> 63.7 us (1.051)
  Pallas kernels: 59.9 us -> 62.9 us
    pallas_call x1, Pallas kernels: 39 us -> 42.1 us  [layer(): pl.pallas_call(functools.partial(layer_kernel, kvs), out_shape=(pltpu.VME...]
where the time goes in v9:
time: 63.7 us; the launch traced here: 63.6 us
  Pallas kernels  62.9 us (99%)
  between operations  0.65 us (1%)
    pallas_call x1, Pallas kernels, layer(): pl.pallas_call(functools.partial(layer_kernel, kvs), out_shape=(pltpu.VME...  42.1 us
    pallas_call x1, Pallas kernels, first_half(): pl.pallas_call(first_kernel, out_shape=(pltpu.VMEM((heads, 3, rows // 2,...  14.1 us
    pallas_call x1, Pallas kernels, write(): pl.pallas_call(write_kernel, out_shape=(*(jax.ShapeDtypeStruct(v.shape, B...  6.77 us

profile of v9, /device:TPU:0, one launch (start us, length us, event | category | flops | bytes accessed | tf_op | source)
XLA Modules:
  0.0 63.6 jit_solution(4844797431793979230)
XLA Ops:
  0.6 14.1 %first.1 = (f32[4,3,32,128]{3,2,1,0:T(8,128)S(1)}, bf16[64,1024,128]{2,1,0:T(8,128)(2,1)}, bf16[64,1024,128]{2,1,0:T(8,128)(2,1)}, f32[512,128]{1,0:T(8,128)S(1)...) custom-call(s32[64]{0:T(128)} %pos_hbm.3, ...), custom_call_target="tpu_custom_call" | custom-call | tf_op jit(solution)/shard_map/first/pallas_call | solution.py:220
  14.7 42.1 %layer.1 = (bf16[64,2560]{1,0:T(8,128)(2,1)S(1)}, bf16[32,1024,128]{2,1,0:T(8,128)(2,1)S(1)}, bf16[32,1024,128]{2,1,0:T(8,128)(2,1)S(1)}) custom-call(bf16[64,2560]{1,0:T(8,128)(2,1)} %x_hbm.3, bf16[2560]{0:T(1024)(128)(2,1)} %gm_hbm.1, bf16[1024,2560]{1,0:T(8,128)(2,1)} %wo_hbm.1, bf16[2560,5120]{1,0:T(8,128)(2,1)} %wg_hbm.1, bf16[2560,5120]{1,0:T(8,128)(2,1)} %wu_hbm.1, ...), custom_call_target="tpu_custom_call" | custom-call | tf_op jit(solution)/shard_map/layer/pallas_call | solution.py:592
  56.8 6.8 %write.1 = (bf16[64,2560]{1,0:T(8,128)(2,1)}, bf16[64,1024,128]{2,1,0:T(8,128)(2,1)}, bf16[64,1024,128]{2,1,0:T(8,128)(2,1)}, bf16[32,1024,128]{2,1,0:T(8,128)(2,1)S(1)}, bf16[32,1024,128]{2,1,0:T(8,128)(2,1)S(1)}) custom-call(s32[64]{0:T(128)} %pos_hbm.3, ...), custom_call_target="tpu_custom_call", output_to_operand_aliasing={{3}: (4, {}), {4}: (5, {}), {1}: (6, {}), {2}: (7, {})} | custom-call | tf_op jit(solution)/shard_map/write/pallas_call | solution.py:696

commit v10 on v9

--- a/solution.py
+++ b/solution.py
@@ -21,7 +21,7 @@
 FIRST = 4
 SLOTS = 22
 LAYER_VMEM = 35
-CHUNKS = 10
+CHUNKS = 2
 GROUPS = 4
 MESH = pl.DeviceIdType.MESH
 
@@ -511,7 +511,7 @@
         swaps[c].wait_recv()
         so[:, cols[c]] = po[own, cols[c]] + ro[:, cols[c]]
         crosses[c].start()
-        fetch(2, SLOTS)
+        fetch(-(-SLOTS // CHUNKS), SLOTS)
 
     def o_cross(c):
         crosses[c].wait_recv()

time: 63.7 us -> 64.2 us (level)
  no operation moved by 1% of the time
where the time goes in v10:
time: 64.2 us; the launch traced here: 64.1 us
  Pallas kernels  63.4 us (99%)
  between operations  0.65 us (1%)
    pallas_call x1, Pallas kernels, layer(): pl.pallas_call(functools.partial(layer_kernel, kvs), out_shape=(pltpu.VME...  42.6 us
    pallas_call x1, Pallas kernels, first_half(): pl.pallas_call(first_kernel, out_shape=(pltpu.VMEM((heads, 3, rows // 2,...  14.1 us
    pallas_call x1, Pallas kernels, write(): pl.pallas_call(write_kernel, out_shape=(*(jax.ShapeDtypeStruct(v.shape, B...  6.77 us

profile of v10, /device:TPU:0, one launch (start us, length us, event | category | flops | bytes accessed | tf_op | source)
XLA Modules:
  0.0 64.1 jit_solution(2488098580275032538)
XLA Ops:
  0.6 14.1 %first.1 = (f32[4,3,32,128]{3,2,1,0:T(8,128)S(1)}, bf16[64,1024,128]{2,1,0:T(8,128)(2,1)}, bf16[64,1024,128]{2,1,0:T(8,128)(2,1)}, f32[512,128]{1,0:T(8,128)S(1)...) custom-call(s32[64]{0:T(128)} %pos_hbm.3, ...), custom_call_target="tpu_custom_call" | custom-call | tf_op jit(solution)/shard_map/first/pallas_call | solution.py:220
  14.7 42.6 %layer.1 = (bf16[64,2560]{1,0:T(8,128)(2,1)S(1)}, bf16[32,1024,128]{2,1,0:T(8,128)(2,1)S(1)}, bf16[32,1024,128]{2,1,0:T(8,128)(2,1)S(1)}) custom-call(bf16[64,2560]{1,0:T(8,128)(2,1)} %x_hbm.3, bf16[2560]{0:T(1024)(128)(2,1)} %gm_hbm.1, bf16[1024,2560]{1,0:T(8,128)(2,1)} %wo_hbm.1, bf16[2560,5120]{1,0:T(8,128)(2,1)} %wg_hbm.1, bf16[2560,5120]{1,0:T(8,128)(2,1)} %wu_hbm.1, ...), custom_call_target="tpu_custom_call" | custom-call | tf_op jit(solution)/shard_map/layer/pallas_call | solution.py:592
  57.3 6.8 %write.1 = (bf16[64,2560]{1,0:T(8,128)(2,1)}, bf16[64,1024,128]{2,1,0:T(8,128)(2,1)}, bf16[64,1024,128]{2,1,0:T(8,128)(2,1)}, bf16[32,1024,128]{2,1,0:T(8,128)(2,1)S(1)}, bf16[32,1024,128]{2,1,0:T(8,128)(2,1)S(1)}) custom-call(s32[64]{0:T(128)} %pos_hbm.3, ...), custom_call_target="tpu_custom_call", output_to_operand_aliasing={{3}: (4, {}), {4}: (5, {}), {1}: (6, {}), {2}: (7, {})} | custom-call | tf_op jit(solution)/shard_map/write/pallas_call | solution.py:696

commit v11 on v10

--- a/solution.py
+++ b/solution.py
@@ -17,11 +17,11 @@
 FAR = 1 << 28
 BLOCK = 4
 EARLY = 3
-EAGER = (2, 5)
+EAGER = (2, 6)
 FIRST = 4
 SLOTS = 22
 LAYER_VMEM = 35
-CHUNKS = 2
+CHUNKS = 5
 GROUPS = 4
 MESH = pl.DeviceIdType.MESH
 
@@ -511,7 +511,8 @@
         swaps[c].wait_recv()
         so[:, cols[c]] = po[own, cols[c]] + ro[:, cols[c]]
         crosses[c].start()
-        fetch(-(-SLOTS // CHUNKS), SLOTS)
+        if c == CHUNKS - 1:
+            fetch(15)
 
     def o_cross(c):
         crosses[c].wait_recv()
@@ -523,6 +524,7 @@
         gathers[c].wait_recv()
 
     staged(o_dot, o_swap, o_cross, o_gather)
+    fetch(SLOTS, SLOTS)
 
     normed_m = rms_norm(hb[...], gm_ref[...])
     for c in range(n_gate):

time: 64.2 us -> 60.6 us (0.944)
  Pallas kernels: 63.4 us -> 59.9 us
    pallas_call x1, Pallas kernels: 42.6 us -> 39 us  [layer(): pl.pallas_call(functools.partial(layer_kernel, kvs), out_shape=(pltpu.VME...]
where the time goes in v11:
time: 60.6 us; the launch traced here: 60.5 us
  Pallas kernels  59.9 us (99%)
  between operations  0.65 us (1%)
    pallas_call x1, Pallas kernels, layer(): pl.pallas_call(functools.partial(layer_kernel, kvs), out_shape=(pltpu.VME...  39 us
    pallas_call x1, Pallas kernels, first_half(): pl.pallas_call(first_kernel, out_shape=(pltpu.VMEM((heads, 3, rows // 2,...  14.1 us
    pallas_call x1, Pallas kernels, write(): pl.pallas_call(write_kernel, out_shape=(*(jax.ShapeDtypeStruct(v.shape, B...  6.77 us

profile of v11, /device:TPU:0, one launch (start us, length us, event | category | flops | bytes accessed | tf_op | source)
XLA Modules:
  0.0 60.5 jit_solution(5729385997190537607)
XLA Ops:
  0.6 14.1 %first.1 = (f32[4,3,32,128]{3,2,1,0:T(8,128)S(1)}, bf16[64,1024,128]{2,1,0:T(8,128)(2,1)}, bf16[64,1024,128]{2,1,0:T(8,128)(2,1)}, f32[512,128]{1,0:T(8,128)S(1)...) custom-call(s32[64]{0:T(128)} %pos_hbm.3, ...), custom_call_target="tpu_custom_call" | custom-call | tf_op jit(solution)/shard_map/first/pallas_call | solution.py:220
  14.7 39.0 %layer.1 = (bf16[64,2560]{1,0:T(8,128)(2,1)S(1)}, bf16[32,1024,128]{2,1,0:T(8,128)(2,1)S(1)}, bf16[32,1024,128]{2,1,0:T(8,128)(2,1)S(1)}) custom-call(bf16[64,2560]{1,0:T(8,128)(2,1)} %x_hbm.3, bf16[2560]{0:T(1024)(128)(2,1)} %gm_hbm.1, bf16[1024,2560]{1,0:T(8,128)(2,1)} %wo_hbm.1, bf16[2560,5120]{1,0:T(8,128)(2,1)} %wg_hbm.1, bf16[2560,5120]{1,0:T(8,128)(2,1)} %wu_hbm.1, ...), custom_call_target="tpu_custom_call" | custom-call | tf_op jit(solution)/shard_map/layer/pallas_call | solution.py:594
  53.7 6.8 %write.1 = (bf16[64,2560]{1,0:T(8,128)(2,1)}, bf16[64,1024,128]{2,1,0:T(8,128)(2,1)}, bf16[64,1024,128]{2,1,0:T(8,128)(2,1)}, bf16[32,1024,128]{2,1,0:T(8,128)(2,1)S(1)}, bf16[32,1024,128]{2,1,0:T(8,128)(2,1)S(1)}) custom-call(s32[64]{0:T(128)} %pos_hbm.3, ...), custom_call_target="tpu_custom_call", output_to_operand_aliasing={{3}: (4, {}), {4}: (5, {}), {1}: (6, {}), {2}: (7, {})} | custom-call | tf_op jit(solution)/shard_map/write/pallas_call | solution.py:698

commit v12 on v11

--- a/solution.py
+++ b/solution.py
@@ -17,7 +17,7 @@
 FAR = 1 << 28
 BLOCK = 4
 EARLY = 3
-EAGER = (2, 6)
+EAGER = (3, 8)
 FIRST = 4
 SLOTS = 22
 LAYER_VMEM = 35

time: 60.6 us -> 60.5 us (level)
  no operation moved by 1% of the time
where the time goes in v12:
time: 60.5 us; the launch traced here: 60.4 us
  Pallas kernels  59.8 us (99%)
  between operations  0.65 us (1%)
    pallas_call x1, Pallas kernels, layer(): pl.pallas_call(functools.partial(layer_kernel, kvs), out_shape=(pltpu.VME...  38.9 us
    pallas_call x1, Pallas kernels, first_half(): pl.pallas_call(first_kernel, out_shape=(pltpu.VMEM((heads, 3, rows // 2,...  14.1 us
    pallas_call x1, Pallas kernels, write(): pl.pallas_call(write_kernel, out_shape=(*(jax.ShapeDtypeStruct(v.shape, B...  6.77 us

profile of v12, /device:TPU:0, one launch (start us, length us, event | category | flops | bytes accessed | tf_op | source)
XLA Modules:
  0.0 60.4 jit_solution(15800186345093643167)
XLA Ops:
  0.6 14.1 %first.1 = (f32[4,3,32,128]{3,2,1,0:T(8,128)S(1)}, bf16[64,1024,128]{2,1,0:T(8,128)(2,1)}, bf16[64,1024,128]{2,1,0:T(8,128)(2,1)}, f32[512,128]{1,0:T(8,128)S(1)...) custom-call(s32[64]{0:T(128)} %pos_hbm.3, ...), custom_call_target="tpu_custom_call" | custom-call | tf_op jit(solution)/shard_map/first/pallas_call | solution.py:220
  14.7 38.9 %layer.1 = (bf16[64,2560]{1,0:T(8,128)(2,1)S(1)}, bf16[32,1024,128]{2,1,0:T(8,128)(2,1)S(1)}, bf16[32,1024,128]{2,1,0:T(8,128)(2,1)S(1)}) custom-call(bf16[64,2560]{1,0:T(8,128)(2,1)} %x_hbm.3, bf16[2560]{0:T(1024)(128)(2,1)} %gm_hbm.1, bf16[1024,2560]{1,0:T(8,128)(2,1)} %wo_hbm.1, bf16[2560,5120]{1,0:T(8,128)(2,1)} %wg_hbm.1, bf16[2560,5120]{1,0:T(8,128)(2,1)} %wu_hbm.1, ...), custom_call_target="tpu_custom_call" | custom-call | tf_op jit(solution)/shard_map/layer/pallas_call | solution.py:594
  53.6 6.8 %write.1 = (bf16[64,2560]{1,0:T(8,128)(2,1)}, bf16[64,1024,128]{2,1,0:T(8,128)(2,1)}, bf16[64,1024,128]{2,1,0:T(8,128)(2,1)}, bf16[32,1024,128]{2,1,0:T(8,128)(2,1)S(1)}, bf16[32,1024,128]{2,1,0:T(8,128)(2,1)S(1)}) custom-call(s32[64]{0:T(128)} %pos_hbm.3, ...), custom_call_target="tpu_custom_call", output_to_operand_aliasing={{3}: (4, {}), {4}: (5, {}), {1}: (6, {}), {2}: (7, {})} | custom-call | tf_op jit(solution)/shard_map/write/pallas_call | solution.py:698

commit v13 on v12

--- a/solution.py
+++ b/solution.py
@@ -482,6 +482,9 @@
     x_peer_rows = pl.ds(pl.multiple_of((1 - x) * half + k * quarter, quarter), quarter)
     cols = [pl.ds(c * span, span) for c in range(CHUNKS)]
     per_span = span // head_dim
+    cuts = (0, 3, CHUNKS)
+    joint = [pl.ds(a * span, (b - a) * span) for a, b in zip(cuts, cuts[1:])]
+    last_of = {b - 1: i for i, b in enumerate(cuts[1:])}
 
     def staged(dot, swap, cross, *rest):
         for c in range(CHUNKS + 2):
@@ -498,7 +501,7 @@
 
     swaps = [remote(po.at[other, c], ro.at[:, c], d_dev) for c in cols]
     crosses = [remote(so.at[:, c], yo.at[:, c], y_dev) for c in cols]
-    gathers = [remote(hb.at[own, c], hb.at[own, c], d_dev) for c in cols]
+    gathers = [remote(hb.at[own, c], hb.at[own, c], d_dev) for c in joint]
 
     def o_dot(c):
         for i in range(c * per_span, (c + 1) * per_span):
@@ -518,10 +521,12 @@
         crosses[c].wait_recv()
         total = so[:, cols[c]] + yo[:, cols[c]]
         hb[own, cols[c]] = (x_ref[my_rows, cols[c]].astype(F32) + total).astype(BF16).astype(F32)
-        gathers[c].start()
+        if c in last_of:
+            gathers[last_of[c]].start()
 
     def o_gather(c):
-        gathers[c].wait_recv()
+        if c in last_of:
+            gathers[last_of[c]].wait_recv()
 
     staged(o_dot, o_swap, o_cross, o_gather)
     fetch(SLOTS, SLOTS)
@@ -537,9 +542,9 @@
 
     swaps_m = [remote(pm.at[other, c], rm.at[:, c], d_dev) for c in cols]
     crosses_m = [remote(sm.at[:, c], ym.at[:, c], y_dev) for c in cols]
-    to_core = [remote(ob.at[my_rows, c], ob.at[my_rows, c], d_dev) for c in cols]
+    to_core = [remote(ob.at[my_rows], ob.at[my_rows], d_dev)]
     to_x = [remote(ob.at[my_rows, c], ob.at[my_rows, c], x_dev) for c in cols]
-    onward = [remote(ob.at[x_peer_rows, c], ob.at[x_peer_rows, c], d_dev) for c in cols]
+    onward = [remote(ob.at[x_peer_rows, c], ob.at[x_peer_rows, c], d_dev) for c in joint]
 
     def m_dot(c):
         for i in range(c * per_span, (c + 1) * per_span):
@@ -559,16 +564,21 @@
         total = sm[:, cols[c]] + ym[:, cols[c]]
         ob[my_rows, cols[c]] = (hb[own, cols[c]] + total).astype(BF16).astype(F32)
         to_x[c].start()
-        to_core[c].start()
+        if c == CHUNKS - 1:
+            to_core[0].start()
 
     def m_gather(c):
         to_x[c].wait_recv()
-        onward[c].start()
+        if c in last_of:
+            onward[last_of[c]].start()
 
     def m_last(c):
-        to_core[c].wait_recv()
-        onward[c].wait_recv()
-        out_ref[:, cols[c]] = ob[:, cols[c]].astype(BF16)
+        if c == 0:
+            to_core[0].wait_recv()
+        if c in last_of:
+            at = joint[last_of[c]]
+            onward[last_of[c]].wait_recv()
+            out_ref[:, at] = ob[:, at].astype(BF16)
 
     staged(m_dot, m_swap, m_cross, m_gather, m_last)
     for copy in [*swaps_a, *cross_a, *swaps, *crosses, *gathers, *swaps_m, *crosses_m, *to_core, *to_x, *onward]:
@@ -588,7 +598,7 @@
     flat = lambda n: pltpu.VMEM((n, width), F32)
     stats = lambda h, n: pltpu.VMEM((h, 3, n, LANES), F32)
     dma = lambda n: pltpu.SemaphoreType.DMA((n,))
-    n_remote = GROUPS + GROUPS // 2 + 8 * CHUNKS
+    n_remote = GROUPS + GROUPS // 2 + 5 * CHUNKS + 5
     args = (tokens, gain, w_o, w_gate, w_up, w_down, rows_k, rows_v)
     shape = (half, *rows_k.shape[1:])
     return pl.pallas_call(

time: 60.5 us -> 60.5 us (level)
  no operation moved by 1% of the time
where the time goes in v13:
time: 60.5 us; the launch traced here: 60.4 us
  Pallas kernels  59.8 us (99%)
  between operations  0.65 us (1%)
    pallas_call x1, Pallas kernels, layer(): pl.pallas_call(functools.partial(layer_kernel, kvs), out_shape=(pltpu.VME...  38.9 us
    pallas_call x1, Pallas kernels, first_half(): pl.pallas_call(first_kernel, out_shape=(pltpu.VMEM((heads, 3, rows // 2,...  14.1 us
    pallas_call x1, Pallas kernels, write(): pl.pallas_call(write_kernel, out_shape=(*(jax.ShapeDtypeStruct(v.shape, B...  6.77 us

profile of v13, /device:TPU:0, one launch (start us, length us, event | category | flops | bytes accessed | tf_op | source)
XLA Modules:
  0.0 60.4 jit_solution(2001516302741807596)
XLA Ops:
  0.6 14.1 %first.1 = (f32[4,3,32,128]{3,2,1,0:T(8,128)S(1)}, bf16[64,1024,128]{2,1,0:T(8,128)(2,1)}, bf16[64,1024,128]{2,1,0:T(8,128)(2,1)}, f32[512,128]{1,0:T(8,128)S(1)...) custom-call(s32[64]{0:T(128)} %pos_hbm.3, ...), custom_call_target="tpu_custom_call" | custom-call | tf_op jit(solution)/shard_map/first/pallas_call | solution.py:220
  14.7 38.9 %layer.1 = (bf16[64,2560]{1,0:T(8,128)(2,1)S(1)}, bf16[32,1024,128]{2,1,0:T(8,128)(2,1)S(1)}, bf16[32,1024,128]{2,1,0:T(8,128)(2,1)S(1)}) custom-call(bf16[64,2560]{1,0:T(8,128)(2,1)} %x_hbm.3, bf16[2560]{0:T(1024)(128)(2,1)} %gm_hbm.1, bf16[1024,2560]{1,0:T(8,128)(2,1)} %wo_hbm.1, bf16[2560,5120]{1,0:T(8,128)(2,1)} %wg_hbm.1, bf16[2560,5120]{1,0:T(8,128)(2,1)} %wu_hbm.1, ...), custom_call_target="tpu_custom_call" | custom-call | tf_op jit(solution)/shard_map/layer/pallas_call | solution.py:604
  53.7 6.8 %write.1 = (bf16[64,2560]{1,0:T(8,128)(2,1)}, bf16[64,1024,128]{2,1,0:T(8,128)(2,1)}, bf16[64,1024,128]{2,1,0:T(8,128)(2,1)}, bf16[32,1024,128]{2,1,0:T(8,128)(2,1)S(1)}, bf16[32,1024,128]{2,1,0:T(8,128)(2,1)S(1)}) custom-call(s32[64]{0:T(128)} %pos_hbm.3, ...), custom_call_target="tpu_custom_call", output_to_operand_aliasing={{3}: (4, {}), {4}: (5, {}), {1}: (6, {}), {2}: (7, {})} | custom-call | tf_op jit(solution)/shard_map/write/pallas_call | solution.py:708

commit v14 on v13

--- a/solution.py
+++ b/solution.py
@@ -416,36 +416,36 @@
 
     size = rows // GROUPS
     my_heads, their_heads = pl.ds(k * mine_h, mine_h), pl.ds((1 - k) * mine_h, mine_h)
-    spans = [pl.ds(g * size, size) for g in range(GROUPS)]
-    near = GROUPS // 2
-    sources = [far_ref.at[their_heads, :, spans[g]] for g in range(near)]
-    sources += [part.at[their_heads, :, spans[g]] for g in range(near)]
+    near = 1
+    spans = [pl.ds(0, half)] + [pl.ds(half + g * size, size) for g in range(GROUPS // 2)]
+    inner = [pl.ds(g * size, size) for g in range(GROUPS // 2)]
+    sources = [far_ref.at[their_heads]] + [part.at[their_heads, :, at] for at in inner]
     swaps_a = [remote(src, rd.at[:, :, at], d_dev) for src, at in zip(sources, spans)]
-    cross_a = [remote(sx.at[:, :, at], rx.at[:, :, at], x_dev) for at in spans[: GROUPS // 2]]
-    left = lax.broadcasted_iota(jnp.int32, (mine_h, size, LANES), 2) < LANES // 2
-    joined = [None] * GROUPS
+    cross_a = remote(sx, rx, x_dev)
+    left = lambda n: lax.broadcasted_iota(jnp.int32, (mine_h, n, LANES), 2) < LANES // 2
+    joined = [None] * len(spans)
 
     def publish(g):
-        at = spans[g - near]
+        at = inner[g - near]
         for h in range(heads):
             lo = pl.ds((g - near) * size * qrows + h, size, stride=qrows)
             hi = pl.ds((g - near) * size * qrows + heads + h, size, stride=qrows)
             part[h, 0, at], part[h, 1, at] = o_s[lo, :], o_s[hi, :]
-            part[h, 2, at] = jnp.where(left[0], m_s[lo, :], l_s[lo, :])
+            part[h, 2, at] = jnp.where(left(size)[0], m_s[lo, :], l_s[lo, :])
         swaps_a[g].start()
 
     def chip(g):
         swaps_a[g].wait_recv()
         at = spans[g]
-        here, local = (far_ref, at) if g < near else (part, spans[g - near])
+        here, local = (far_ref, at) if g < near else (part, inner[g - near])
         o_a, o_b, m, l = combine(
             [here[my_heads, i, local] for i in range(3)], [rd[:, i, at] for i in range(3)]
         )
-        value = [o_a, o_b, jnp.where(left, m, l)]
-        if g < GROUPS // 2:
+        value = [o_a, o_b, jnp.where(left(m.shape[1]), m, l)]
+        if g < near:
             for i in range(3):
-                sx[:, i, at] = value[i]
-            cross_a[g].start()
+                sx[:, i] = value[i]
+            cross_a.start()
         joined[g] = value
 
     pl.semaphore_wait(barrier, 3)
@@ -454,7 +454,7 @@
     read(range(*EAGER))
     for copy in small:
         copy.start()
-    step = n_blocks // near
+    step = n_blocks // 2
     lax.fori_loop(0, step, block_step, 0)
     for g in range(near):
         chip(g)
@@ -463,14 +463,14 @@
     for copy in o_copies:
         copy.start()
     lax.fori_loop(step, n_blocks, block_step, 0)
-    publish(GROUPS - 1)
+    publish(near + 1)
     fetch(3)
-    for g in range(near, GROUPS):
+    for g in range(near, len(spans)):
         chip(g)
+    cross_a.wait_recv()
     pieces = []
     for g in range(GROUPS // 2):
-        cross_a[g].wait_recv()
-        o_a, o_b, _, l = combine(joined[GROUPS // 2 + g], [rx[:, i, spans[g]] for i in range(3)])
+        o_a, o_b, _, l = combine(joined[near + g], [rx[:, i, inner[g]] for i in range(3)])
         o_a, o_b = (o_a / l).astype(BF16), (o_b / l).astype(BF16)
         pieces.append(jnp.concatenate([v[h] for h in range(mine_h) for v in (o_a, o_b)], axis=-1))
     attended = jnp.concatenate(pieces, axis=0)
@@ -581,7 +581,7 @@
             out_ref[:, at] = ob[:, at].astype(BF16)
 
     staged(m_dot, m_swap, m_cross, m_gather, m_last)
-    for copy in [*swaps_a, *cross_a, *swaps, *crosses, *gathers, *swaps_m, *crosses_m, *to_core, *to_x, *onward]:
+    for copy in [*swaps_a, cross_a, *swaps, *crosses, *gathers, *swaps_m, *crosses_m, *to_core, *to_x, *onward]:
         copy.wait_send()
 
 
@@ -598,7 +598,7 @@
     flat = lambda n: pltpu.VMEM((n, width), F32)
     stats = lambda h, n: pltpu.VMEM((h, 3, n, LANES), F32)
     dma = lambda n: pltpu.SemaphoreType.DMA((n,))
-    n_remote = GROUPS + GROUPS // 2 + 5 * CHUNKS + 5
+    n_remote = GROUPS // 2 + 2 + 5 * CHUNKS + 5
     args = (tokens, gain, w_o, w_gate, w_up, w_down, rows_k, rows_v)
     shape = (half, *rows_k.shape[1:])
     return pl.pallas_call(
@@ -629,7 +629,7 @@
     )(*(pltpu.with_memory_space_constraint(v, pltpu.HBM) for v in args), *carried)
 
 
-def write_kernel(pos_hbm, t_ref, kn_s, vn_s, _bk, _bv, _k, _v, out_ref, nk_hbm, nv_hbm, kbuf, vbuf, pos, sem, tile_sem, pos_sem):
+def write_kernel(pos_hbm, t_ref, kn_s, vn_s, _bk, _bv, _k, _v, out_hbm, nk_hbm, nv_hbm, kbuf, vbuf, pos, sem, tile_sem, pos_sem, out_sem):
     rows, key_rows, _ = kbuf.shape
     per_slot = 4
     local_slots = key_rows // per_slot
@@ -673,7 +673,8 @@
     for j in range(EARLY):
         for copy in copies(j):
             copy.start()
-    out_ref[...] = t_ref[...]
+    out_copy = pltpu.make_async_copy(t_ref, out_hbm, out_sem)
+    out_copy.start()
     pos_copy.wait()
     for j in range(EARLY, n_blocks + 1):
         if j < n_blocks:
@@ -700,6 +701,7 @@
     for n in range(EARLY * BLOCK):
         for copy in tile_copies(n):
             copy.wait()
+    out_copy.wait()
 
 
 def write(positions, layer_out, fresh_k, fresh_v, buf_k, buf_v, new_k, new_v):
@@ -713,13 +715,14 @@
             pltpu.VMEM(buf_v.shape, BF16),
         ),
         in_specs=[hbm] + [vmem] * 5 + [hbm] * 2,
-        out_specs=(vmem, hbm, hbm, vmem, vmem),
+        out_specs=(hbm, hbm, hbm, vmem, vmem),
         input_output_aliases={4: 3, 5: 4, 6: 1, 7: 2},
         scratch_shapes=[
             pltpu.SMEM(positions.shape, jnp.int32),
             pltpu.SemaphoreType.DMA((2, buf_k.shape[0] // BLOCK)),
             pltpu.SemaphoreType.DMA((2,)),
             pltpu.SemaphoreType.DMA,
+            pltpu.SemaphoreType.DMA,
         ],
         compiler_params=pltpu.CompilerParams(vmem_limit_bytes=LAYER_VMEM << 20),
         name="write",

time: 60.5 us -> 59.7 us (0.987)
  Pallas kernels: 59.8 us -> 59 us
    pallas_call x1, Pallas kernels: 6.77 us -> 6.16 us  [write(): pl.pallas_call(write_kernel, out_shape=(*(jax.ShapeDtypeStruct(v.shape, B...]
where the time goes in v14:
time: 59.7 us; the launch traced here: 59.6 us
  Pallas kernels  59 us (99%)
  between operations  0.65 us (1%)
    pallas_call x1, Pallas kernels, layer(): pl.pallas_call(functools.partial(layer_kernel, kvs), out_shape=(pltpu.VME...  38.7 us
    pallas_call x1, Pallas kernels, first_half(): pl.pallas_call(first_kernel, out_shape=(pltpu.VMEM((heads, 3, rows // 2,...  14.1 us
    pallas_call x1, Pallas kernels, write(): pl.pallas_call(write_kernel, out_shape=(*(jax.ShapeDtypeStruct(v.shape, B...  6.16 us

profile of v14, /device:TPU:0, one launch (start us, length us, event | category | flops | bytes accessed | tf_op | source)
XLA Modules:
  0.0 59.6 jit_solution(10450695986067420857)
XLA Ops:
  0.6 14.1 %first.1 = (f32[4,3,32,128]{3,2,1,0:T(8,128)S(1)}, bf16[64,1024,128]{2,1,0:T(8,128)(2,1)}, bf16[64,1024,128]{2,1,0:T(8,128)(2,1)}, f32[512,128]{1,0:T(8,128)S(1)...) custom-call(s32[64]{0:T(128)} %pos_hbm.3, ...), custom_call_target="tpu_custom_call" | custom-call | tf_op jit(solution)/shard_map/first/pallas_call | solution.py:220
  14.7 38.7 %layer.1 = (bf16[64,2560]{1,0:T(8,128)(2,1)S(1)}, bf16[32,1024,128]{2,1,0:T(8,128)(2,1)S(1)}, bf16[32,1024,128]{2,1,0:T(8,128)(2,1)S(1)}) custom-call(bf16[64,2560]{1,0:T(8,128)(2,1)} %x_hbm.3, bf16[2560]{0:T(1024)(128)(2,1)} %gm_hbm.1, bf16[1024,2560]{1,0:T(8,128)(2,1)} %wo_hbm.1, bf16[2560,5120]{1,0:T(8,128)(2,1)} %wg_hbm.1, bf16[2560,5120]{1,0:T(8,128)(2,1)} %wu_hbm.1, ...), custom_call_target="tpu_custom_call" | custom-call | tf_op jit(solution)/shard_map/layer/pallas_call | solution.py:604
  53.5 6.2 %write.1 = (bf16[64,2560]{1,0:T(8,128)(2,1)}, bf16[64,1024,128]{2,1,0:T(8,128)(2,1)}, bf16[64,1024,128]{2,1,0:T(8,128)(2,1)}, bf16[32,1024,128]{2,1,0:T(8,128)(2,1)S(1)}, bf16[32,1024,128]{2,1,0:T(8,128)(2,1)S(1)}) custom-call(s32[64]{0:T(128)} %pos_hbm.3, ...), custom_call_target="tpu_custom_call", output_to_operand_aliasing={{3}: (4, {}), {4}: (5, {}), {1}: (6, {}), {2}: (7, {})} | custom-call | tf_op jit(solution)/shard_map/write/pallas_call | solution.py:710

commit v15 on v14

--- a/solution.py
+++ b/solution.py
@@ -15,13 +15,14 @@
 F32 = jnp.float32
 BF16 = jnp.bfloat16
 FAR = 1 << 28
-BLOCK = 4
-EARLY = 3
-EAGER = (3, 8)
-FIRST = 4
+BLOCK = 2
+EARLY = 6
+EAGER = (6, 16)
+FIRST = 8
 SLOTS = 22
 LAYER_VMEM = 35
-CHUNKS = 5
+CUTS = (0, 4, 8, 10)
+CHUNKS = len(CUTS) - 1
 GROUPS = 4
 MESH = pl.DeviceIdType.MESH
 
@@ -291,7 +292,6 @@
     x, k = sp // 2, lax.rem(sp, 2)
     d_dev, x_dev, y_dev = {"sp": x * 2 + 1 - k}, {"sp": (1 - x) * 2 + k}, {"tp": 1 - tp}
     m_cols = act.shape[1]
-    span = width // CHUNKS
 
     barrier = pltpu.get_barrier_semaphore()
     for dev in (d_dev, x_dev, y_dev):
@@ -480,11 +480,10 @@
     own, other = pl.ds(k * quarter, quarter), pl.ds((1 - k) * quarter, quarter)
     my_rows = pl.ds(pl.multiple_of(x * half + k * quarter, quarter), quarter)
     x_peer_rows = pl.ds(pl.multiple_of((1 - x) * half + k * quarter, quarter), quarter)
-    cols = [pl.ds(c * span, span) for c in range(CHUNKS)]
-    per_span = span // head_dim
-    cuts = (0, 3, CHUNKS)
-    joint = [pl.ds(a * span, (b - a) * span) for a, b in zip(cuts, cuts[1:])]
-    last_of = {b - 1: i for i, b in enumerate(cuts[1:])}
+    columns = lambda a, b: pl.ds(a * head_dim, (b - a) * head_dim)
+    cols = [columns(a, b) for a, b in zip(CUTS, CUTS[1:])]
+    joint = [columns(0, CUTS[-2]), columns(*CUTS[-2:])]
+    last_of = {CHUNKS - 2: 0, CHUNKS - 1: 1}
 
     def staged(dot, swap, cross, *rest):
         for c in range(CHUNKS + 2):
@@ -504,7 +503,7 @@
     gathers = [remote(hb.at[own, c], hb.at[own, c], d_dev) for c in joint]
 
     def o_dot(c):
-        for i in range(c * per_span, (c + 1) * per_span):
+        for i in range(CUTS[c], CUTS[c + 1]):
             o_copies[i].wait()
             w = ring[n_w + i // per_o, (i % per_o) * o_rows : (i % per_o + 1) * o_rows, :]
             po[:, i * head_dim : (i + 1) * head_dim] = jnp.dot(attended, w, preferred_element_type=F32)
@@ -547,7 +546,7 @@
     onward = [remote(ob.at[x_peer_rows, c], ob.at[x_peer_rows, c], d_dev) for c in joint]
 
     def m_dot(c):
-        for i in range(c * per_span, (c + 1) * per_span):
+        for i in range(CUTS[c], CUTS[c + 1]):
             chunks[2 * n_gate + i].wait()
             pm[:, i * head_dim : (i + 1) * head_dim] = jnp.dot(
                 act[...], ring[ring_at(2 * n_gate + i)], preferred_element_type=F32

time: 59.7 us -> 69.8 us (1.17)
  Pallas kernels: 59 us -> 69.1 us
    pallas_call x1, Pallas kernels: 38.7 us -> 45.4 us  [layer(): pl.pallas_call(functools.partial(layer_kernel, kvs), out_shape=(pltpu.VME...]
    pallas_call x1, Pallas kernels: 14.1 us -> 17.4 us  [first_half(): pl.pallas_call(first_kernel, out_shape=(pltpu.VMEM((heads, 3, rows // 2,...]
where the time goes in v15:
time: 69.8 us; the launch traced here: 69.7 us
  Pallas kernels  69.1 us (99%)
    pallas_call x1, Pallas kernels, layer(): pl.pallas_call(functools.partial(layer_kernel, kvs), out_shape=(pltpu.VME...  45.4 us
    pallas_call x1, Pallas kernels, first_half(): pl.pallas_call(first_kernel, out_shape=(pltpu.VMEM((heads, 3, rows // 2,...  17.4 us
    pallas_call x1, Pallas kernels, write(): pl.pallas_call(write_kernel, out_shape=(*(jax.ShapeDtypeStruct(v.shape, B...  6.27 us

profile of v15, /device:TPU:0, one launch (start us, length us, event | category | flops | bytes accessed | tf_op | source)
XLA Modules:
  0.0 69.7 jit_solution(15922899992013914023)
XLA Ops:
  0.6 17.4 %first.1 = (f32[4,3,32,128]{3,2,1,0:T(8,128)S(1)}, bf16[64,1024,128]{2,1,0:T(8,128)(2,1)}, bf16[64,1024,128]{2,1,0:T(8,128)(2,1)}, f32[512,128]{1,0:T(8,128)S(1)...) custom-call(s32[64]{0:T(128)} %pos_hbm.3, ...), custom_call_target="tpu_custom_call" | custom-call | tf_op jit(solution)/shard_map/first/pallas_call | solution.py:221
  18.0 45.4 %layer.1 = (bf16[64,2560]{1,0:T(8,128)(2,1)S(1)}, bf16[32,1024,128]{2,1,0:T(8,128)(2,1)S(1)}, bf16[32,1024,128]{2,1,0:T(8,128)(2,1)S(1)}) custom-call(bf16[64,2560]{1,0:T(8,128)(2,1)} %x_hbm.3, bf16[2560]{0:T(1024)(128)(2,1)} %gm_hbm.1, bf16[1024,2560]{1,0:T(8,128)(2,1)} %wo_hbm.1, bf16[2560,5120]{1,0:T(8,128)(2,1)} %wg_hbm.1, bf16[2560,5120]{1,0:T(8,128)(2,1)} %wu_hbm.1, ...), custom_call_target="tpu_custom_call" | custom-call | tf_op jit(solution)/shard_map/layer/pallas_call | solution.py:603
  63.4 6.3 %write.1 = (bf16[64,2560]{1,0:T(8,128)(2,1)}, bf16[64,1024,128]{2,1,0:T(8,128)(2,1)}, bf16[64,1024,128]{2,1,0:T(8,128)(2,1)}, bf16[32,1024,128]{2,1,0:T(8,128)(2,1)S(1)}, bf16[32,1024,128]{2,1,0:T(8,128)(2,1)S(1)}) custom-call(s32[64]{0:T(128)} %pos_hbm.3, ...), custom_call_target="tpu_custom_call", output_to_operand_aliasing={{3}: (4, {}), {4}: (5, {}), {1}: (6, {}), {2}: (7, {})} | custom-call | tf_op jit(solution)/shard_map/write/pallas_call | solution.py:709

commit v16 on v14

--- a/solution.py
+++ b/solution.py
@@ -81,19 +81,19 @@
     for copy in small:
         copy.start()
     n_w = heads + 2 * kvs
-    for n in range(n_w // 2):
+    for n in range(n_w):
         w_copy(n).start()
 
     lane = lax.broadcasted_iota(jnp.int32, (1, LANES), 1).astype(F32)
     freq = jnp.exp2(lane * (-math.log2(ROPE_THETA) / LANES))
 
-    for copy in small:
+    for copy in small[1:]:
         copy.wait()
-    for n in range(n_w // 2, n_w):
-        w_copy(n).start()
     for j in range(FIRST):
         for copy in in_copies(j):
             copy.start()
+    normed = rms_norm(x_ref[...], gain_ref[...])
+    small[0].wait()
 
     def angle_row(b, carry):
         p = pos[b]
@@ -108,8 +108,6 @@
     lax.fori_loop(0, rows, angle_row, 0, unroll=8)
     angles = ang_s[...]
     cos_t, sin_t = jnp.cos(angles), jnp.sin(angles)
-    normed = rms_norm(x_ref[...], gain_ref[...])
-
     for n in range(n_w):
         w_copy(n).wait()
         if FIRST + n < n_blocks:

time: 59.7 us -> 61.2 us (1.025)
  Pallas kernels: 59 us -> 60.5 us
    pallas_call x1, Pallas kernels: 14.1 us -> 15.6 us  [first_half(): pl.pallas_call(first_kernel, out_shape=(pltpu.VMEM((heads, 3, rows // 2,...]
where the time goes in v16:
time: 61.2 us; the launch traced here: 61.1 us
  Pallas kernels  60.5 us (99%)
  between operations  0.65 us (1%)
    pallas_call x1, Pallas kernels, layer(): pl.pallas_call(functools.partial(layer_kernel, kvs), out_shape=(pltpu.VME...  38.7 us
    pallas_call x1, Pallas kernels, first_half(): pl.pallas_call(first_kernel, out_shape=(pltpu.VMEM((heads, 3, rows // 2,...  15.6 us
    pallas_call x1, Pallas kernels, write(): pl.pallas_call(write_kernel, out_shape=(*(jax.ShapeDtypeStruct(v.shape, B...  6.16 us

profile of v16, /device:TPU:0, one launch (start us, length us, event | category | flops | bytes accessed | tf_op | source)
XLA Modules:
  0.0 61.1 jit_solution(17101888415882595402)
XLA Ops:
  0.6 15.6 %first.1 = (f32[4,3,32,128]{3,2,1,0:T(8,128)S(1)}, bf16[64,1024,128]{2,1,0:T(8,128)(2,1)}, bf16[64,1024,128]{2,1,0:T(8,128)(2,1)}, f32[512,128]{1,0:T(8,128)S(1)...) custom-call(s32[64]{0:T(128)} %pos_hbm.3, ...), custom_call_target="tpu_custom_call" | custom-call | tf_op jit(solution)/shard_map/first/pallas_call | solution.py:218
  16.2 38.7 %layer.1 = (bf16[64,2560]{1,0:T(8,128)(2,1)S(1)}, bf16[32,1024,128]{2,1,0:T(8,128)(2,1)S(1)}, bf16[32,1024,128]{2,1,0:T(8,128)(2,1)S(1)}) custom-call(bf16[64,2560]{1,0:T(8,128)(2,1)} %x_hbm.3, bf16[2560]{0:T(1024)(128)(2,1)} %gm_hbm.1, bf16[1024,2560]{1,0:T(8,128)(2,1)} %wo_hbm.1, bf16[2560,5120]{1,0:T(8,128)(2,1)} %wg_hbm.1, bf16[2560,5120]{1,0:T(8,128)(2,1)} %wu_hbm.1, ...), custom_call_target="tpu_custom_call" | custom-call | tf_op jit(solution)/shard_map/layer/pallas_call | solution.py:602
  55.0 6.2 %write.1 = (bf16[64,2560]{1,0:T(8,128)(2,1)}, bf16[64,1024,128]{2,1,0:T(8,128)(2,1)}, bf16[64,1024,128]{2,1,0:T(8,128)(2,1)}, bf16[32,1024,128]{2,1,0:T(8,128)(2,1)S(1)}, bf16[32,1024,128]{2,1,0:T(8,128)(2,1)S(1)}) custom-call(s32[64]{0:T(128)} %pos_hbm.3, ...), custom_call_target="tpu_custom_call", output_to_operand_aliasing={{3}: (4, {}), {4}: (5, {}), {1}: (6, {}), {2}: (7, {})} | custom-call | tf_op jit(solution)/shard_map/write/pallas_call | solution.py:708

commit v17 on v16

--- a/solution.py
+++ b/solution.py
@@ -81,7 +81,7 @@
     for copy in small:
         copy.start()
     n_w = heads + 2 * kvs
-    for n in range(n_w):
+    for n in range(n_w // 4):
         w_copy(n).start()
 
     lane = lax.broadcasted_iota(jnp.int32, (1, LANES), 1).astype(F32)
@@ -89,11 +89,13 @@
 
     for copy in small[1:]:
         copy.wait()
+    for n in range(n_w // 4, n_w):
+        w_copy(n).start()
+    normed = rms_norm(x_ref[...], gain_ref[...])
+    small[0].wait()
     for j in range(FIRST):
         for copy in in_copies(j):
             copy.start()
-    normed = rms_norm(x_ref[...], gain_ref[...])
-    small[0].wait()
 
     def angle_row(b, carry):
         p = pos[b]

time: 61.2 us -> 60.9 us (level)
  no operation moved by 1% of the time
where the time goes in v17:
time: 60.9 us; the launch traced here: 60.8 us
  Pallas kernels  60.1 us (99%)
  between operations  0.65 us (1%)
    pallas_call x1, Pallas kernels, layer(): pl.pallas_call(functools.partial(layer_kernel, kvs), out_shape=(pltpu.VME...  38.8 us
    pallas_call x1, Pallas kernels, first_half(): pl.pallas_call(first_kernel, out_shape=(pltpu.VMEM((heads, 3, rows // 2,...  15.2 us
    pallas_call x1, Pallas kernels, write(): pl.pallas_call(write_kernel, out_shape=(*(jax.ShapeDtypeStruct(v.shape, B...  6.16 us

profile of v17, /device:TPU:0, one launch (start us, length us, event | category | flops | bytes accessed | tf_op | source)
XLA Modules:
  0.0 60.8 jit_solution(6732558833769714630)
XLA Ops:
  0.6 15.2 %first.1 = (f32[4,3,32,128]{3,2,1,0:T(8,128)S(1)}, bf16[64,1024,128]{2,1,0:T(8,128)(2,1)}, bf16[64,1024,128]{2,1,0:T(8,128)(2,1)}, f32[512,128]{1,0:T(8,128)S(1)...) custom-call(s32[64]{0:T(128)} %pos_hbm.3, ...), custom_call_target="tpu_custom_call" | custom-call | tf_op jit(solution)/shard_map/first/pallas_call | solution.py:220
  15.9 38.8 %layer.1 = (bf16[64,2560]{1,0:T(8,128)(2,1)S(1)}, bf16[32,1024,128]{2,1,0:T(8,128)(2,1)S(1)}, bf16[32,1024,128]{2,1,0:T(8,128)(2,1)S(1)}) custom-call(bf16[64,2560]{1,0:T(8,128)(2,1)} %x_hbm.3, bf16[2560]{0:T(1024)(128)(2,1)} %gm_hbm.1, bf16[1024,2560]{1,0:T(8,128)(2,1)} %wo_hbm.1, bf16[2560,5120]{1,0:T(8,128)(2,1)} %wg_hbm.1, bf16[2560,5120]{1,0:T(8,128)(2,1)} %wu_hbm.1, ...), custom_call_target="tpu_custom_call" | custom-call | tf_op jit(solution)/shard_map/layer/pallas_call | solution.py:604
  54.6 6.2 %write.1 = (bf16[64,2560]{1,0:T(8,128)(2,1)}, bf16[64,1024,128]{2,1,0:T(8,128)(2,1)}, bf16[64,1024,128]{2,1,0:T(8,128)(2,1)}, bf16[32,1024,128]{2,1,0:T(8,128)(2,1)S(1)}, bf16[32,1024,128]{2,1,0:T(8,128)(2,1)S(1)}) custom-call(s32[64]{0:T(128)} %pos_hbm.3, ...), custom_call_target="tpu_custom_call", output_to_operand_aliasing={{3}: (4, {}), {4}: (5, {}), {1}: (6, {}), {2}: (7, {})} | custom-call | tf_op jit(solution)/shard_map/write/pallas_call | solution.py:710

commit v18 on v14

--- a/solution.py
+++ b/solution.py
@@ -17,7 +17,8 @@
 FAR = 1 << 28
 BLOCK = 4
 EARLY = 3
-EAGER = (3, 8)
+WIDE = 8
+EAGER = (2, 4)
 FIRST = 4
 SLOTS = 22
 LAYER_VMEM = 35
@@ -284,7 +285,7 @@
     key_rows = ck_hbm.shape[1]
     local_slots = key_rows // per_slot
     slices = key_rows // LANES
-    n_blocks = rows // 2 // BLOCK
+    n_blocks = rows // 2 // WIDE
     mine_h = heads // 2
     half, quarter = rows // 2, rows // 4
     sp, tp = lax.axis_index("sp"), lax.axis_index("tp")
@@ -308,7 +309,7 @@
         )
 
     def in_copies(j):
-        near, here = pl.ds(x * half + j * BLOCK, BLOCK), pl.ds(j * BLOCK, BLOCK)
+        near, here = pl.ds(x * half + j * WIDE, WIDE), pl.ds(j * WIDE, WIDE)
         return (
             pltpu.make_async_copy(ck_hbm.at[near], kbuf.at[here], k_sem.at[j]),
             pltpu.make_async_copy(cv_hbm.at[near], vbuf.at[here], v_sem.at[j]),
@@ -370,18 +371,18 @@
     def block_step(j, carry):
         for copy in in_copies(j):
             copy.wait()
-        first = x * half + j * BLOCK
-        at_rows = [pl.ds(pl.multiple_of((first + i) * qrows, qrows), qrows) for i in range(BLOCK)]
+        first = x * half + j * WIDE
+        at_rows = [pl.ds(pl.multiple_of((first + i) * qrows, qrows), qrows) for i in range(WIDE)]
         scores = []
-        for i in range(BLOCK):
+        for i in range(WIDE):
             scores.append(
                 lax.dot_general(
-                    q_s[at_rows[i], :].astype(BF16), kbuf[j * BLOCK + i], (((1,), (1,)), ((), ())),
+                    q_s[at_rows[i], :].astype(BF16), kbuf[j * WIDE + i], (((1,), (1,)), ((), ())),
                     preferred_element_type=F32,
                 )
             )
         probs, news = [], []
-        for i in range(BLOCK):
+        for i in range(WIDE):
             limit, hidden = lim_s[at_rows[i], :], hid_s[at_rows[i], :]
             fresh = q_s[at_rows[i], :] * kx_s[at_rows[i], :]
             fresh = jnp.sum(fresh + pltpu.roll(fresh, heads, 0), axis=1, keepdims=True) * scale
@@ -402,15 +403,15 @@
             parts = [jnp.exp(part_t - floor) for part_t in parts]
             new = jnp.exp(fresh - floor)
             total = jnp.sum(functools.reduce(jnp.add, parts), axis=1, keepdims=True) + new
-            at = pl.ds(pl.multiple_of((j * BLOCK + i) * qrows, qrows), qrows)
+            at = pl.ds(pl.multiple_of((j * WIDE + i) * qrows, qrows), qrows)
             m_s[at, :] = jnp.broadcast_to(top, (qrows, LANES))
             l_s[at, :] = jnp.broadcast_to(total, (qrows, LANES))
             news.append(new)
             probs.append(jnp.concatenate([part_t.astype(BF16) for part_t in parts], axis=1))
-        for i in range(BLOCK):
-            at = pl.ds(pl.multiple_of((j * BLOCK + i) * qrows, qrows), qrows)
+        for i in range(WIDE):
+            at = pl.ds(pl.multiple_of((j * WIDE + i) * qrows, qrows), qrows)
             o_s[at, :] = (
-                jnp.dot(probs[i], vbuf[j * BLOCK + i], preferred_element_type=F32) + news[i] * vx_s[at_rows[i], :]
+                jnp.dot(probs[i], vbuf[j * WIDE + i], preferred_element_type=F32) + news[i] * vx_s[at_rows[i], :]
             )
         return carry
 
@@ -592,7 +593,7 @@
     qrows = 2 * heads
     half, quarter = rows // 2, rows // 4
     cut = w_gate.shape[1] // 2
-    n_blocks = half // BLOCK
+    n_blocks = half // WIDE
     vmem = pl.BlockSpec(memory_space=pltpu.VMEM)
     hbm = pl.BlockSpec(memory_space=pltpu.HBM)
     flat = lambda n: pltpu.VMEM((n, width), F32)

time: 59.7 us -> 58.8 us (0.985)
  Pallas kernels: 59 us -> 58 us
    pallas_call x1, Pallas kernels: 38.7 us -> 37.8 us  [layer(): pl.pallas_call(functools.partial(layer_kernel, kvs), out_shape=(pltpu.VME...]
where the time goes in v18:
time: 58.8 us; the launch traced here: 58.7 us
  Pallas kernels  58 us (99%)
  between operations  0.65 us (1%)
    pallas_call x1, Pallas kernels, layer(): pl.pallas_call(functools.partial(layer_kernel, kvs), out_shape=(pltpu.VME...  37.8 us
    pallas_call x1, Pallas kernels, first_half(): pl.pallas_call(first_kernel, out_shape=(pltpu.VMEM((heads, 3, rows // 2,...  14.1 us
    pallas_call x1, Pallas kernels, write(): pl.pallas_call(write_kernel, out_shape=(*(jax.ShapeDtypeStruct(v.shape, B...  6.16 us

profile of v18, /device:TPU:0, one launch (start us, length us, event | category | flops | bytes accessed | tf_op | source)
XLA Modules:
  0.0 58.7 jit_solution(4076097817435438608)
XLA Ops:
  0.6 14.1 %first.1 = (f32[4,3,32,128]{3,2,1,0:T(8,128)S(1)}, bf16[64,1024,128]{2,1,0:T(8,128)(2,1)}, bf16[64,1024,128]{2,1,0:T(8,128)(2,1)}, f32[512,128]{1,0:T(8,128)S(1)...) custom-call(s32[64]{0:T(128)} %pos_hbm.3, ...), custom_call_target="tpu_custom_call" | custom-call | tf_op jit(solution)/shard_map/first/pallas_call | solution.py:221
  14.7 37.8 %layer.1 = (bf16[64,2560]{1,0:T(8,128)(2,1)S(1)}, bf16[32,1024,128]{2,1,0:T(8,128)(2,1)S(1)}, bf16[32,1024,128]{2,1,0:T(8,128)(2,1)S(1)}) custom-call(bf16[64,2560]{1,0:T(8,128)(2,1)} %x_hbm.3, bf16[2560]{0:T(1024)(128)(2,1)} %gm_hbm.1, bf16[1024,2560]{1,0:T(8,128)(2,1)} %wo_hbm.1, bf16[2560,5120]{1,0:T(8,128)(2,1)} %wg_hbm.1, bf16[2560,5120]{1,0:T(8,128)(2,1)} %wu_hbm.1, ...), custom_call_target="tpu_custom_call" | custom-call | tf_op jit(solution)/shard_map/layer/pallas_call | solution.py:605
  52.5 6.2 %write.1 = (bf16[64,2560]{1,0:T(8,128)(2,1)}, bf16[64,1024,128]{2,1,0:T(8,128)(2,1)}, bf16[64,1024,128]{2,1,0:T(8,128)(2,1)}, bf16[32,1024,128]{2,1,0:T(8,128)(2,1)S(1)}, bf16[32,1024,128]{2,1,0:T(8,128)(2,1)S(1)}) custom-call(s32[64]{0:T(128)} %pos_hbm.3, ...), custom_call_target="tpu_custom_call", output_to_operand_aliasing={{3}: (4, {}), {4}: (5, {}), {1}: (6, {}), {2}: (7, {})} | custom-call | tf_op jit(solution)/shard_map/write/pallas_call | solution.py:711
